TPU v7x, 32 devices: a whole 2x2x4 slice. The times are simulated.
32 devices in a mesh: dp: 4 (over y, x), ctx: 2 (over core), tensor: 4 (over z).
Axes of the slice: x: 2, y: 2, z: 4, core: 2. Of those that a mesh axis runs over, the one named last changes fastest.
Arguments:
- prompt_in: bfloat16 [4, 1024, 2048], P('dp', 'ctx'), may hold values from -6 to 6
- cont_in: bfloat16 [4, 8, 128, 2048], P('dp', 'ctx'), may hold values from -6 to 6
- prompt_len: int32 [4], P('dp'), may hold values from 256 to 1024, as said below
- norm_attn: bfloat16 [2048], replicated, may hold values from 0.5 to 1.5
- w_query: bfloat16 [2048, 2048], P(None, 'tensor'), may hold values from -0.4375 to 0.4375
- key_weight: bfloat16 [2048, 512], P(None, 'tensor'), may hold values from -0.4375 to 0.4375
- value_weight: bfloat16 [2048, 512], P(None, 'tensor'), may hold values from -0.125 to 0.125
- w_out: bfloat16 [2048, 2048], P('tensor'), may hold values from -4 to 4
- norm_mlp: bfloat16 [2048], replicated, may hold values from 0.5 to 1.5
- w_gate: bfloat16 [2048, 8192], P(None, 'tensor'), may hold values from -0.125 to 0.125
- w_up: bfloat16 [2048, 8192], P(None, 'tensor'), may hold values from -0.125 to 0.125
- w_down: bfloat16 [8192, 2048], P('tensor'), may hold values from -0.5 to 0.5
- prompt_cot: bfloat16 [4, 1024, 2048], P('dp', 'ctx'), may hold values from -6 to 6
- cont_cot: bfloat16 [4, 8, 128, 2048], P('dp', 'ctx'), may hold values from -6 to 6
Outputs:
- prompt_out: bfloat16 [4, 1024, 2048], P('dp', 'ctx')
- cont_out: bfloat16 [4, 8, 128, 2048], P('dp', 'ctx')
- prompt_grad: bfloat16 [4, 1024, 2048], P('dp', 'ctx')
- cont_grad: bfloat16 [4, 8, 128, 2048], P('dp', 'ctx')
- grad_norm_attn: float32 [2048], P(('dp', 'ctx'))
- grad_query: float32 [2048, 2048], P(('dp', 'ctx'), 'tensor')
- grad_key: float32 [2048, 512], P(('dp', 'ctx'), 'tensor')
- grad_value: float32 [2048, 512], P(('dp', 'ctx'), 'tensor')
- grad_out: float32 [2048, 2048], P('tensor', ('dp', 'ctx'))
- grad_norm_mlp: float32 [2048], P(('dp', 'ctx'))
- grad_gate: float32 [2048, 8192], P(('dp', 'ctx'), 'tensor')
- grad_up: float32 [2048, 8192], P(('dp', 'ctx'), 'tensor')
- grad_down: float32 [8192, 2048], P('tensor', ('dp', 'ctx'))
Inputs may be any that keep to these rules, and one draw needn't show every extreme that they name: `prompt_len`: in every draw at least one prompt has all 1024 tokens valid.
All inputs are finite; a program needn't handle non-finite values.
Results may differ from a plain program's by a relative error of at most 0.015.
Values may be sent and summed in bfloat16 or wider, within the bound.
A program may use at most 320 MiB of HBM per device.

v0:
```python
import math

import jax
import jax.numpy as jnp
from jax import lax
from jax.sharding import PartitionSpec as P

QUERY_HEADS = 32
KEY_VALUE_HEADS = 8
HEAD_WIDTH = 64
CONT_LENGTH = 128


norm_eps = 1e-05
rope_base = 10000000.0
score_scale = 0.015625
branch_scale = 0.22
masked_score = -1e30


def norm_rows(inputs, weight):
    return inputs * lax.rsqrt(jnp.mean(inputs * inputs, axis=-1, keepdims=True) + norm_eps) * weight


def norm_back(inputs, weight, upstream):
    factor = lax.rsqrt(jnp.mean(inputs * inputs, axis=-1, keepdims=True) + norm_eps)
    scaled = inputs * factor
    weighted = upstream * weight
    through = factor * (weighted - scaled * jnp.mean(weighted * scaled, axis=-1, keepdims=True))
    return (through, jnp.sum(upstream * scaled, axis=0))


def angle_tables(position):
    freq = jnp.exp(
        jnp.arange(HEAD_WIDTH // 2, dtype=jnp.float32) * (-2.0 * math.log(rope_base) / HEAD_WIDTH)
    )
    angle = position.astype(jnp.float32)[:, None] * freq[None, :]
    return (jnp.cos(angle), jnp.sin(angle))


def rotate(inputs, cos_table, sin_table):
    halves = inputs.reshape(inputs.shape[0], -1, 2, HEAD_WIDTH // 2)
    first_half = halves[:, :, 0]
    second_half = halves[:, :, 1]
    cos_rows = cos_table[:, None, :]
    sin_rows = sin_table[:, None, :]
    turned = jnp.stack(
        [
            first_half * cos_rows - second_half * sin_rows,
            second_half * cos_rows + first_half * sin_rows,
        ],
        axis=2,
    )
    return turned.reshape(inputs.shape)


def score_block(query_rows, joined_keys, allowed):
    query_total = query_rows.shape[0]
    key_total = joined_keys.shape[0]
    key_value_heads = joined_keys.shape[1] // HEAD_WIDTH
    query_head_rows = query_rows.reshape(
        query_total, key_value_heads, QUERY_HEADS // KEY_VALUE_HEADS, HEAD_WIDTH
    )
    key_head_rows = joined_keys.reshape(key_total, key_value_heads, HEAD_WIDTH)
    scores = (
        jnp.einsum(
            "bhgd,khd->hgbk", query_head_rows, key_head_rows, preferred_element_type=jnp.float32
        )
        * score_scale
    )
    return (jnp.where(allowed[None, None], scores, masked_score), query_head_rows, key_head_rows)


def attend_forward(query_rows, joined_keys, joined_values, allowed):
    scores, query_head_rows, key_head_rows = score_block(query_rows, joined_keys, allowed)
    highest_score = jnp.max(scores, axis=-1, keepdims=True)
    log_total = highest_score + jnp.log(
        jnp.sum(jnp.exp(scores - highest_score), axis=-1, keepdims=True)
    )
    weights = jnp.exp(scores - log_total).astype(jnp.bfloat16)
    value_head_rows = joined_values.reshape(key_head_rows.shape)
    mixed_heads = jnp.einsum(
        "hgbk,khd->bhgd", weights, value_head_rows, preferred_element_type=jnp.float32
    )
    return (mixed_heads.reshape(query_rows.shape[0], -1), log_total)


def attend_backward(query_rows, joined_keys, joined_values, allowed, log_total, upstream):
    scores, query_head_rows, key_head_rows = score_block(query_rows, joined_keys, allowed)
    weights = jnp.exp(scores - log_total)
    value_head_rows = joined_values.reshape(key_head_rows.shape)
    grad_heads = upstream.reshape(query_head_rows.shape)
    grad_weights = jnp.einsum(
        "bhgd,khd->hgbk", grad_heads, value_head_rows, preferred_element_type=jnp.float32
    )
    grad_scores = (
        weights * (grad_weights - jnp.sum(grad_weights * weights, axis=-1, keepdims=True))
    ).astype(jnp.bfloat16)
    grad_query = (
        jnp.einsum("hgbk,khd->bhgd", grad_scores, key_head_rows, preferred_element_type=jnp.float32)
        * score_scale
    )
    grad_key = (
        jnp.einsum(
            "hgbk,bhgd->khd", grad_scores, query_head_rows, preferred_element_type=jnp.float32
        )
        * score_scale
    )
    grad_value = jnp.einsum(
        "hgbk,bhgd->khd",
        weights.astype(jnp.bfloat16),
        grad_heads,
        preferred_element_type=jnp.float32,
    )
    return (
        grad_query.reshape(query_rows.shape[0], -1),
        grad_key.reshape(joined_keys.shape[0], -1),
        grad_value.reshape(joined_keys.shape[0], -1),
    )


def shards(
    prompt_in,
    cont_in,
    prompt_len,
    norm_attn,
    w_query,
    key_weight,
    value_weight,
    w_out,
    norm_mlp,
    w_gate,
    w_up,
    w_down,
    prompt_cot,
    cont_cot,
):
    own_rows = prompt_in.shape[1]
    cont_count = cont_in.shape[1]
    width = prompt_in.shape[2]
    cont_rows = cont_count * CONT_LENGTH
    total_rows = own_rows + cont_rows
    key_width = key_weight.shape[1]
    ctx_index = lax.axis_index("ctx")
    share_rows = total_rows // lax.axis_size("tensor")
    share_start = lax.axis_index("tensor") * share_rows
    token_length = prompt_len[0]
    gain_attn = norm_attn.astype(jnp.float32)
    gain_mlp = norm_mlp.astype(jnp.float32)

    def share_of(values):
        return lax.dynamic_slice_in_dim(values, share_start, share_rows, 0)

    all_rows = jnp.concatenate([prompt_in[0], cont_in[0].reshape(cont_rows, width)], axis=0).astype(
        jnp.float32
    )
    input_share = share_of(all_rows)
    within = jnp.arange(cont_rows, dtype=jnp.int32) % CONT_LENGTH
    owner = jnp.arange(cont_rows, dtype=jnp.int32) // CONT_LENGTH
    positions = jnp.concatenate(
        [ctx_index * own_rows + jnp.arange(own_rows, dtype=jnp.int32), token_length + within]
    )
    cos_table, sin_table = angle_tables(positions)
    act_a = norm_rows(all_rows, gain_attn).astype(jnp.bfloat16)
    query_rows = rotate(
        jnp.dot(act_a, w_query, preferred_element_type=jnp.float32), cos_table, sin_table
    ).astype(jnp.bfloat16)
    joined_keys = rotate(
        jnp.dot(act_a, key_weight, preferred_element_type=jnp.float32), cos_table, sin_table
    ).astype(jnp.bfloat16)
    joined_values = jnp.dot(act_a, value_weight, preferred_element_type=jnp.float32).astype(
        jnp.bfloat16
    )
    local_pairs = jnp.concatenate([joined_keys[:own_rows], joined_values[:own_rows]], axis=1)
    prompt_pairs = lax.all_gather(local_pairs, "ctx", axis=0, tiled=True)
    prompt_total = prompt_pairs.shape[0]
    shared_prompt_keys = prompt_pairs[:, :key_width]
    shared_prompt_values = prompt_pairs[:, key_width:]
    key_place = jnp.arange(prompt_total, dtype=jnp.int32)
    key_valid = key_place < token_length
    block_rows = min(512, own_rows)
    block_index = 0
    query_place = (
        ctx_index * own_rows + block_index * block_rows + jnp.arange(block_rows, dtype=jnp.int32)
    )
    block_masks = [(key_place[None, :] <= query_place[:, None]) & key_valid[None, :]]
    cont_mask = jnp.concatenate(
        [
            jnp.broadcast_to(key_valid[None, :], (cont_rows, prompt_total)),
            (owner[:, None] == owner[None, :]) & (within[None, :] <= within[:, None]),
        ],
        axis=1,
    )
    cont_keys = jnp.concatenate([shared_prompt_keys, joined_keys[own_rows:]], axis=0)
    cont_values = jnp.concatenate([shared_prompt_values, joined_values[own_rows:]], axis=0)
    block_index = 0
    block_queries = query_rows[block_index * block_rows : (block_index + 1) * block_rows]
    mixed_block, total_block = attend_forward(
        block_queries, shared_prompt_keys, shared_prompt_values, block_masks[block_index]
    )
    mixed_list = [mixed_block]
    total_list = [total_block]
    mixed_cont, total_cont = attend_forward(
        query_rows[own_rows:], cont_keys, cont_values, cont_mask
    )
    mixed_heads = jnp.concatenate(mixed_list + [mixed_cont], axis=0).astype(jnp.bfloat16)
    attn_share = lax.psum_scatter(
        jnp.dot(mixed_heads, w_out, preferred_element_type=jnp.float32),
        "tensor",
        scatter_dimension=0,
        tiled=True,
    )
    hidden_share = input_share + branch_scale * attn_share
    act_b_share = norm_rows(hidden_share, gain_mlp).astype(jnp.bfloat16)
    act_b = lax.all_gather(act_b_share, "tensor", axis=0, tiled=True)
    gate_proj = jnp.dot(act_b, w_gate, preferred_element_type=jnp.float32)
    up_proj = jnp.dot(act_b, w_up, preferred_element_type=jnp.float32)
    sigmoid_gate = jax.nn.sigmoid(gate_proj)
    silu_gate = gate_proj * sigmoid_gate
    hidden_act = (silu_gate * up_proj).astype(jnp.bfloat16)
    mlp_share = lax.psum_scatter(
        jnp.dot(hidden_act, w_down, preferred_element_type=jnp.float32),
        "tensor",
        scatter_dimension=0,
        tiled=True,
    )
    result_share = (hidden_share + branch_scale * mlp_share).astype(jnp.bfloat16)
    result = lax.all_gather(result_share, "tensor", axis=0, tiled=True)
    prompt_out = result[:own_rows][None]
    cont_out = result[own_rows:].reshape(1, cont_count, CONT_LENGTH, width)
    upstream = jnp.concatenate(
        [prompt_cot[0], cont_cot[0].reshape(cont_rows, width)], axis=0
    ).astype(jnp.float32)
    grad_mlp = (branch_scale * upstream).astype(jnp.bfloat16)
    grad_down = jnp.einsum("rf,rd->fd", hidden_act, grad_mlp, preferred_element_type=jnp.float32)
    grad_hidden = jnp.einsum("rd,fd->rf", grad_mlp, w_down, preferred_element_type=jnp.float32)
    grad_gate_act = (
        grad_hidden * up_proj * sigmoid_gate * (1.0 + gate_proj * (1.0 - sigmoid_gate))
    ).astype(jnp.bfloat16)
    grad_up_act = (grad_hidden * silu_gate).astype(jnp.bfloat16)
    grad_gate = jnp.einsum("rd,rf->df", act_b, grad_gate_act, preferred_element_type=jnp.float32)
    grad_up = jnp.einsum("rd,rf->df", act_b, grad_up_act, preferred_element_type=jnp.float32)
    normed_grad = jnp.einsum(
        "rf,df->rd", grad_gate_act, w_gate, preferred_element_type=jnp.float32
    ) + jnp.einsum("rf,df->rd", grad_up_act, w_up, preferred_element_type=jnp.float32)
    normed_share = lax.psum_scatter(normed_grad, "tensor", scatter_dimension=0, tiled=True)
    through_mlp, gain_mlp_part = norm_back(hidden_share, gain_mlp, normed_share)
    res_share = share_of(upstream) + through_mlp
    grad_res, gain_mlp_parts = (
        lax.all_gather(res_share, "tensor", axis=0, tiled=True),
        lax.all_gather(gain_mlp_part[None], "tensor", axis=0, tiled=True),
    )
    grad_norm_mlp = jnp.sum(gain_mlp_parts, axis=0)
    grad_attn = (branch_scale * grad_res).astype(jnp.bfloat16)
    grad_out = jnp.einsum("rq,rd->qd", mixed_heads, grad_attn, preferred_element_type=jnp.float32)
    grad_mixed = jnp.einsum(
        "rd,qd->rq", grad_attn, w_out, preferred_element_type=jnp.float32
    ).astype(jnp.bfloat16)
    query_grads = []
    block_index = 0
    low_row = block_index * block_rows
    block_queries = query_rows[low_row : low_row + block_rows]
    block_grad = grad_mixed[low_row : low_row + block_rows]
    grad_query_block, grad_key_block, grad_value_block = attend_backward(
        block_queries,
        shared_prompt_keys,
        shared_prompt_values,
        block_masks[block_index],
        total_list[block_index],
        block_grad,
    )
    query_grads.append(grad_query_block)
    prompt_key_grad = grad_key_block
    prompt_value_grad = grad_value_block
    grad_query_cont, grad_key_cont, grad_value_cont = attend_backward(
        query_rows[own_rows:], cont_keys, cont_values, cont_mask, total_cont, grad_mixed[own_rows:]
    )
    query_grads.append(grad_query_cont)
    prompt_key_grad = prompt_key_grad + grad_key_cont[:prompt_total]
    prompt_value_grad = prompt_value_grad + grad_value_cont[:prompt_total]
    pair_grads = lax.psum_scatter(
        jnp.concatenate([prompt_key_grad, prompt_value_grad], axis=1),
        "ctx",
        scatter_dimension=0,
        tiled=True,
    )
    key_grad_rows = jnp.concatenate(
        [pair_grads[:, :key_width], grad_key_cont[prompt_total:]], axis=0
    )
    value_grad_rows = jnp.concatenate(
        [pair_grads[:, key_width:], grad_value_cont[prompt_total:]], axis=0
    )
    query_grad_rows = jnp.concatenate(query_grads, axis=0)
    grad_query_lin = rotate(query_grad_rows, cos_table, -sin_table).astype(jnp.bfloat16)
    grad_key_lin = rotate(key_grad_rows, cos_table, -sin_table).astype(jnp.bfloat16)
    grad_value_lin = value_grad_rows.astype(jnp.bfloat16)
    grad_query = jnp.einsum("rd,rq->dq", act_a, grad_query_lin, preferred_element_type=jnp.float32)
    grad_key = jnp.einsum("rd,rq->dq", act_a, grad_key_lin, preferred_element_type=jnp.float32)
    grad_value = jnp.einsum("rd,rq->dq", act_a, grad_value_lin, preferred_element_type=jnp.float32)
    input_grad = (
        jnp.einsum("rq,dq->rd", grad_query_lin, w_query, preferred_element_type=jnp.float32)
        + jnp.einsum("rq,dq->rd", grad_key_lin, key_weight, preferred_element_type=jnp.float32)
        + jnp.einsum("rq,dq->rd", grad_value_lin, value_weight, preferred_element_type=jnp.float32)
    )
    input_grad_share = lax.psum_scatter(input_grad, "tensor", scatter_dimension=0, tiled=True)
    through_attn, gain_attn_part = norm_back(input_share, gain_attn, input_grad_share)
    grad_rows, gain_attn_parts = (
        lax.all_gather(res_share + through_attn, "tensor", axis=0, tiled=True),
        lax.all_gather(gain_attn_part[None], "tensor", axis=0, tiled=True),
    )
    grad_norm_attn = jnp.sum(gain_attn_parts, axis=0)
    grad_input = grad_rows.astype(jnp.bfloat16)
    prompt_grad = grad_input[:own_rows][None]
    cont_grad = grad_input[own_rows:].reshape(1, cont_count, CONT_LENGTH, width)
    summed = (
        lax.psum_scatter(grad_norm_attn, ("dp", "ctx"), scatter_dimension=0, tiled=True),
        lax.psum_scatter(grad_query, ("dp", "ctx"), scatter_dimension=0, tiled=True),
        lax.psum_scatter(grad_key, ("dp", "ctx"), scatter_dimension=0, tiled=True),
        lax.psum_scatter(grad_value, ("dp", "ctx"), scatter_dimension=0, tiled=True),
        lax.psum_scatter(grad_out, ("dp", "ctx"), scatter_dimension=1, tiled=True),
        lax.psum_scatter(grad_norm_mlp, ("dp", "ctx"), scatter_dimension=0, tiled=True),
        lax.psum_scatter(grad_gate, ("dp", "ctx"), scatter_dimension=0, tiled=True),
        lax.psum_scatter(grad_up, ("dp", "ctx"), scatter_dimension=0, tiled=True),
        lax.psum_scatter(grad_down, ("dp", "ctx"), scatter_dimension=1, tiled=True),
    )
    return (
        prompt_out,
        cont_out,
        prompt_grad,
        cont_grad,
        summed[0],
        summed[1],
        summed[2],
        summed[3],
        summed[4],
        summed[5],
        summed[6],
        summed[7],
        summed[8],
    )


def solution(mesh):
    in_specs = (
        P("dp", "ctx", None),
        P("dp", "ctx", None, None),
        P("dp"),
        P(),
        P(None, "tensor"),
        P(None, "tensor"),
        P(None, "tensor"),
        P("tensor", None),
        P(),
        P(None, "tensor"),
        P(None, "tensor"),
        P("tensor", None),
        P("dp", "ctx", None),
        P("dp", "ctx", None, None),
    )
    out_specs = (
        P("dp", "ctx", None),
        P("dp", "ctx", None, None),
        P("dp", "ctx", None),
        P("dp", "ctx", None, None),
        P(("dp", "ctx")),
        P(("dp", "ctx"), "tensor"),
        P(("dp", "ctx"), "tensor"),
        P(("dp", "ctx"), "tensor"),
        P("tensor", ("dp", "ctx")),
        P(("dp", "ctx")),
        P(("dp", "ctx"), "tensor"),
        P(("dp", "ctx"), "tensor"),
        P("tensor", ("dp", "ctx")),
    )
    return jax.shard_map(shards, mesh=mesh, in_specs=in_specs, out_specs=out_specs, check_vma=False)
```

profile of v0, /device:TPU:0, one launch (start us, length us, event | category | flops | bytes accessed | tf_op | source)
XLA Modules:
  0.0 1842.2 jit_solution(2165430167676067746)
XLA Ops:
  65.2 10.5 fusion.61
  85.9 10.5 fusion.25
  109.4 140.9 %reduce-scatter.13.cloned.1.call-done = f32[256,2048]{1,0:T(8,128)} async-done(((f32[1024,2048]{1,0:T(8,128)}), f32[256,2048]{1,0:T(8,128)}) %reduce-scatter.13.cloned.1.call-update) | async-done | bytes 2097168 | tf_op jit(solution)/shard_map/reduce_scatter | solution.py:207
  256.2 81.5 %all-gather.7.cloned.1.call-done = bf16[1024,2048]{1,0:T(8,128)(2,1)} async-done(((bf16[256,2048]{1,0:T(8,128)(2,1)}), bf16[1024,2048]{1,0:T(8,128)(2,1)}) %all-gather.7.cloned.1.call-update) | async-done | bytes 4194320 | tf_op jit(solution)/shard_map/all_gather | solution.py:215
  337.6 15.4 fusion.65
  353.1 13.2 fusion.64
  366.3 20.7 %multiply_convert_fusion.1 = (bf16[1024,2048]{1,0:T(8,128)(2,1)}, bf16[1024,2048]{1,0:T(8,128)(2,1)}, bf16[1024,2048]{1,0:T(8,128)(2,1)}) fusion(f32[1024,2048]{1,0:T(8,128)} %fusion.64, f32[1024,2048]{1,0:T(8,128)} %fusion.65, bf16[2048,2048]{1,0:T(8,128)(2,1)} %param.25, bf16[512,2048]{1,0:T(8,128)(2,1)} %bitcast.217, bf16[512,2048]{1,0:T(8,128)(2,1)} %bitcast.220), kind=kOutput, calls=%fused_computation.21 | convolution fusion | flops 8633974784 | bytes 41943040 | tf_op jit(solution)/shard_map/rd,fd->rf/dot_general | solution.py:236
  387.0 13.1 fusion.67
  400.2 13.5 convolution_add_fusion
  413.7 14.4 fusion.66
  434.6 122.3 %reduce-scatter.17.cloned.1.call-done = f32[256,2048]{1,0:T(8,128)} async-done(((f32[1024,2048]{1,0:T(8,128)}), f32[256,2048]{1,0:T(8,128)}) %reduce-scatter.17.cloned.1.call-update) | async-done | bytes 2097168 | tf_op jit(solution)/shard_map/reduce_scatter | solution.py:246
  560.3 144.1 %reduce-scatter.15.cloned.1.call-done = f32[256,2048]{1,0:T(8,128)} async-done(((f32[1024,2048]{1,0:T(8,128)}), f32[256,2048]{1,0:T(8,128)}) %reduce-scatter.15.cloned.1.call-update) | async-done | bytes 2097168 | tf_op jit(solution)/shard_map/reduce_scatter | solution.py:221
  710.3 150.3 %all-gather.11.cloned.1.call-done = f32[1024,2048]{1,0:T(8,128)} async-done(((f32[256,2048]{1,0:T(8,128)}), f32[1024,2048]{1,0:T(8,128)}) %all-gather.11.cloned.1.call-update) | async-done | bytes 8388624 | tf_op jit(solution)/shard_map/all_gather | solution.py:250
  885.8 11.8 fusion.4
  897.6 15.8 fusion
  913.4 17.0 fusion.2
  934.3 12.8 fusion.6
  979.3 142.5 %reduce-scatter.21.cloned.1.call-done = f32[256,2048]{1,0:T(8,128)} async-done(((f32[1024,2048]{1,0:T(8,128)}), f32[256,2048]{1,0:T(8,128)}) %reduce-scatter.21.cloned.1.call-update) | async-done | bytes 2097168 | tf_op jit(solution)/shard_map/reduce_scatter | solution.py:305
  1128.4 15.9 fusion.20
  1144.3 15.3 fusion.73
  1159.7 15.4 fusion.72
  1200.2 13.9 all-gather.1
  1219.4 13.9 all-gather
  1233.3 23.9 %all-reduce.2 = (f32[2048]{0:T(1024)S(1)}, f32[2048]{0:T(1024)S(1)}) all-reduce(f32[2048]{0:T(1024)S(1)} %reduce_sum.131, f32[2048]{0:T(1024)S(1)} %reduce_sum.133), channel_id=9, replica_groups=mesh['dp'=4,'ctx'=2,'tensor'=4] {'dp','ctx'}, use_global_device_ids=true, to_apply=%region_18.19.clone | all-reduce | flops 4096 | bytes 32768
  1258.5 28.6 %all-gather.13.cloned.1.call-done = bf16[1024,2048]{1,0:T(8,128)(2,1)} async-done(((bf16[256,2048]{1,0:T(8,128)(2,1)}), bf16[1024,2048]{1,0:T(8,128)(2,1)}) %all-gather.13.cloned.1.call-update) | async-done | bytes 4194320 | tf_op jit(solution)/shard_map/all_gather | solution.py:308
  1291.9 113.8 %reduce-scatter.35.cloned.1.call-done = f32[2048,256]{1,0:T(8,128)} async-done(((f32[2048,2048]{1,0:T(8,128)}), f32[2048,256]{1,0:T(8,128)}) %reduce-scatter.35.cloned.1.call-update) | async-done | bytes 2097168 | tf_op jit(solution)/shard_map/reduce_scatter | solution.py:324
  1405.7 120.4 %reduce-scatter.33.cloned.1.call-done = f32[256,2048]{1,0:T(8,128)} async-done(((f32[2048,2048]{1,0:T(8,128)}), f32[256,2048]{1,0:T(8,128)}) %reduce-scatter.33.cloned.1.call-update) | async-done | bytes 2097168 | tf_op jit(solution)/shard_map/reduce_scatter | solution.py:323
  1526.0 120.2 %reduce-scatter.31.cloned.1.call-done = f32[256,2048]{1,0:T(8,128)} async-done(((f32[2048,2048]{1,0:T(8,128)}), f32[256,2048]{1,0:T(8,128)}) %reduce-scatter.31.cloned.1.call-update) | async-done | bytes 2097168 | tf_op jit(solution)/shard_map/reduce_scatter | solution.py:322
  1646.3 39.7 %reduce-scatter.25.cloned.1.call-done = f32[256,128]{1,0:T(8,128)} async-done(((f32[2048,128]{1,0:T(8,128)}), f32[256,128]{1,0:T(8,128)}) %reduce-scatter.25.cloned.1.call-update) | async-done | bytes 131088 | tf_op jit(solution)/shard_map/reduce_scatter | solution.py:318
  1686.0 39.6 %reduce-scatter.27.cloned.1.call-done = f32[256,128]{1,0:T(8,128)} async-done(((f32[2048,128]{1,0:T(8,128)}), f32[256,128]{1,0:T(8,128)}) %reduce-scatter.27.cloned.1.call-update) | async-done | bytes 131088 | tf_op jit(solution)/shard_map/reduce_scatter | solution.py:319
  1725.6 54.9 %reduce-scatter.29.cloned.1.call-done = f32[512,256]{1,0:T(8,128)} async-done(((f32[512,2048]{1,0:T(8,128)}), f32[512,256]{1,0:T(8,128)}) %reduce-scatter.29.cloned.1.call-update) | async-done | bytes 524304 | tf_op jit(solution)/shard_map/reduce_scatter | solution.py:320
  1780.5 55.0 %reduce-scatter.23.cloned.1.call-done = f32[256,512]{1,0:T(8,128)} async-done(((f32[2048,512]{1,0:T(8,128)}), f32[256,512]{1,0:T(8,128)}) %reduce-scatter.23.cloned.1.call-update) | async-done | bytes 524304 | tf_op jit(solution)/shard_map/reduce_scatter | solution.py:317
  (228 shorter events, 204.9 us)
Async XLA Ops:
  7.2 90.0 %copy-start = (bf16[512,2048]{1,0:T(8,128)(2,1)S(1)}, bf16[512,2048]{1,0:T(8,128)(2,1)}, u32[]{:S(2)}) copy-start(bf16[512,2048]{1,0:T(8,128)(2,1)} %param.21) | copy-start | bytes 6291460
  7.2 243.1 %reduce-scatter.13.cloned.1.call-start = ((), (), s32[]{:S(2)}) async-start(), calls=%async_computation.12 | async-start | bytes 10485760 | tf_op jit(solution)/shard_map/reduce_scatter | solution.py:207
  11.9 43.1 %copy-start.6 = (pred[512,1024]{0,1:T(8,128)(4,1)}, pred[512,1024]{0,1:T(8,128)(4,1)S(1)}, u32[]{:S(2)}) copy-start(pred[512,1024]{0,1:T(8,128)(4,1)S(1)} %fusion.19) | copy-start | bytes 1572868
  19.6 15.1 copy-start.16
  29.2 56.6 %copy-start.14 = (bf16[1536,128]{0,1:T(8,128)(2,1)}, bf16[1536,128]{0,1:T(8,128)(2,1)S(1)}, u32[]{:S(2)}) copy-start(bf16[1536,128]{0,1:T(8,128)(2,1)S(1)} %copy.77) | copy-start | bytes 1179652
  36.8 28.4 %copy-start.12 = (bf16[512,8,2,32]{0,3,2,1:T(8,128)(2,1)}, bf16[512,8,2,32]{0,3,2,1:T(8,128)(2,1)S(1)}, u32[]{:S(2)}) copy-start(bf16[512,8,2,32]{0,3,2,1:T(8,128)(2,1)S(1)} %get-tuple-element.38) | copy-start | bytes 1572868
  65.2 31.2 %copy-start.47 = (bf16[2,64,4,512]{3,1,2,0:T(8,128)(2,1)}, bf16[2,64,4,512]{3,1,2,0:T(8,128)(2,1)S(1)}, u32[]{:S(2)}) copy-start(bf16[2,64,4,512]{3,1,2,0:T(8,128)(2,1)S(1)} %convolution_convert_fusion) | copy-start | bytes 1572868
  102.9 234.7 %all-gather.7.cloned.1.call-start = ((), (), s32[]{:S(2)}) async-start(), calls=%async_computation.13 | async-start | bytes 5242880 | tf_op jit(solution)/shard_map/all_gather | solution.py:215
  256.1 300.8 %reduce-scatter.17.cloned.1.call-start = ((), (), s32[]{:S(2)}) async-start(), calls=%async_computation.16 | async-start | bytes 10485760 | tf_op jit(solution)/shard_map/reduce_scatter | solution.py:246
  337.6 15.4 copy-start.45
  387.0 13.2 copy-start.50
  413.7 290.7 %reduce-scatter.15.cloned.1.call-start = ((), (), s32[]{:S(2)}) async-start(), calls=%async_computation.14 | async-start | bytes 10485760 | tf_op jit(solution)/shard_map/reduce_scatter | solution.py:221
  428.2 432.4 %all-gather.11.cloned.1.call-start = ((), (), s32[]{:S(2)}) async-start(), calls=%async_computation.17 | async-start | bytes 10485760 | tf_op jit(solution)/shard_map/all_gather | solution.py:250
  710.2 156.2 %copy-start.37 = (f32[1,8,512]{2,1,0:T(8,128)S(1)}, f32[1,8,512]{2,1,0:T(8,128)}, u32[]{:S(2)}) copy-start(f32[1,8,512]{2,1,0:T(8,128)} %copy-done.36) | copy-start | bytes 49156
  710.2 259.6 %reduce-scatter.19.cloned.1.call-start = ((), (), s32[]{:S(2)}) async-start(), calls=%async_computation.18 | async-start | bytes 1572864 | tf_op jit(solution)/shard_map/reduce_scatter | solution.py:281
  913.4 17.0 copy-start.13
  930.3 16.7 copy-start.2
  934.2 12.9 copy-start.9
  934.3 12.9 copy-start.11
  951.4 170.3 %reduce-scatter.21.cloned.1.call-start = ((), (), s32[]{:S(2)}) async-start(), calls=%async_computation.19 | async-start | bytes 10485760 | tf_op jit(solution)/shard_map/reduce_scatter | solution.py:305
  978.4 143.3 %copy-start.41 = (f32[2048]{0:T(1024)S(1)}, f32[2048]{0:T(1024)}, u32[]{:S(2)}) copy-start(f32[2048]{0:T(1024)} %copy-done.40) | copy-start | bytes 24580
  978.4 146.2 %copy-start.8 = (f32[256,2048]{1,0:T(8,128)S(1)}, f32[256,2048]{1,0:T(8,128)}, u32[]{:S(2)}) copy-start(f32[256,2048]{1,0:T(8,128)} %get-tuple-element.33) | copy-start | bytes 6291460
  978.4 235.7 %all-gather.9.cloned.1.call-start = ((), (), s32[]{:S(2)}) async-start(), calls=%async_computation.15 | async-start | bytes 5242880 | tf_op jit(solution)/shard_map/all_gather | solution.py:228
  979.2 307.9 %all-gather.13.cloned.1.call-start = ((), (), s32[]{:S(2)}) async-start(), calls=%async_computation.20 | async-start | bytes 5242880 | tf_op jit(solution)/shard_map/all_gather | solution.py:308
  1128.3 277.3 %reduce-scatter.35.cloned.1.call-start = ((), (), s32[]{:S(2)}) async-start(), calls=%async_computation.27 | async-start | bytes 18874368 | tf_op jit(solution)/shard_map/reduce_scatter | solution.py:324
  1144.3 381.8 %reduce-scatter.33.cloned.1.call-start = ((), (), s32[]{:S(2)}) async-start(), calls=%async_computation.26 | async-start | bytes 18874368 | tf_op jit(solution)/shard_map/reduce_scatter | solution.py:323
  1159.6 486.6 %reduce-scatter.31.cloned.1.call-start = ((), (), s32[]{:S(2)}) async-start(), calls=%async_computation.25 | async-start | bytes 18874368 | tf_op jit(solution)/shard_map/reduce_scatter | solution.py:322
  1175.1 510.9 %reduce-scatter.25.cloned.1.call-start = ((), (), s32[]{:S(2)}) async-start(), calls=%async_computation.22 | async-start | bytes 1179648 | tf_op jit(solution)/shard_map/reduce_scatter | solution.py:318
  1179.8 545.8 %reduce-scatter.27.cloned.1.call-start = ((), (), s32[]{:S(2)}) async-start(), calls=%async_computation.23 | async-start | bytes 1179648 | tf_op jit(solution)/shard_map/reduce_scatter | solution.py:319
  1184.3 596.1 %reduce-scatter.29.cloned.1.call-start = ((), (), s32[]{:S(2)}) async-start(), calls=%async_computation.24 | async-start | bytes 4718592 | tf_op jit(solution)/shard_map/reduce_scatter | solution.py:320
  1192.2 643.2 %reduce-scatter.23.cloned.1.call-start = ((), (), s32[]{:S(2)}) async-start(), calls=%async_computation.21 | async-start | bytes 4718592 | tf_op jit(solution)/shard_map/reduce_scatter | solution.py:317
  1214.1 621.4 %copy-start.1 = (bf16[512,2048]{1,0:T(8,128)(2,1)S(1)}, bf16[512,2048]{1,0:T(8,128)(2,1)}, u32[]{:S(2)}) copy-start(bf16[512,2048]{1,0:T(8,128)(2,1)} %param.21) | copy-start | bytes 6291460
  (38 other events, 240.1 us)
Sparse Core Ops, SparseCore 0:
  103.0 147.2 reduce-scatter.12
  256.2 81.3 all-gather.6
  413.8 143.0 reduce-scatter.16
  559.1 145.2 reduce-scatter.14
  710.3 150.2 all-gather.10
  951.5 6.5 reduce-scatter.18
  978.6 143.1 reduce-scatter.20
  1123.9 81.4 all-gather.8
  1207.5 79.5 all-gather.12
  1291.1 114.5 reduce-scatter.34
  1409.8 116.1 reduce-scatter.32
  1530.0 116.1 reduce-scatter.30
  1650.0 35.9 reduce-scatter.24
  1689.6 35.9 reduce-scatter.26
  1729.4 51.0 reduce-scatter.28
  1784.3 51.1 reduce-scatter.22
where the time goes:
time: 1850 us; the launch traced here: 1840 us
  waiting for transfers between devices  1350 us (73%)
  matrix products  296 us (16%)
  other arithmetic  96.5 us (5%)
  blocking collectives  54 us (3%)
  local copies, waits for them, and re-layouts  23.9 us (1%)
    all_gather x1, waiting for transfers between devices, shards(): lax.all_gather(res_share, 'tensor', axis=0, tiled=True)  150 us
    reduce_scatter x1, waiting for transfers between devices, shards(): lax.psum_scatter(jnp.dot(hidden_act, w_down, preferred_element_type=jnp.f...  144 us
    reduce_scatter x1, waiting for transfers between devices, shards(): lax.psum_scatter(input_grad, 'tensor', scatter_dimension=0, tiled=True)  142 us
    reduce_scatter x1, waiting for transfers between devices, shards(): lax.psum_scatter(jnp.dot(mixed_heads, w_out, preferred_element_type=jnp.f...  141 us
    reduce_scatter x1, waiting for transfers between devices, shards(): lax.psum_scatter(normed_grad, 'tensor', scatter_dimension=0, tiled=True)  122 us
    reduce_scatter x1, waiting for transfers between devices, shards(): lax.psum_scatter(grad_up, ('dp', 'ctx'), scatter_dimension=0, tiled=True)  120 us
    reduce_scatter x1, waiting for transfers between devices, shards(): lax.psum_scatter(grad_gate, ('dp', 'ctx'), scatter_dimension=0, tiled=True)  120 us
    reduce_scatter x1, waiting for transfers between devices, shards(): lax.psum_scatter(grad_down, ('dp', 'ctx'), scatter_dimension=1, tiled=True)  114 us
  transfers between devices with their start and end apart: 16, of which 14 were waited for; matrix products, arithmetic and copies ran while one was open for 7% of the time, Pallas kernels for 0%

commit v1 on v0

--- a/solution.py
+++ b/solution.py
@@ -117,6 +117,12 @@
         grad_key.reshape(joined_keys.shape[0], -1),
         grad_value.reshape(joined_keys.shape[0], -1),
     )
+
+
+def sum_share(values):
+    return lax.psum_scatter(
+        values.astype(jnp.bfloat16), "tensor", scatter_dimension=0, tiled=True
+    ).astype(jnp.float32)
 
 
 def shards(
@@ -204,12 +210,7 @@
         query_rows[own_rows:], cont_keys, cont_values, cont_mask
     )
     mixed_heads = jnp.concatenate(mixed_list + [mixed_cont], axis=0).astype(jnp.bfloat16)
-    attn_share = lax.psum_scatter(
-        jnp.dot(mixed_heads, w_out, preferred_element_type=jnp.float32),
-        "tensor",
-        scatter_dimension=0,
-        tiled=True,
-    )
+    attn_share = sum_share(jnp.dot(mixed_heads, w_out, preferred_element_type=jnp.float32))
     hidden_share = input_share + branch_scale * attn_share
     act_b_share = norm_rows(hidden_share, gain_mlp).astype(jnp.bfloat16)
     act_b = lax.all_gather(act_b_share, "tensor", axis=0, tiled=True)
@@ -218,12 +219,7 @@
     sigmoid_gate = jax.nn.sigmoid(gate_proj)
     silu_gate = gate_proj * sigmoid_gate
     hidden_act = (silu_gate * up_proj).astype(jnp.bfloat16)
-    mlp_share = lax.psum_scatter(
-        jnp.dot(hidden_act, w_down, preferred_element_type=jnp.float32),
-        "tensor",
-        scatter_dimension=0,
-        tiled=True,
-    )
+    mlp_share = sum_share(jnp.dot(hidden_act, w_down, preferred_element_type=jnp.float32))
     result_share = (hidden_share + branch_scale * mlp_share).astype(jnp.bfloat16)
     result = lax.all_gather(result_share, "tensor", axis=0, tiled=True)
     prompt_out = result[:own_rows][None]
@@ -232,7 +228,7 @@
         [prompt_cot[0], cont_cot[0].reshape(cont_rows, width)], axis=0
     ).astype(jnp.float32)
     grad_mlp = (branch_scale * upstream).astype(jnp.bfloat16)
-    grad_down = jnp.einsum("rf,rd->fd", hidden_act, grad_mlp, preferred_element_type=jnp.float32)
+    grad_down = jnp.einsum("rf,rd->df", hidden_act, grad_mlp, preferred_element_type=jnp.float32)
     grad_hidden = jnp.einsum("rd,fd->rf", grad_mlp, w_down, preferred_element_type=jnp.float32)
     grad_gate_act = (
         grad_hidden * up_proj * sigmoid_gate * (1.0 + gate_proj * (1.0 - sigmoid_gate))
@@ -243,16 +239,13 @@
     normed_grad = jnp.einsum(
         "rf,df->rd", grad_gate_act, w_gate, preferred_element_type=jnp.float32
     ) + jnp.einsum("rf,df->rd", grad_up_act, w_up, preferred_element_type=jnp.float32)
-    normed_share = lax.psum_scatter(normed_grad, "tensor", scatter_dimension=0, tiled=True)
+    normed_share = sum_share(normed_grad)
     through_mlp, gain_mlp_part = norm_back(hidden_share, gain_mlp, normed_share)
     res_share = share_of(upstream) + through_mlp
-    grad_res, gain_mlp_parts = (
-        lax.all_gather(res_share, "tensor", axis=0, tiled=True),
-        lax.all_gather(gain_mlp_part[None], "tensor", axis=0, tiled=True),
-    )
-    grad_norm_mlp = jnp.sum(gain_mlp_parts, axis=0)
-    grad_attn = (branch_scale * grad_res).astype(jnp.bfloat16)
-    grad_out = jnp.einsum("rq,rd->qd", mixed_heads, grad_attn, preferred_element_type=jnp.float32)
+    grad_attn = lax.all_gather(
+        (branch_scale * res_share).astype(jnp.bfloat16), "tensor", axis=0, tiled=True
+    )
+    grad_out = jnp.einsum("rq,rd->dq", mixed_heads, grad_attn, preferred_element_type=jnp.float32)
     grad_mixed = jnp.einsum(
         "rd,qd->rq", grad_attn, w_out, preferred_element_type=jnp.float32
     ).astype(jnp.bfloat16)
@@ -302,26 +295,41 @@
         + jnp.einsum("rq,dq->rd", grad_key_lin, key_weight, preferred_element_type=jnp.float32)
         + jnp.einsum("rq,dq->rd", grad_value_lin, value_weight, preferred_element_type=jnp.float32)
     )
-    input_grad_share = lax.psum_scatter(input_grad, "tensor", scatter_dimension=0, tiled=True)
+    input_grad_share = sum_share(input_grad)
     through_attn, gain_attn_part = norm_back(input_share, gain_attn, input_grad_share)
-    grad_rows, gain_attn_parts = (
-        lax.all_gather(res_share + through_attn, "tensor", axis=0, tiled=True),
-        lax.all_gather(gain_attn_part[None], "tensor", axis=0, tiled=True),
-    )
-    grad_norm_attn = jnp.sum(gain_attn_parts, axis=0)
-    grad_input = grad_rows.astype(jnp.bfloat16)
+    grad_input = lax.all_gather(
+        (res_share + through_attn).astype(jnp.bfloat16), "tensor", axis=0, tiled=True
+    )
     prompt_grad = grad_input[:own_rows][None]
     cont_grad = grad_input[own_rows:].reshape(1, cont_count, CONT_LENGTH, width)
+    gain_parts = lax.psum(jnp.stack([gain_attn_part, gain_mlp_part]), ("dp", "ctx", "tensor"))
+    gain_rows = width // (lax.axis_size("dp") * lax.axis_size("ctx"))
+    gain_start = (lax.axis_index("dp") * lax.axis_size("ctx") + ctx_index) * gain_rows
+    gain_own = lax.dynamic_slice_in_dim(gain_parts, gain_start, gain_rows, 1)
+    mlp_sum = lax.psum_scatter(
+        jnp.concatenate([grad_gate, grad_up, grad_down], axis=1).astype(jnp.bfloat16),
+        ("dp", "ctx"),
+        scatter_dimension=0,
+        tiled=True,
+    ).astype(jnp.float32)
+    attn_sum = lax.psum_scatter(
+        jnp.concatenate([grad_query, grad_key, grad_value, grad_out], axis=1).astype(jnp.bfloat16),
+        ("dp", "ctx"),
+        scatter_dimension=0,
+        tiled=True,
+    ).astype(jnp.float32)
+    ff = grad_gate.shape[1]
+    qw = grad_query.shape[1]
     summed = (
-        lax.psum_scatter(grad_norm_attn, ("dp", "ctx"), scatter_dimension=0, tiled=True),
-        lax.psum_scatter(grad_query, ("dp", "ctx"), scatter_dimension=0, tiled=True),
-        lax.psum_scatter(grad_key, ("dp", "ctx"), scatter_dimension=0, tiled=True),
-        lax.psum_scatter(grad_value, ("dp", "ctx"), scatter_dimension=0, tiled=True),
-        lax.psum_scatter(grad_out, ("dp", "ctx"), scatter_dimension=1, tiled=True),
-        lax.psum_scatter(grad_norm_mlp, ("dp", "ctx"), scatter_dimension=0, tiled=True),
-        lax.psum_scatter(grad_gate, ("dp", "ctx"), scatter_dimension=0, tiled=True),
-        lax.psum_scatter(grad_up, ("dp", "ctx"), scatter_dimension=0, tiled=True),
-        lax.psum_scatter(grad_down, ("dp", "ctx"), scatter_dimension=1, tiled=True),
+        gain_own[0],
+        attn_sum[:, :qw],
+        attn_sum[:, qw : qw + key_width],
+        attn_sum[:, qw + key_width : qw + 2 * key_width],
+        attn_sum[:, qw + 2 * key_width :].T,
+        gain_own[1],
+        mlp_sum[:, :ff],
+        mlp_sum[:, ff : 2 * ff],
+        mlp_sum[:, 2 * ff :].T,
     )
     return (
         prompt_out,

time: 1850 us -> 1200 us (0.65)
  waiting for transfers between devices: 1350 us -> 683 us
  other arithmetic: 96.5 us -> 128 us
    reduce_scatter x11 -> x6, waiting for transfers between devices: 1090 us -> 414 us  [the longest x4 261 us: sum_share(): lax.psum_scatter(values.astype(jnp.bfloat16), 'tensor', scatter_dimension...]
    all_gather x1, waiting for transfers between devices: 0.02 us -> 76.5 us  [shards(): result = lax.all_gather(result_share, 'tensor', axis=0, tiled=True)]
    all_gather x2, waiting for transfers between devices: 179 us -> 110 us  [the longest x1 81.3 us: shards(): lax.all_gather((branch_scale * res_share).astype(jnp.bfloat16), 'tensor',...]
    psum x0 -> x1, blocking collectives: none -> 46.7 us  [shards(): lax.psum(jnp.stack([gain_attn_part, gain_mlp_part]), ('dp', 'ctx', 'tenso...]
    concatenate x0 -> x2, other arithmetic: none -> 28.6 us  [the longest x1 18.6 us: shards(): jnp.concatenate([grad_gate, grad_up, grad_down], axis=1)]
    all_gather x2 -> x0, blocking collectives: 27.7 us -> none  [the longest x1 13.9 us: shards(): lax.all_gather(gain_mlp_part[None], 'tensor', axis=0, tiled=True)]
    unnamed x1 -> x0, blocking collectives: 23.9 us -> none
  transfers between devices with their start and end apart: 16 -> 11, of which waited for: 14 -> 9; matrix products, arithmetic and copies ran while one was open for 7% -> 12% of each run, Pallas kernels for 0% -> 0%
where the time goes in v1:
time: 1200 us
  waiting for transfers between devices  683 us (57%)
  matrix products  278 us (23%)
  other arithmetic  128 us (11%)
  blocking collectives  49 us (4%)
  local copies, waits for them, and re-layouts  42.1 us (4%)
  between operations  15.9 us (1%)
    reduce_scatter x4, waiting for transfers between devices, sum_share(): lax.psum_scatter(values.astype(jnp.bfloat16), 'tensor', scatter_dimension...  261 us
    reduce_scatter x1, waiting for transfers between devices, shards(): lax.psum_scatter(jnp.concatenate([grad_gate, grad_up, grad_down], axis=1)...  153 us
    all_gather x1, waiting for transfers between devices, shards(): act_b = lax.all_gather(act_b_share, 'tensor', axis=0, tiled=True)  81.4 us
    all_gather x1, waiting for transfers between devices, shards(): lax.all_gather((branch_scale * res_share).astype(jnp.bfloat16), 'tensor',...  81.3 us
    all_gather x1, waiting for transfers between devices, shards(): result = lax.all_gather(result_share, 'tensor', axis=0, tiled=True)  76.5 us
    psum x1, blocking collectives, shards(): lax.psum(jnp.stack([gain_attn_part, gain_mlp_part]), ('dp', 'ctx', 'tenso...  46.7 us
    dot_general x2, matrix products, attend_forward(): jnp.einsum('hgbk,khd->bhgd', weights, value_head_rows, preferred_element_...  32.4 us
    convert_element_type x2, other arithmetic, attend_backward(): grad_scores = (weights * (grad_weights - jnp.sum(grad_weights * weights,...  29.5 us
  transfers between devices with their start and end apart: 11, of which 9 were waited for; matrix products, arithmetic and copies ran while one was open for 12% of the time, Pallas kernels for 0%

profile of v1, /device:TPU:0, one launch (start us, length us, event | category | flops | bytes accessed | tf_op | source)
XLA Modules:
  0.0 1196.5 jit_solution(1936004587753179589)
XLA Ops:
  43.9 9.8 exponential_reduce_fusion.1
  54.5 10.1 convolution_convert_fusion.10
  64.6 10.6 fusion.69
  75.2 10.1 exponential_reduce_fusion
  85.3 22.3 %fusion.34 = bf16[2,64,4,512]{3,1,2,0:T(8,128)(2,1)S(1)} fusion(bf16[1536,2,64,1]{0,2,3,1:T(8,128)(2,1)S(1)} %bitcast.215, f32[2,4,512,1536]{2,3,1,0:T(8,128)} %get-tuple-element.83, f32[2,4,512]{2,1,0:T(4,128)S(1)} %bitcast.248), kind=kOutput, calls=%fused_computation.83 | convolution fusion | flops 818151424 | bytes 26099712 | tf_op jit(solution)/shard_map/hgbk,khd->bhgd/dot_general | solution.py:82
  119.4 73.0 %reduce-scatter.8.cloned.1.call-done = bf16[256,2048]{1,0:T(8,128)(2,1)} async-done(((bf16[1024,2048]{1,0:T(8,128)(2,1)}), bf16[256,2048]{1,0:T(8,128)(2,1)}) %reduce-scatter.8.cloned.1.call-update) | async-done | bytes 1048592 | tf_op jit(solution)/shard_map/reduce_scatter | solution.py:123
  198.0 81.4 %all-gather.5.cloned.1.call-done = bf16[1024,2048]{1,0:T(8,128)(2,1)} async-done(((bf16[256,2048]{1,0:T(8,128)(2,1)}), bf16[1024,2048]{1,0:T(8,128)(2,1)}) %all-gather.5.cloned.1.call-update) | async-done | bytes 4194320 | tf_op jit(solution)/shard_map/all_gather | solution.py:216
  279.4 15.6 %fusion.73 = f32[1024,2048]{1,0:T(8,128)} fusion(bf16[1024,2048]{1,0:T(8,128)(2,1)} %all-gather.5.cloned.1.call-done, bf16[2048,2048]{1,0:T(8,128)(2,1)} %param.24), kind=kOutput, calls=%fused_computation.173 | convolution fusion | flops 8589934592 | bytes 20971520 | tf_op jit(solution)/shard_map/dot_general | solution.py:218
  295.0 13.3 %fusion.72 = f32[1024,2048]{1,0:T(8,128)} fusion(bf16[1024,2048]{1,0:T(8,128)(2,1)S(1)} %copy-done.48, bf16[2048,2048]{1,0:T(8,128)(2,1)} %param.23), kind=kOutput, calls=%fused_computation.172 | convolution fusion | flops 8589934592 | bytes 20971520 | tf_op jit(solution)/shard_map/dot_general | solution.py:217
  308.3 20.8 %multiply_convert_fusion = (bf16[1024,2048]{1,0:T(8,128)(2,1)}, bf16[1024,2048]{1,0:T(8,128)(2,1)}, bf16[1024,2048]{1,0:T(8,128)(2,1)}) fusion(f32[1024,2048]{1,0:T(8,128)} %fusion.72, f32[1024,2048]{1,0:T(8,128)} %fusion.73, bf16[2048,2048]{1,0:T(8,128)(2,1)} %param.25, bf16[512,2048]{1,0:T(8,128)(2,1)} %bitcast.226, bf16[512,2048]{1,0:T(8,128)(2,1)} %bitcast.229), kind=kOutput, calls=%fused_computation.22 | convolution fusion | flops 8633974784 | bytes 41943040 | tf_op jit(solution)/shard_map/rd,fd->rf/dot_general | solution.py:232
  329.1 13.1 %fusion.74 = f32[1024,2048]{1,0:T(8,128)S(1)} fusion(bf16[1024,2048]{1,0:T(8,128)(2,1)} %get-tuple-element.46, bf16[2048,2048]{1,0:T(8,128)(2,1)} %param.23), kind=kOutput, calls=%fused_computation.174 | convolution fusion | flops 8589934592 | bytes 20971520 | tf_op jit(solution)/shard_map/rf,df->rd/dot_general | solution.py:239
  342.3 13.0 %add_convert_fusion.1 = bf16[1024,2048]{1,0:T(8,128)(2,1)} fusion(f32[1024,2048]{1,0:T(8,128)S(1)} %fusion.74, bf16[1024,2048]{1,0:T(8,128)(2,1)S(1)} %copy-done.53, bf16[2048,2048]{1,0:T(8,128)(2,1)} %param.24), kind=kOutput, calls=%fused_computation.21 | convolution fusion | flops 8594128896 | bytes 25165824 | tf_op jit(solution)/shard_map/rf,df->rd/dot_general | solution.py:241
  362.0 68.7 %reduce-scatter.12.cloned.1.call-done = bf16[256,2048]{1,0:T(8,128)(2,1)} async-done(((bf16[1024,2048]{1,0:T(8,128)(2,1)}), bf16[256,2048]{1,0:T(8,128)(2,1)}) %reduce-scatter.12.cloned.1.call-update) | async-done | bytes 1048592 | tf_op jit(solution)/shard_map/reduce_scatter | solution.py:123
  438.2 81.3 %all-gather.9.cloned.1.call-done = bf16[1024,2048]{1,0:T(8,128)(2,1)} async-done(((bf16[256,2048]{1,0:T(8,128)(2,1)}), bf16[1024,2048]{1,0:T(8,128)(2,1)}) %all-gather.9.cloned.1.call-update) | async-done | bytes 4194320 | tf_op jit(solution)/shard_map/all_gather | solution.py:245
  524.2 10.4 fusion.18
  534.7 7.9 fusion.40
  542.6 11.9 fusion.4
  554.6 15.8 %fusion = (f32[2,4,512]{2,1,0:T(4,128)S(1)}, f32[2,1536,512,4]{2,1,3,0:T(8,128)}) fusion(f32[2,4,512,1536]{2,3,1,0:T(8,128)} %get-tuple-element.83, f32[2,4,512]{2,1,0:T(4,128)S(1)} %bitcast.250, bf16[1536,2,64,1]{0,2,3,1:T(8,128)(2,1)S(1)} %bitcast.216, bf16[512,2,4,64]{0,3,2,1:T(8,128)(2,1)S(1)} %bitcast.208), kind=kOutput, calls=%fused_computation.3 | convolution fusion | flops 824176640 | bytes 51281920 | tf_op jit(solution)/shard_map/bhgd,khd->hgbk/dot_general | solution.py:93
  570.4 17.0 %fusion.2 = bf16[2,4,512,1536]{2,3,1,0:T(8,128)(2,1)S(1)} fusion(f32[2,1536,512,4]{2,1,3,0:T(8,128)} %get-tuple-element.87, f32[2,4,512,1536]{2,3,1,0:T(8,128)} %get-tuple-element.83, f32[2,4,512]{2,1,0:T(4,128)S(1)} %get-tuple-element.86, f32[2,4,512]{2,1,0:T(4,128)S(1)} %bitcast.251), kind=kLoop, calls=%fused_computation.5 | loop fusion | flops 25165824 | bytes 62947328 | tf_op jit(solution)/shard_map/convert_element_type | solution.py:98
  591.9 12.6 %fusion.6 = bf16[2,4,512,1024]{2,3,1,0:T(8,128)(2,1)S(1)} fusion(f32[2,1024,512,4]{2,1,3,0:T(8,128)} %get-tuple-element.89, f32[2,1024,512,4]{2,1,3,0:T(8,128)} %get-tuple-element.85, f32[2,4,512]{2,1,0:T(4,128)S(1)} %get-tuple-element.88, f32[2,4,512]{2,1,0:T(4,128)S(1)} %bitcast.255, pred[512,1024]{0,1:T(8,128)(4,1)S(1)} %copy-done.9), kind=kLoop, calls=%fused_computation.14 | loop fusion | flops 25165824 | bytes 42500096 | tf_op jit(solution)/shard_map/convert_element_type | solution.py:98
  638.9 14.3 %convolution_convert_fusion.3 = bf16[1024,2048]{1,0:T(8,128)(2,1)} fusion(bf16[1024,2048]{1,0:T(8,128)(2,1)} %get-tuple-element.47, bf16[2048,2048]{1,0:T(8,128)(2,1)} %param.25), kind=kOutput, calls=%fused_computation.36 | convolution fusion | flops 8592031744 | bytes 16777216 | tf_op jit(solution)/shard_map/dot_general | solution.py:222
  661.9 10.0 pad_maximum_fusion.1
  672.6 42.0 %reduce-scatter.16.cloned.1.call-done = bf16[256,2048]{1,0:T(8,128)(2,1)} async-done(((bf16[1024,2048]{1,0:T(8,128)(2,1)}), bf16[256,2048]{1,0:T(8,128)(2,1)}) %reduce-scatter.16.cloned.1.call-update) | async-done | bytes 1048592 | tf_op jit(solution)/shard_map/reduce_scatter | solution.py:123
  717.3 76.9 %reduce-scatter.10.cloned.1.call-done = bf16[256,2048]{1,0:T(8,128)(2,1)} async-done(((bf16[1024,2048]{1,0:T(8,128)(2,1)}), bf16[256,2048]{1,0:T(8,128)(2,1)}) %reduce-scatter.10.cloned.1.call-update) | async-done | bytes 1048592 | tf_op jit(solution)/shard_map/reduce_scatter | solution.py:123
  800.2 14.1 %convolution_convert_fusion = bf16[2048,2048]{0,1:T(8,128)(2,1)} fusion(bf16[1024,2048]{1,0:T(8,128)(2,1)} %get-tuple-element.47, bf16[512,2048]{1,0:T(8,128)(2,1)} %bitcast.228, bf16[512,2048]{1,0:T(8,128)(2,1)} %bitcast.231), kind=kOutput, calls=%fused_computation.30 | convolution fusion | flops 8606711808 | bytes 16777216 | tf_op jit(solution)/shard_map/rf,rd->df/dot_general | solution.py:231
  814.4 11.4 convolution_convert_fusion.1
  825.8 11.5 convolution_convert_fusion.2
  837.4 18.6 %pad_maximum_fusion = bf16[2048,6144]{0,1:T(8,128)(2,1)} fusion(bf16[2048,2048]{0,1:T(8,128)(2,1)} %convolution_convert_fusion, bf16[2048,2048]{0,1:T(8,128)(2,1)} %convolution_convert_fusion.1, bf16[2048,2048]{0,1:T(8,128)(2,1)} %convolution_convert_fusion.2), kind=kLoop, calls=%fused_computation | loop fusion | flops 75497472 | bytes 50331648 | tf_op jit(solution)/shard_map/concatenate | solution.py:310
  862.5 46.7 %psum.7 = f32[2,2048]{1,0:T(2,128)S(1)} all-reduce(f32[2,2048]{1,0:T(2,128)S(1)} %pad_maximum_fusion.18), channel_id=1, replica_groups=mesh['dp'=4,'ctx'=2,'tensor'=4] {'dp','ctx','tensor'}, use_global_device_ids=true, to_apply=%region_18.19 | all-reduce | flops 4096 | bytes 32768 | tf_op jit(solution)/shard_map/psum | solution.py:305
  909.8 28.7 %all-gather.11.cloned.1.call-done = bf16[1024,2048]{1,0:T(8,128)(2,1)} async-done(((bf16[256,2048]{1,0:T(8,128)(2,1)}), bf16[1024,2048]{1,0:T(8,128)(2,1)}) %all-gather.11.cloned.1.call-update) | async-done | bytes 4194320 | tf_op jit(solution)/shard_map/all_gather | solution.py:300
  943.2 76.5 %all-gather.7.cloned.1.call-done = bf16[1024,2048]{1,0:T(8,128)(2,1)} async-done(((bf16[256,2048]{1,0:T(8,128)(2,1)}), bf16[1024,2048]{1,0:T(8,128)(2,1)}) %all-gather.7.cloned.1.call-update) | async-done | bytes 4194320 | tf_op jit(solution)/shard_map/all_gather | solution.py:224
  1024.5 153.3 %reduce-scatter.20.cloned.1.call-done = bf16[256,6144]{0,1:T(8,128)(2,1)} async-done(((bf16[2048,6144]{0,1:T(8,128)(2,1)}), bf16[256,6144]{0,1:T(8,128)(2,1)}) %reduce-scatter.20.cloned.1.call-update) | async-done | bytes 3145744 | tf_op jit(solution)/shard_map/reduce_scatter | solution.py:309
  (230 shorter events, 157.9 us)
Async XLA Ops:
  7.2 101.3 %copy-start = (bf16[512,2048]{1,0:T(8,128)(2,1)S(1)}, bf16[512,2048]{1,0:T(8,128)(2,1)}, u32[]{:S(2)}) copy-start(bf16[512,2048]{1,0:T(8,128)(2,1)} %param.21) | copy-start | bytes 6291460
  7.2 185.2 %reduce-scatter.8.cloned.1.call-start = ((), (), s32[]{:S(2)}) async-start(), calls=%async_computation.7 | async-start | bytes 5242880 | tf_op jit(solution)/shard_map/reduce_scatter | solution.py:123
  12.1 42.3 %copy-start.8 = (pred[512,1024]{0,1:T(8,128)(4,1)}, pred[512,1024]{0,1:T(8,128)(4,1)S(1)}, u32[]{:S(2)}) copy-start(pred[512,1024]{0,1:T(8,128)(4,1)S(1)} %fusion.32) | copy-start | bytes 1572868
  19.2 15.1 %copy-start.18 = (f32[1024,32]{0,1:T(8,128)}, f32[1024,32]{0,1:T(8,128)S(1)}, u32[]{:S(2)}) copy-start(f32[1024,32]{0,1:T(8,128)S(1)} %get-tuple-element.81) | copy-start | bytes 393220
  28.9 56.5 %copy-start.16 = (bf16[1536,128]{0,1:T(8,128)(2,1)}, bf16[1536,128]{0,1:T(8,128)(2,1)S(1)}, u32[]{:S(2)}) copy-start(bf16[1536,128]{0,1:T(8,128)(2,1)S(1)} %copy.54) | copy-start | bytes 1179652
  36.4 28.2 %copy-start.14 = (bf16[512,8,2,32]{0,3,2,1:T(8,128)(2,1)}, bf16[512,8,2,32]{0,3,2,1:T(8,128)(2,1)S(1)}, u32[]{:S(2)}) copy-start(bf16[512,8,2,32]{0,3,2,1:T(8,128)(2,1)S(1)} %get-tuple-element.64) | copy-start | bytes 1572868
  64.6 43.1 %copy-start.51 = (bf16[2,64,4,512]{3,1,2,0:T(8,128)(2,1)}, bf16[2,64,4,512]{3,1,2,0:T(8,128)(2,1)S(1)}, u32[]{:S(2)}) copy-start(bf16[2,64,4,512]{3,1,2,0:T(8,128)(2,1)S(1)} %convolution_convert_fusion.10) | copy-start | bytes 1572868
  112.9 166.5 %all-gather.5.cloned.1.call-start = ((), (), s32[]{:S(2)}) async-start(), calls=%async_computation.8 | async-start | bytes 5242880 | tf_op jit(solution)/shard_map/all_gather | solution.py:216
  112.9 321.0 %copy-start.35 = (f32[2048]{0:T(1024)}, f32[2048]{0:T(1024)S(1)}, u32[]{:S(2)}) copy-start(f32[2048]{0:T(1024)S(1)} %convert_element_type.121) | copy-start | bytes 24580
  195.4 238.5 %copy-start.42 = (f32[256]{0:T(256)}, f32[256]{0:T(256)S(1)}, u32[]{:S(2)}) copy-start(f32[256]{0:T(256)S(1)} %add_rsqrt_fusion.2) | copy-start | bytes 3076
  198.0 232.7 %reduce-scatter.12.cloned.1.call-start = ((), (), s32[]{:S(2)}) async-start(), calls=%async_computation.11 | async-start | bytes 5242880 | tf_op jit(solution)/shard_map/reduce_scatter | solution.py:123
  279.4 15.6 %copy-start.48 = (bf16[1024,2048]{1,0:T(8,128)(2,1)S(1)}, bf16[1024,2048]{1,0:T(8,128)(2,1)}, u32[]{:S(2)}) copy-start(bf16[1024,2048]{1,0:T(8,128)(2,1)} %all-gather.5.cloned.1.call-done) | copy-start | bytes 12582916
  355.2 164.3 %all-gather.9.cloned.1.call-start = ((), (), s32[]{:S(2)}) async-start(), calls=%async_computation.12 | async-start | bytes 5242880 | tf_op jit(solution)/shard_map/all_gather | solution.py:245
  434.0 90.2 %copy-start.44 = (f32[256]{0:T(256)}, f32[256]{0:T(256)S(1)}, u32[]{:S(2)}) copy-start(f32[256]{0:T(256)S(1)} %broadcast_multiply_fusion.1) | copy-start | bytes 3076
  438.2 192.8 %reduce-scatter.14.cloned.1.call-start = ((), (), s32[]{:S(2)}) async-start(), calls=%async_computation.13 | async-start | bytes 1572864 | tf_op jit(solution)/shard_map/reduce_scatter | solution.py:274
  570.4 17.0 %copy-start.15 = (bf16[512,8,2,32]{0,3,2,1:T(8,128)(2,1)S(1)}, bf16[512,8,2,32]{0,3,2,1:T(8,128)(2,1)}, u32[]{:S(2)}) copy-start(bf16[512,8,2,32]{0,3,2,1:T(8,128)(2,1)} %copy-done.14) | copy-start | bytes 1572868
  591.9 15.8 %copy-start.13 = (bf16[512,8,2,32]{0,3,2,1:T(8,128)(2,1)S(1)}, bf16[512,8,2,32]{0,3,2,1:T(8,128)(2,1)}, u32[]{:S(2)}) copy-start(bf16[512,8,2,32]{0,3,2,1:T(8,128)(2,1)} %copy-done.12) | copy-start | bytes 1572868
  611.5 103.1 %reduce-scatter.16.cloned.1.call-start = ((), (), s32[]{:S(2)}) async-start(), calls=%async_computation.14 | async-start | bytes 5242880 | tf_op jit(solution)/shard_map/reduce_scatter | solution.py:123
  638.8 155.4 %reduce-scatter.10.cloned.1.call-start = ((), (), s32[]{:S(2)}) async-start(), calls=%async_computation.9 | async-start | bytes 5242880 | tf_op jit(solution)/shard_map/reduce_scatter | solution.py:123
  638.9 14.4 %copy-start.34 = (bf16[2,64,4,512]{3,1,2,0:T(8,128)(2,1)S(1)}, bf16[2,64,4,512]{3,1,2,0:T(8,128)(2,1)}, u32[]{:S(2)}) copy-start(bf16[2,64,4,512]{3,1,2,0:T(8,128)(2,1)} %copy-done.33) | copy-start | bytes 1572868
  638.9 14.4 %copy-start.52 = (bf16[2,64,4,512]{3,1,2,0:T(8,128)(2,1)S(1)}, bf16[2,64,4,512]{3,1,2,0:T(8,128)(2,1)}, u32[]{:S(2)}) copy-start(bf16[2,64,4,512]{3,1,2,0:T(8,128)(2,1)} %copy-done.51) | copy-start | bytes 1572868
  653.2 202.8 %reduce-scatter.18.cloned.1.call-start = ((), (), s32[]{:S(2)}) async-start(), calls=%async_computation.16 | async-start | bytes 5898240 | tf_op jit(solution)/shard_map/reduce_scatter | solution.py:315
  671.9 42.7 %copy-start.40 = (f32[2048]{0:T(1024)S(1)}, f32[2048]{0:T(1024)}, u32[]{:S(2)}) copy-start(f32[2048]{0:T(1024)} %copy-done.39) | copy-start | bytes 24580
  671.9 122.3 %copy-start.7 = (f32[256,2048]{1,0:T(8,128)S(1)}, f32[256,2048]{1,0:T(8,128)}, u32[]{:S(2)}) copy-start(f32[256,2048]{1,0:T(8,128)} %copy-done.6) | copy-start | bytes 6291460
  671.9 122.3 %copy-start.10 = (bf16[256,2048]{1,0:T(8,128)(2,1)S(1)}, bf16[256,2048]{1,0:T(8,128)(2,1)}, u32[]{:S(2)}) copy-start(bf16[256,2048]{1,0:T(8,128)(2,1)} %reduce-scatter.12.cloned.1.call-done) | copy-start | bytes 3145732
  671.9 122.3 %copy-start.36 = (f32[2048]{0:T(1024)S(1)}, f32[2048]{0:T(1024)}, u32[]{:S(2)}) copy-start(f32[2048]{0:T(1024)} %copy-done.35) | copy-start | bytes 24580
  671.9 122.3 %copy-start.43 = (f32[256]{0:T(256)S(1)}, f32[256]{0:T(256)}, u32[]{:S(2)}) copy-start(f32[256]{0:T(256)} %copy-done.42) | copy-start | bytes 3076
  671.9 122.3 %copy-start.45 = (f32[256]{0:T(256)S(1)}, f32[256]{0:T(256)}, u32[]{:S(2)}) copy-start(f32[256]{0:T(256)} %copy-done.44) | copy-start | bytes 3076
  672.0 266.5 %all-gather.11.cloned.1.call-start = ((), (), s32[]{:S(2)}) async-start(), calls=%async_computation.15 | async-start | bytes 5242880 | tf_op jit(solution)/shard_map/all_gather | solution.py:300
  799.6 220.2 %all-gather.7.cloned.1.call-start = ((), (), s32[]{:S(2)}) async-start(), calls=%async_computation.10 | async-start | bytes 5242880 | tf_op jit(solution)/shard_map/all_gather | solution.py:224
  800.1 377.7 %reduce-scatter.20.cloned.1.call-start = ((), (), s32[]{:S(2)}) async-start(), calls=%async_computation.17 | async-start | bytes 28311552 | tf_op jit(solution)/shard_map/reduce_scatter | solution.py:309
  800.2 14.2 %copy-start.49 = (bf16[1024,2048]{1,0:T(8,128)(2,1)S(1)}, bf16[1024,2048]{1,0:T(8,128)(2,1)}, u32[]{:S(2)}) copy-start(bf16[1024,2048]{1,0:T(8,128)(2,1)} %all-gather.5.cloned.1.call-done) | copy-start | bytes 12582916
  (38 other events, 228.9 us)
Sparse Core Ops, SparseCore 0:
  113.0 79.3 reduce-scatter.7
  198.1 81.2 all-gather.4
  355.4 75.2 reduce-scatter.11
  438.3 81.2 all-gather.8
  611.6 6.8 reduce-scatter.13
  638.9 75.6 reduce-scatter.15
  716.9 77.2 reduce-scatter.9
  797.6 56.8 reduce-scatter.17
  856.7 81.6 all-gather.10
  940.4 79.2 all-gather.6
  1023.3 154.4 reduce-scatter.19

commit v2 on v1

--- a/solution.py
+++ b/solution.py
@@ -1,4 +1,6 @@
+import functools
 import math
+import operator
 
 import jax
 import jax.numpy as jnp
@@ -119,10 +121,67 @@
     )
 
 
-def sum_share(values):
-    return lax.psum_scatter(
-        values.astype(jnp.bfloat16), "tensor", scatter_dimension=0, tiled=True
-    ).astype(jnp.float32)
+def picked(me, arrays, keys):
+    out = None
+    for key in dict.fromkeys(keys.values()):
+        if out is None:
+            out = arrays[key]
+        else:
+            chosen = functools.reduce(
+                operator.or_, [me == device for device, held in keys.items() if held == key]
+            )
+            out = jnp.where(chosen, arrays[key], out)
+    return out
+
+
+def slot_tables(count):
+    chunk_of = []
+    for device in range(count):
+        near = min(device, count - 1 - device)
+        far = 1 if device < count - 1 - device else -1
+        order = [device]
+        for slot in range(1, count):
+            if slot <= 2 * near:
+                distance = (slot + 1) // 2
+                order.append(device - distance if slot % 2 else device + distance)
+            else:
+                order.append(device + far * (slot - near))
+        chunk_of.append(order)
+    return chunk_of
+
+
+def line_hops(share, count):
+    arrived = {0: share}
+    forward = backward = share
+    for step in range(1, count):
+        forward = lax.ppermute(forward, "tensor", [(i, i + 1) for i in range(step - 1, count - 1)])
+        backward = lax.ppermute(backward, "tensor", [(i, i - 1) for i in range(1, count - step + 1)])
+        arrived[-step] = forward
+        arrived[step] = backward
+    return arrived
+
+
+def line_sum(part_at, count):
+    from_left = from_right = None
+    for distance in range(count - 1, 0, -1):
+        to_right = part_at(distance)
+        to_left = part_at(-distance)
+        if from_left is not None:
+            to_right = (to_right.astype(jnp.float32) + from_left.astype(jnp.float32)).astype(
+                jnp.bfloat16
+            )
+            to_left = (to_left.astype(jnp.float32) + from_right.astype(jnp.float32)).astype(
+                jnp.bfloat16
+            )
+        from_left = lax.ppermute(
+            to_right, "tensor", [(i, i + 1) for i in range(0, count - distance)]
+        )
+        from_right = lax.ppermute(to_left, "tensor", [(i, i - 1) for i in range(distance, count)])
+    return (
+        part_at(0).astype(jnp.float32)
+        + from_left.astype(jnp.float32)
+        + from_right.astype(jnp.float32)
+    )
 
 
 def shards(
@@ -148,8 +207,17 @@
     total_rows = own_rows + cont_rows
     key_width = key_weight.shape[1]
     ctx_index = lax.axis_index("ctx")
-    share_rows = total_rows // lax.axis_size("tensor")
-    share_start = lax.axis_index("tensor") * share_rows
+    count = lax.axis_size("tensor")
+    me = lax.axis_index("tensor")
+    share_rows = total_rows // count
+    share_start = me * share_rows
+    head_half = w_out.shape[0] // 2
+    order = slot_tables(count)
+    slot_chunks = [
+        picked(me, {i: jnp.int32(i) for i in range(count)}, {i: order[i][s] for i in range(count)})
+        for s in range(count)
+    ]
+    slot_of = [[order[i].index(c) for c in range(count)] for i in range(count)]
     token_length = prompt_len[0]
     gain_attn = norm_attn.astype(jnp.float32)
     gain_mlp = norm_mlp.astype(jnp.float32)
@@ -157,6 +225,24 @@
     def share_of(values):
         return lax.dynamic_slice_in_dim(values, share_start, share_rows, 0)
 
+    def slot_order(values):
+        return jnp.concatenate(
+            [
+                lax.dynamic_slice_in_dim(values, slot_chunks[s] * share_rows, share_rows, 0)
+                for s in range(count)
+            ],
+            axis=0,
+        )
+
+    def slots_from(share):
+        arrived = line_hops(share, count)
+        return [
+            picked(me, arrived, {i: order[i][s] - i for i in range(count)}) for s in range(count)
+        ]
+
+    own_out_half = lax.dynamic_slice_in_dim(w_out, ctx_index * head_half, head_half, 0)
+    half_out = lax.all_gather(own_out_half, "tensor", axis=0, tiled=True)
+    full_out = lax.all_gather(half_out, "ctx", axis=0, tiled=True)
     all_rows = jnp.concatenate([prompt_in[0], cont_in[0].reshape(cont_rows, width)], axis=0).astype(
         jnp.float32
     )
@@ -210,45 +296,120 @@
         query_rows[own_rows:], cont_keys, cont_values, cont_mask
     )
     mixed_heads = jnp.concatenate(mixed_list + [mixed_cont], axis=0).astype(jnp.bfloat16)
-    attn_share = sum_share(jnp.dot(mixed_heads, w_out, preferred_element_type=jnp.float32))
+    mixed_share = jnp.concatenate(
+        [
+            lax.all_to_all(
+                mixed_heads[:, h * head_half : (h + 1) * head_half],
+                "tensor",
+                split_axis=0,
+                concat_axis=1,
+                tiled=True,
+            )
+            for h in range(2)
+        ],
+        axis=1,
+    )
+    attn_share = jnp.dot(mixed_share, full_out, preferred_element_type=jnp.float32)
     hidden_share = input_share + branch_scale * attn_share
     act_b_share = norm_rows(hidden_share, gain_mlp).astype(jnp.bfloat16)
-    act_b = lax.all_gather(act_b_share, "tensor", axis=0, tiled=True)
-    gate_proj = jnp.dot(act_b, w_gate, preferred_element_type=jnp.float32)
-    up_proj = jnp.dot(act_b, w_up, preferred_element_type=jnp.float32)
-    sigmoid_gate = jax.nn.sigmoid(gate_proj)
-    silu_gate = gate_proj * sigmoid_gate
-    hidden_act = (silu_gate * up_proj).astype(jnp.bfloat16)
-    mlp_share = sum_share(jnp.dot(hidden_act, w_down, preferred_element_type=jnp.float32))
+    upstream = jnp.concatenate([prompt_cot[0], cont_cot[0].reshape(cont_rows, width)], axis=0)
+    grad_mlp = slot_order((branch_scale * upstream.astype(jnp.float32)).astype(jnp.bfloat16))
+    grad_hidden = jnp.einsum("rd,fd->rf", grad_mlp, w_down, preferred_element_type=jnp.float32)
+    act_b_slots = slots_from(act_b_share)
+    hidden_list, gate_list, up_list, part_list = ([], [], [], [])
+    for s in range(count):
+        gate_proj = jnp.dot(act_b_slots[s], w_gate, preferred_element_type=jnp.float32)
+        up_proj = jnp.dot(act_b_slots[s], w_up, preferred_element_type=jnp.float32)
+        sigmoid_gate = jax.nn.sigmoid(gate_proj)
+        silu_gate = gate_proj * sigmoid_gate
+        grad_slot = grad_hidden[s * share_rows : (s + 1) * share_rows]
+        hidden_list.append((silu_gate * up_proj).astype(jnp.bfloat16))
+        gate_list.append(
+            (grad_slot * up_proj * sigmoid_gate * (1.0 + gate_proj * (1.0 - sigmoid_gate))).astype(
+                jnp.bfloat16
+            )
+        )
+        up_list.append((grad_slot * silu_gate).astype(jnp.bfloat16))
+        part_list.append(
+            (
+                jnp.einsum("rf,df->rd", gate_list[s], w_gate, preferred_element_type=jnp.float32)
+                + jnp.einsum("rf,df->rd", up_list[s], w_up, preferred_element_type=jnp.float32)
+            ).astype(jnp.bfloat16)
+        )
+
+    def slot_part(distance):
+        return picked(
+            me,
+            part_list,
+            {
+                i: slot_of[i][i + distance]
+                for i in range(count)
+                if 0 <= i + distance < count
+            },
+        )
+
+    normed_share = line_sum(slot_part, count)
+    through_mlp, gain_mlp_part = norm_back(hidden_share, gain_mlp, normed_share)
+    res_share = share_of(upstream).astype(jnp.float32) + through_mlp
+    grad_attn_share = (branch_scale * res_share).astype(jnp.bfloat16)
+    mixed_grad = jnp.einsum(
+        "rd,qd->rq", grad_attn_share, full_out, preferred_element_type=jnp.float32
+    ).astype(jnp.bfloat16)
+    grad_mixed = jnp.concatenate(
+        [
+            lax.all_to_all(
+                mixed_grad[:, h * count * head_half : (h + 1) * count * head_half],
+                "tensor",
+                split_axis=1,
+                concat_axis=0,
+                tiled=True,
+            )
+            for h in range(2)
+        ],
+        axis=1,
+    )
+    act_b = jnp.concatenate(act_b_slots, axis=0)
+    hidden_act = jnp.concatenate(hidden_list, axis=0)
+    grad_gate_act = jnp.concatenate(gate_list, axis=0)
+    grad_up_act = jnp.concatenate(up_list, axis=0)
+    grad_down = jnp.einsum("rf,rd->df", hidden_act, grad_mlp, preferred_element_type=jnp.float32)
+    grad_gate = jnp.einsum("rd,rf->df", act_b, grad_gate_act, preferred_element_type=jnp.float32)
+    grad_up = jnp.einsum("rd,rf->df", act_b, grad_up_act, preferred_element_type=jnp.float32)
+    mlp_sum = lax.psum_scatter(
+        jnp.concatenate([grad_gate, grad_up, grad_down], axis=1).astype(jnp.bfloat16),
+        ("dp", "ctx"),
+        scatter_dimension=0,
+        tiled=True,
+    )
+    mlp_part = jnp.dot(hidden_act, w_down, preferred_element_type=jnp.float32).astype(jnp.bfloat16)
+    mlp_part, mlp_sum = lax.optimization_barrier((mlp_part, mlp_sum))
+    mlp_natural = jnp.concatenate(
+        [
+            lax.dynamic_slice_in_dim(
+                mlp_part,
+                picked(
+                    me,
+                    {s: jnp.int32(s * share_rows) for s in range(count)},
+                    {i: slot_of[i][c] for i in range(count)},
+                ),
+                share_rows,
+                0,
+            )
+            for c in range(count)
+        ],
+        axis=0,
+    )
+    mlp_share = lax.psum_scatter(
+        mlp_natural, "tensor", scatter_dimension=0, tiled=True
+    ).astype(jnp.float32)
     result_share = (hidden_share + branch_scale * mlp_share).astype(jnp.bfloat16)
     result = lax.all_gather(result_share, "tensor", axis=0, tiled=True)
     prompt_out = result[:own_rows][None]
     cont_out = result[own_rows:].reshape(1, cont_count, CONT_LENGTH, width)
-    upstream = jnp.concatenate(
-        [prompt_cot[0], cont_cot[0].reshape(cont_rows, width)], axis=0
-    ).astype(jnp.float32)
-    grad_mlp = (branch_scale * upstream).astype(jnp.bfloat16)
-    grad_down = jnp.einsum("rf,rd->df", hidden_act, grad_mlp, preferred_element_type=jnp.float32)
-    grad_hidden = jnp.einsum("rd,fd->rf", grad_mlp, w_down, preferred_element_type=jnp.float32)
-    grad_gate_act = (
-        grad_hidden * up_proj * sigmoid_gate * (1.0 + gate_proj * (1.0 - sigmoid_gate))
-    ).astype(jnp.bfloat16)
-    grad_up_act = (grad_hidden * silu_gate).astype(jnp.bfloat16)
-    grad_gate = jnp.einsum("rd,rf->df", act_b, grad_gate_act, preferred_element_type=jnp.float32)
-    grad_up = jnp.einsum("rd,rf->df", act_b, grad_up_act, preferred_element_type=jnp.float32)
-    normed_grad = jnp.einsum(
-        "rf,df->rd", grad_gate_act, w_gate, preferred_element_type=jnp.float32
-    ) + jnp.einsum("rf,df->rd", grad_up_act, w_up, preferred_element_type=jnp.float32)
-    normed_share = sum_share(normed_grad)
-    through_mlp, gain_mlp_part = norm_back(hidden_share, gain_mlp, normed_share)
-    res_share = share_of(upstream) + through_mlp
-    grad_attn = lax.all_gather(
-        (branch_scale * res_share).astype(jnp.bfloat16), "tensor", axis=0, tiled=True
-    )
-    grad_out = jnp.einsum("rq,rd->dq", mixed_heads, grad_attn, preferred_element_type=jnp.float32)
-    grad_mixed = jnp.einsum(
-        "rd,qd->rq", grad_attn, w_out, preferred_element_type=jnp.float32
-    ).astype(jnp.bfloat16)
+    grad_attn = jnp.concatenate(slots_from(grad_attn_share), axis=0)
+    grad_out = jnp.einsum(
+        "rq,rd->dq", slot_order(mixed_heads), grad_attn, preferred_element_type=jnp.float32
+    )
     query_grads = []
     block_index = 0
     low_row = block_index * block_rows
@@ -295,23 +456,31 @@
         + jnp.einsum("rq,dq->rd", grad_key_lin, key_weight, preferred_element_type=jnp.float32)
         + jnp.einsum("rq,dq->rd", grad_value_lin, value_weight, preferred_element_type=jnp.float32)
     )
-    input_grad_share = sum_share(input_grad)
+    input_part = input_grad.astype(jnp.bfloat16)
+
+    def row_part(distance):
+        place = jnp.clip(me + distance, 0, count - 1) * share_rows
+        return lax.dynamic_slice_in_dim(input_part, place, share_rows, 0)
+
+    input_grad_share = line_sum(row_part, count)
     through_attn, gain_attn_part = norm_back(input_share, gain_attn, input_grad_share)
-    grad_input = lax.all_gather(
-        (res_share + through_attn).astype(jnp.bfloat16), "tensor", axis=0, tiled=True
-    )
+    arrived = line_hops((res_share + through_attn).astype(jnp.bfloat16), count)
+    grad_chunks = [
+        picked(me, arrived, {i: c - i for i in range(count)}) for c in range(count)
+    ]
+    grad_input = jnp.concatenate(grad_chunks, axis=0)
     prompt_grad = grad_input[:own_rows][None]
     cont_grad = grad_input[own_rows:].reshape(1, cont_count, CONT_LENGTH, width)
-    gain_parts = lax.psum(jnp.stack([gain_attn_part, gain_mlp_part]), ("dp", "ctx", "tensor"))
-    gain_rows = width // (lax.axis_size("dp") * lax.axis_size("ctx"))
-    gain_start = (lax.axis_index("dp") * lax.axis_size("ctx") + ctx_index) * gain_rows
-    gain_own = lax.dynamic_slice_in_dim(gain_parts, gain_start, gain_rows, 1)
-    mlp_sum = lax.psum_scatter(
-        jnp.concatenate([grad_gate, grad_up, grad_down], axis=1).astype(jnp.bfloat16),
-        ("dp", "ctx"),
-        scatter_dimension=0,
-        tiled=True,
-    ).astype(jnp.float32)
+    gain_own = lax.psum(
+        lax.psum_scatter(
+            jnp.stack([gain_attn_part, gain_mlp_part]),
+            ("dp", "ctx"),
+            scatter_dimension=1,
+            tiled=True,
+        ),
+        "tensor",
+    )
+    mlp_sum = mlp_sum.astype(jnp.float32)
     attn_sum = lax.psum_scatter(
         jnp.concatenate([grad_query, grad_key, grad_value, grad_out], axis=1).astype(jnp.bfloat16),
         ("dp", "ctx"),

time: 1200 us -> 1170 us (0.975)
  waiting for transfers between devices: 683 us -> 529 us
  starting transfers between devices: 0.62 us -> 77.1 us
  matrix products: 278 us -> 314 us
  blocking collectives: 49 us -> 32.5 us
  local copies, waits for them, and re-layouts: 42.1 us -> 58.3 us
    ppermute x0 -> x30, waiting for transfers between devices: none -> 309 us  [the longest x6 153 us: line_sum(): lax.ppermute(to_right, 'tensor', [(i, i + 1) for i in range(0, count - di...]
    reduce_scatter x4 -> x1, waiting for transfers between devices: 261 us -> 0.01 us  [shards(): lax.psum_scatter(mlp_natural, 'tensor', scatter_dimension=0, tiled=True)]
    all_gather x3 -> x2, waiting for transfers between devices: 191 us -> 47.1 us  [the longest x1 47.1 us: shards(): half_out = lax.all_gather(own_out_half, 'tensor', axis=0, tiled=True)]
    all_gather x1, waiting for transfers between devices: 76.5 us -> 0.01 us  [shards(): result = lax.all_gather(result_share, 'tensor', axis=0, tiled=True)]
    ppermute x0 -> x30, starting transfers between devices: none -> 60.8 us  [the longest x6 26.5 us: line_sum(): lax.ppermute(to_right, 'tensor', [(i, i + 1) for i in range(0, count - di...]
    dot_general x7 -> x19, matrix products: 68.6 us -> 109 us  [the longest x4 32 us: shards(): jnp.dot(act_b_slots[s], w_gate, preferred_element_type=jnp.float32)]
    psum x1, blocking collectives: 46.7 us -> 12.3 us  [shards(): lax.psum(lax.psum_scatter(jnp.stack([gain_attn_part, gain_mlp_part]), ('d...]
    all_to_all x0 -> x3, waiting for transfers between devices: none -> 32.3 us  [the longest x2 25.9 us: shards(): lax.all_to_all(mixed_grad[:, h * count * head_half:(h + 1) * count * head...]
  transfers between devices with their start and end apart: 11 -> 41, of which waited for: 9 -> 21; matrix products, arithmetic and copies ran while one was open for 12% -> 23% of each run, Pallas kernels for 0% -> 0%
where the time goes in v2:
time: 1170 us
  waiting for transfers between devices  529 us (45%)
  matrix products  314 us (27%)
  other arithmetic  137 us (12%)
  starting transfers between devices  77.1 us (7%)
  local copies, waits for them, and re-layouts  58.3 us (5%)
  blocking collectives  32.5 us (3%)
  between operations  17.6 us (2%)
    ppermute x6, waiting for transfers between devices, line_sum(): lax.ppermute(to_right, 'tensor', [(i, i + 1) for i in range(0, count - di...  153 us
    reduce_scatter x1, waiting for transfers between devices, shards(): lax.psum_scatter(jnp.concatenate([grad_gate, grad_up, grad_down], axis=1)...  136 us
    ppermute x9, waiting for transfers between devices, line_hops(): lax.ppermute(backward, 'tensor', [(i, i - 1) for i in range(1, count - st...  76.2 us
    ppermute x9, waiting for transfers between devices, line_hops(): lax.ppermute(forward, 'tensor', [(i, i + 1) for i in range(step - 1, coun...  49.1 us
    all_gather x1, waiting for transfers between devices, shards(): half_out = lax.all_gather(own_out_half, 'tensor', axis=0, tiled=True)  47.1 us
    dot_general x4, matrix products, shards(): jnp.dot(act_b_slots[s], w_gate, preferred_element_type=jnp.float32)  32 us
    ppermute x6, waiting for transfers between devices, line_sum(): lax.ppermute(to_left, 'tensor', [(i, i - 1) for i in range(distance, coun...  30.1 us
    convert_element_type x2, other arithmetic, attend_backward(): grad_scores = (weights * (grad_weights - jnp.sum(grad_weights * weights,...  29.5 us
  transfers between devices with their start and end apart: 41, of which 21 were waited for; matrix products, arithmetic and copies ran while one was open for 23% of the time, Pallas kernels for 0%

profile of v2, /device:TPU:0, one launch (start us, length us, event | category | flops | bytes accessed | tf_op | source)
XLA Modules:
  0.0 1165.3 jit_solution(3056979443910753377)
XLA Ops:
  46.6 47.1 %all-gather.4.cloned.1.call-done = bf16[1024,2048]{1,0:T(8,128)(2,1)} async-done(((bf16[256,2048]{1,0:T(8,128)(2,1)}), bf16[1024,2048]{1,0:T(8,128)(2,1)}) %all-gather.4.cloned.1.call-update) | async-done | bytes 4194320 | tf_op jit(solution)/shard_map/all_gather | solution.py:244
  102.9 13.5 %convolution_convert_fusion.8 = bf16[2,64,4,512]{3,1,2,0:T(8,128)(2,1)} fusion(bf16[1024,2,64,1]{0,2,3,1:T(8,128)(2,1)} %bitcast.286, f32[2,1024,512,4]{2,1,3,0:T(8,128)} %get-tuple-element.158, f32[2,4,512]{2,1,0:T(4,128)S(1)} %bitcast.299, pred[512,1024]{0,1:T(8,128)(4,1)S(1)} %fusion.53), kind=kOutput, calls=%fused_computation.146 | convolution fusion | flops 553910272 | bytes 18104320 | tf_op jit(solution)/shard_map/hgbk,khd->bhgd/dot_general | solution.py:84
  124.8 11.7 %fusion.108 = (f32[2,4,512]{2,1,0:T(4,128)S(1)}, f32[2,4,512,1536]{2,3,1,0:T(8,128)}) fusion(bf16[1536,2,64,1]{0,2,3,1:T(8,128)(2,1)} %bitcast.282, bf16[512,2,4,64]{0,3,2,1:T(8,128)(2,1)S(1)} %bitcast.254, pred[512,1536]{0,1:T(8,128)(4,1)S(1)} %pad_add_fusion), kind=kOutput, calls=%fused_computation.274 | convolution fusion | flops 824176640 | bytes 26886144 | tf_op jit(solution)/shard_map/bhgd,khd->hgbk/dot_general | solution.py:68
  146.6 11.1 fusion.54
  159.9 18.0 %all_to_all.76 = bf16[4,256,256]{2,1,0:T(8,128)(2,1)} all-to-all(bf16[4,256,256]{2,1,0:T(8,128)(2,1)S(1)} %bitcast.280), channel_id=1, replica_groups=mesh['dp'=4,'ctx'=2,'tensor'=4] {'tensor'}, dimensions={0} | all-to-all | bytes 1048576 | tf_op jit(solution)/shard_map/all_to_all | solution.py:301
  212.3 16.5 %collective-permute-done = bf16[256,2048]{1,0:T(8,128)(2,1)} collective-permute-done((bf16[256,2048]{1,0:T(8,128)(2,1)S(1)}, bf16[256,2048]{1,0:T(8,128)(2,1)}, u32[]{:S(2)}, u32[]{:S(2)}) %collective-permute-start) | collective-permute-done | bytes 1048608 | tf_op jit(solution)/shard_map/ppermute | solution.py:157
  235.2 13.2 %fusion.73 = f32[1024,2048]{1,0:T(8,128)} fusion(bf16[2048,2048]{1,0:T(8,128)(2,1)} %param.25, bf16[256,2048]{1,0:T(8,128)(2,1)S(1)} %get-tuple-element.104, bf16[256,2048]{1,0:T(8,128)(2,1)S(1)} %get-tuple-element.105, bf16[256,2048]{1,0:T(8,128)(2,1)S(1)} %get-tuple-element.106, bf16[256,2048]{1,0:T(8,128)(2,1)S(1)} %get-tuple-element.103), kind=kOutput, calls=%fused_computation.188 | convolution fusion | flops 8606711808 | bytes 20971520 | tf_op jit(solution)/shard_map/rd,fd->rf/dot_general | solution.py:317
  304.4 17.5 %multiply_convert_fusion.10 = (bf16[256,2048]{1,0:T(8,128)(2,1)}, bf16[256,2048]{1,0:T(8,128)(2,1)}, bf16[256,2048]{1,0:T(8,128)(2,1)}, bf16[256,2048]{1,0:T(8,1...) fusion(f32[256,2048]{1,0:T(8,128)} %fusion.111, ...), kind=kOutput, calls=%fused_computation.114 | convolution fusion | flops 2178940928 | bytes 45088768 | tf_op jit(solution)/shard_map/dot_general | solution.py:321
  321.9 12.9 %convolution_convert_fusion = bf16[2048,2048]{0,1:T(8,128)(2,1)} fusion(bf16[256,2048]{1,0:T(8,128)(2,1)S(1)} %get-tuple-element.104, bf16[256,2048]{1,0:T(8,128)(2,1)S(1)} %get-tuple-element.105, bf16[256,2048]{1,0:T(8,128)(2,1)S(1)} %get-tuple-element.106, bf16[256,2048]{1,0:T(8,128)(2,1)S(1)} %get-tuple-element.103, ...), kind=kOutput, calls=%fused_computation.24 | convolution fusion | flops 8627683328 | bytes 16777216 | tf_op jit(solution)/shard_map/rf,rd->df/dot_general | solution.py:375
  334.8 14.3 %convolution_convert_fusion.1 = bf16[2048,2048]{0,1:T(8,128)(2,1)} fusion(bf16[256,2048]{1,0:T(8,128)(2,1)} %get-tuple-element.83, bf16[256,2048]{1,0:T(8,128)(2,1)} %get-tuple-element.85, bf16[256,2048]{1,0:T(8,128)(2,1)} %get-tuple-element.87, bf16[256,2048]{1,0:T(8,128)(2,1)} %get-tuple-element.76, bf16[256,2048]{1,0:T(8,128)(2,1)} %copy-done.50, ...), kind=kOutput, calls=%fused_computation.25 | convolution fusion | flops 8627683328 | bytes 16777216 | tf_op jit(solution)/shard_map/rd,rf->df/dot_general | solution.py:377
  349.1 12.8 %convolution_convert_fusion.2 = bf16[2048,2048]{0,1:T(8,128)(2,1)} fusion(bf16[256,2048]{1,0:T(8,128)(2,1)} %get-tuple-element.84, bf16[256,2048]{1,0:T(8,128)(2,1)} %get-tuple-element.86, bf16[256,2048]{1,0:T(8,128)(2,1)} %get-tuple-element.88, bf16[256,2048]{1,0:T(8,128)(2,1)S(1)} %copy-done.74, bf16[256,2048]{1,0:T(8,128)(2,1)S(1)} %copy-done.51, ...), kind=kOutput, calls=%fused_computation.26 | convolution fusion | flops 8627683328 | bytes 16777216 | tf_op jit(solution)/shard_map/rd,rf->df/dot_general | solution.py:376
  361.9 18.0 %pad_maximum_fusion = bf16[2048,6144]{0,1:T(8,128)(2,1)} fusion(bf16[2048,2048]{0,1:T(8,128)(2,1)} %convolution_convert_fusion, bf16[2048,2048]{0,1:T(8,128)(2,1)} %convolution_convert_fusion.1, bf16[2048,2048]{0,1:T(8,128)(2,1)} %convolution_convert_fusion.2), kind=kLoop, calls=%fused_computation | loop fusion | flops 75497472 | bytes 50331648 | tf_op jit(solution)/shard_map/concatenate | solution.py:379
  381.1 16.7 %convolution_convert_fusion.3 = bf16[1024,2048]{1,0:T(8,128)(2,1)} fusion(bf16[2048,2048]{1,0:T(8,128)(2,1)} %param.25, bf16[256,2048]{1,0:T(8,128)(2,1)} %get-tuple-element.91, bf16[256,2048]{1,0:T(8,128)(2,1)} %get-tuple-element.90, bf16[256,2048]{1,0:T(8,128)(2,1)S(1)} %copy-done.78, bf16[256,2048]{1,0:T(8,128)(2,1)} %get-tuple-element.102), kind=kOutput, calls=%fused_computation.58 | convolution fusion | flops 8608808960 | bytes 16777216 | tf_op jit(solution)/shard_map/dot_general | solution.py:384
  397.8 136.4 %reduce-scatter.8.cloned.1.call-done = bf16[256,6144]{0,1:T(8,128)(2,1)} async-done(((bf16[2048,6144]{0,1:T(8,128)(2,1)}), bf16[256,6144]{0,1:T(8,128)(2,1)}) %reduce-scatter.8.cloned.1.call-update) | async-done | bytes 3145744 | tf_op jit(solution)/shard_map/reduce_scatter | solution.py:378
  559.2 42.3 %collective-permute-done.6 = bf16[256,2048]{1,0:T(8,128)(2,1)S(1)} collective-permute-done((bf16[256,2048]{1,0:T(8,128)(2,1)S(1)}, bf16[256,2048]{1,0:T(8,128)(2,1)S(1)}, u32[]{:S(2)}, u32[]{:S(2)}) %collective-permute-start.6) | collective-permute-done | bytes 1048608 | tf_op jit(solution)/shard_map/ppermute | solution.py:176
  623.0 34.8 %collective-permute-done.7 = bf16[256,2048]{1,0:T(8,128)(2,1)S(1)} collective-permute-done((bf16[256,2048]{1,0:T(8,128)(2,1)S(1)}, bf16[256,2048]{1,0:T(8,128)(2,1)S(1)}, u32[]{:S(2)}, u32[]{:S(2)}) %collective-permute-start.7) | collective-permute-done | bytes 1048608 | tf_op jit(solution)/shard_map/ppermute | solution.py:176
  667.9 17.0 %collective-permute-done.11 = bf16[256,2048]{1,0:T(8,128)(2,1)S(1)} collective-permute-done((bf16[256,2048]{1,0:T(8,128)(2,1)S(1)}, bf16[256,2048]{1,0:T(8,128)(2,1)S(1)}, u32[]{:S(2)}, u32[]{:S(2)}) %collective-permute-start.11) | collective-permute-done | bytes 1048608 | tf_op jit(solution)/shard_map/ppermute | solution.py:179
  717.7 12.3 %all-to-all-done.2 = bf16[256,4,256]{2,0,1:T(8,128)(2,1)S(1)} async-done(((bf16[256,4,256]{2,0,1:T(8,128)(2,1)}), bf16[256,4,256]{2,0,1:T(8,128)(2,1)S(1)}, u32[]{:S(2)}, u32[]{:S(2)}) %all-to-all-start.2) | async-done | bytes 524320 | tf_op jit(solution)/shard_map/all_to_all | solution.py:360
  733.6 13.6 %all-to-all-done.3 = bf16[256,4,256]{2,0,1:T(8,128)(2,1)S(1)} async-done(((bf16[256,4,256]{2,0,1:T(8,128)(2,1)}), bf16[256,4,256]{2,0,1:T(8,128)(2,1)S(1)}, u32[]{:S(2)}, u32[]{:S(2)}) %all-to-all-start.3) | async-done | bytes 524320 | tf_op jit(solution)/shard_map/all_to_all | solution.py:360
  749.5 16.9 %fusion = (f32[2,4,512]{2,1,0:T(4,128)}, f32[2,1536,512,4]{2,1,3,0:T(8,128)}) fusion(f32[2,4,512,1536]{2,3,1,0:T(8,128)} %get-tuple-element.160, f32[2,4,512]{2,1,0:T(4,128)S(1)} %bitcast.296, bf16[1536,2,64,1]{0,2,3,1:T(8,128)(2,1)S(1)} %bitcast.260, bf16[512,2,4,64]{0,3,2,1:T(8,128)(2,1)S(1)} %bitcast.250), kind=kOutput, calls=%fused_computation.3 | convolution fusion | flops 824176640 | bytes 51281920 | tf_op jit(solution)/shard_map/bhgd,khd->hgbk/dot_general | solution.py:95
  766.4 11.2 fusion.44
  778.9 11.8 %fusion.4 = (f32[2,4,512]{2,1,0:T(4,128)S(1)}, f32[2,1024,512,4]{2,1,3,0:T(8,128)}) fusion(f32[2,1024,512,4]{2,1,3,0:T(8,128)} %get-tuple-element.158, f32[2,4,512]{2,1,0:T(4,128)S(1)} %bitcast.300, pred[512,1024]{0,1:T(8,128)(4,1)S(1)} %copy-done.8, bf16[1024,2,64,1]{0,2,3,1:T(8,128)(2,1)S(1)} %bitcast.287, bf16[512,2,4,64]{0,3,2,1:T(8,128)(2,1)S(1)} %bitcast.265), kind=kOutput, calls=%fused_computation.12 | convolution fusion | flops 557838336 | bytes 34897920 | tf_op jit(solution)/shard_map/bhgd,khd->hgbk/dot_general | solution.py:95
  799.6 16.9 %fusion.2 = bf16[2,4,512,1536]{2,3,1,0:T(8,128)(2,1)S(1)} fusion(f32[2,1536,512,4]{2,1,3,0:T(8,128)} %get-tuple-element.166, f32[2,4,512,1536]{2,3,1,0:T(8,128)} %get-tuple-element.160, f32[2,4,512]{2,1,0:T(4,128)S(1)} %copy-done.66, f32[2,4,512]{2,1,0:T(4,128)S(1)} %bitcast.298), kind=kLoop, calls=%fused_computation.5 | loop fusion | flops 25165824 | bytes 62947328 | tf_op jit(solution)/shard_map/convert_element_type | solution.py:100
  821.9 12.6 %fusion.6 = bf16[2,4,512,1024]{2,3,1,0:T(8,128)(2,1)S(1)} fusion(f32[2,1024,512,4]{2,1,3,0:T(8,128)} %get-tuple-element.168, f32[2,1024,512,4]{2,1,3,0:T(8,128)} %get-tuple-element.158, f32[2,4,512]{2,1,0:T(4,128)S(1)} %get-tuple-element.167, f32[2,4,512]{2,1,0:T(4,128)S(1)} %bitcast.302, pred[512,1024]{0,1:T(8,128)(4,1)S(1)} %copy-done.8), kind=kLoop, calls=%fused_computation.14 | loop fusion | flops 25165824 | bytes 42500096 | tf_op jit(solution)/shard_map/convert_element_type | solution.py:100
  875.3 33.3 %collective-permute-done.12 = bf16[256,2048]{1,0:T(8,128)(2,1)} collective-permute-done((bf16[256,2048]{1,0:T(8,128)(2,1)}, bf16[256,2048]{1,0:T(8,128)(2,1)}, u32[]{:S(2)}, u32[]{:S(2)}) %collective-permute-start.12) | collective-permute-done | bytes 1048608 | tf_op jit(solution)/shard_map/ppermute | solution.py:176
  921.0 32.6 %collective-permute-done.24 = bf16[256,2048]{1,0:T(8,128)(2,1)} collective-permute-done((bf16[256,2048]{1,0:T(8,128)(2,1)}, bf16[256,2048]{1,0:T(8,128)(2,1)}, u32[]{:S(2)}, u32[]{:S(2)}) %collective-permute-start.24) | collective-permute-done | bytes 1048608 | tf_op jit(solution)/shard_map/ppermute | solution.py:157
  955.6 41.4 %collective-permute-done.13 = bf16[256,2048]{1,0:T(8,128)(2,1)} collective-permute-done((bf16[256,2048]{1,0:T(8,128)(2,1)}, bf16[256,2048]{1,0:T(8,128)(2,1)}, u32[]{:S(2)}, u32[]{:S(2)}) %collective-permute-start.13) | collective-permute-done | bytes 1048608 | tf_op jit(solution)/shard_map/ppermute | solution.py:176
  1014.4 18.5 %collective-permute-done.29 = bf16[256,2048]{1,0:T(8,128)(2,1)S(1)} collective-permute-done((bf16[256,2048]{1,0:T(8,128)(2,1)S(1)}, bf16[256,2048]{1,0:T(8,128)(2,1)S(1)}, u32[]{:S(2)}, u32[]{:S(2)}) %collective-permute-start.29) | collective-permute-done | bytes 1048608 | tf_op jit(solution)/shard_map/ppermute | solution.py:158
  1038.5 13.1 %collective-permute-done.17 = bf16[256,2048]{1,0:T(8,128)(2,1)S(1)} collective-permute-done((bf16[256,2048]{1,0:T(8,128)(2,1)S(1)}, bf16[256,2048]{1,0:T(8,128)(2,1)S(1)}, u32[]{:S(2)}, u32[]{:S(2)}) %collective-permute-start.17) | collective-permute-done | bytes 1048608 | tf_op jit(solution)/shard_map/ppermute | solution.py:179
  1071.8 17.4 %collective-permute-done.21 = bf16[256,2048]{1,0:T(8,128)(2,1)S(1)} collective-permute-done((bf16[256,2048]{1,0:T(8,128)(2,1)S(1)}, bf16[256,2048]{1,0:T(8,128)(2,1)S(1)}, u32[]{:S(2)}, u32[]{:S(2)}) %collective-permute-start.21) | collective-permute-done | bytes 1048608 | tf_op jit(solution)/shard_map/ppermute | solution.py:158
  1095.0 17.3 %collective-permute-done.22 = bf16[256,2048]{1,0:T(8,128)(2,1)} collective-permute-done((bf16[256,2048]{1,0:T(8,128)(2,1)S(1)}, bf16[256,2048]{1,0:T(8,128)(2,1)}, u32[]{:S(2)}, u32[]{:S(2)}) %collective-permute-start.22) | collective-permute-done | bytes 1048608 | tf_op jit(solution)/shard_map/ppermute | solution.py:158
  1128.4 12.3 %psum.7 = f32[2,256]{1,0:T(2,128)S(1)} all-reduce(f32[2,256]{1,0:T(2,128)S(1)} %copy.144), channel_id=1, replica_groups=mesh['dp'=4,'ctx'=2,'tensor'=4] {'tensor'}, use_global_device_ids=true, to_apply=%region_17.18 | all-reduce | flops 512 | bytes 4096 | tf_op jit(solution)/shard_map/psum | solution.py:474
  (386 shorter events, 412.9 us)
Async XLA Ops:
  7.2 86.4 %all-gather.4.cloned.1.call-start = ((), (), s32[]{:S(2)}) async-start(), calls=%async_computation.9 | async-start | bytes 5242880 | tf_op jit(solution)/shard_map/all_gather | solution.py:244
  9.7 187.7 %all-gather.6.cloned.1.call-start = ((), (), s32[]{:S(2)}) async-start(), calls=%async_computation.10 | async-start | bytes 12582912 | tf_op jit(solution)/shard_map/all_gather | solution.py:245
  182.0 352.2 %reduce-scatter.8.cloned.1.call-start = ((), (), s32[]{:S(2)}) async-start(), calls=%async_computation.11 | async-start | bytes 28311552 | tf_op jit(solution)/shard_map/reduce_scatter | solution.py:378
  207.8 26.2 %collective-permute-start.1 = (bf16[256,2048]{1,0:T(8,128)(2,1)S(1)}, bf16[256,2048]{1,0:T(8,128)(2,1)}, u32[]{:S(2)}, u32[]{:S(2)}) collective-permute-start(bf16[256,2048]{1,0:T(8,128)(2,1)S(1)} %multiply_convert_fusion.15), channel_id=1, source_target_pairs={{1,0},{2,1},{3,2},{5,4},{6,5},{7,6},{9,8},{10,9},{11,10},{13,12},{... | collective-permute-start | bytes 3145736 | tf_op jit(solution)/shard_map/ppermute | solution.py:158
  233.9 25.4 %collective-permute-start.3 = (bf16[256,2048]{1,0:T(8,128)(2,1)}, bf16[256,2048]{1,0:T(8,128)(2,1)S(1)}, u32[]{:S(2)}, u32[]{:S(2)}) collective-permute-start(bf16[256,2048]{1,0:T(8,128)(2,1)} %collective-permute-done.1), channel_id=1, source_target_pairs={{1,0},{2,1},{5,4},{6,5},{9,8},{10,9},{13,12},{14,13},{17,16},{18,1... | collective-permute-start | bytes 3145736 | tf_op jit(solution)/shard_map/ppermute | solution.py:158
  248.5 27.0 %collective-permute-start.4 = (bf16[256,2048]{1,0:T(8,128)(2,1)S(1)}, bf16[256,2048]{1,0:T(8,128)(2,1)S(1)}, u32[]{:S(2)}, u32[]{:S(2)}) collective-permute-start(bf16[256,2048]{1,0:T(8,128)(2,1)S(1)} %collective-permute-done.2), channel_id=1, source_target_pairs={{2,3},{6,7},{10,11},{14,15},{18,19},{22,23},{26,27},{30,31}} | collective-permute-start | bytes 3145736 | tf_op jit(solution)/shard_map/ppermute | solution.py:157
  259.4 24.3 %collective-permute-start.5 = (bf16[256,2048]{1,0:T(8,128)(2,1)S(1)}, bf16[256,2048]{1,0:T(8,128)(2,1)S(1)}, u32[]{:S(2)}, u32[]{:S(2)}) collective-permute-start(bf16[256,2048]{1,0:T(8,128)(2,1)S(1)} %collective-permute-done.3), channel_id=1, source_target_pairs={{1,0},{5,4},{9,8},{13,12},{17,16},{21,20},{25,24},{29,28}} | collective-permute-start | bytes 3145736 | tf_op jit(solution)/shard_map/ppermute | solution.py:158
  379.9 315.3 %reduce-scatter.10.cloned.1.call-start = ((), (), s32[]{:S(2)}) async-start(), calls=%async_computation.12 | async-start | bytes 5242880 | tf_op jit(solution)/shard_map/reduce_scatter | solution.py:402
  552.4 49.1 %collective-permute-start.6 = (bf16[256,2048]{1,0:T(8,128)(2,1)S(1)}, bf16[256,2048]{1,0:T(8,128)(2,1)S(1)}, u32[]{:S(2)}, u32[]{:S(2)}) collective-permute-start(bf16[256,2048]{1,0:T(8,128)(2,1)S(1)} %fusion.43), channel_id=1, source_target_pairs={{0,1},{4,5},{8,9},{12,13},{16,17},{20,21},{24,25},{28,29}} | collective-permute-start | bytes 3145736 | tf_op jit(solution)/shard_map/ppermute | solution.py:176
  555.9 45.6 %collective-permute-start.9 = (bf16[256,2048]{1,0:T(8,128)(2,1)S(1)}, bf16[256,2048]{1,0:T(8,128)(2,1)S(1)}, u32[]{:S(2)}, u32[]{:S(2)}) collective-permute-start(bf16[256,2048]{1,0:T(8,128)(2,1)S(1)} %fusion.43), channel_id=1, source_target_pairs={{3,2},{7,6},{11,10},{15,14},{19,18},{23,22},{27,26},{31,30}} | collective-permute-start | bytes 3145736 | tf_op jit(solution)/shard_map/ppermute | solution.py:179
  608.3 49.5 %collective-permute-start.7 = (bf16[256,2048]{1,0:T(8,128)(2,1)S(1)}, bf16[256,2048]{1,0:T(8,128)(2,1)S(1)}, u32[]{:S(2)}, u32[]{:S(2)}) collective-permute-start(bf16[256,2048]{1,0:T(8,128)(2,1)S(1)} %get-tuple-element.120), channel_id=1, source_target_pairs={{0,1},{1,2},{4,5},{5,6},{8,9},{9,10},{12,13},{13,14},{16,17},{17,1... | collective-permute-start | bytes 3145736 | tf_op jit(solution)/shard_map/ppermute | solution.py:176
  612.7 45.1 %collective-permute-start.10 = (bf16[256,2048]{1,0:T(8,128)(2,1)S(1)}, bf16[256,2048]{1,0:T(8,128)(2,1)S(1)}, u32[]{:S(2)}, u32[]{:S(2)}) collective-permute-start(bf16[256,2048]{1,0:T(8,128)(2,1)S(1)} %get-tuple-element.121), channel_id=1, source_target_pairs={{2,1},{3,2},{6,5},{7,6},{10,9},{11,10},{14,13},{15,14},{18,17},{19... | collective-permute-start | bytes 3145736 | tf_op jit(solution)/shard_map/ppermute | solution.py:179
  658.6 26.3 %collective-permute-start.11 = (bf16[256,2048]{1,0:T(8,128)(2,1)S(1)}, bf16[256,2048]{1,0:T(8,128)(2,1)S(1)}, u32[]{:S(2)}, u32[]{:S(2)}) collective-permute-start(bf16[256,2048]{1,0:T(8,128)(2,1)S(1)} %get-tuple-element.134), channel_id=1, source_target_pairs={{1,0},{2,1},{3,2},{5,4},{6,5},{7,6},{9,8},{10,9},{11,10},{13,12},{... | collective-permute-start | bytes 3145736 | tf_op jit(solution)/shard_map/ppermute | solution.py:179
  660.0 26.5 %collective-permute-start.8 = (bf16[256,2048]{1,0:T(8,128)(2,1)S(1)}, bf16[256,2048]{1,0:T(8,128)(2,1)S(1)}, u32[]{:S(2)}, u32[]{:S(2)}) collective-permute-start(bf16[256,2048]{1,0:T(8,128)(2,1)S(1)} %get-tuple-element.133), channel_id=1, source_target_pairs={{0,1},{1,2},{2,3},{4,5},{5,6},{6,7},{8,9},{9,10},{10,11},{12,13},{... | collective-permute-start | bytes 3145736 | tf_op jit(solution)/shard_map/ppermute | solution.py:176
  733.5 124.7 %reduce-scatter.12.cloned.1.call-start = ((), (), s32[]{:S(2)}) async-start(), calls=%async_computation.14 | async-start | bytes 1572864 | tf_op jit(solution)/shard_map/reduce_scatter | solution.py:435
  838.9 283.7 %all-gather.8.cloned.1.call-start = ((), (), s32[]{:S(2)}) async-start(), calls=%async_computation.13 | async-start | bytes 5242880 | tf_op jit(solution)/shard_map/all_gather | solution.py:406
  867.5 41.1 %collective-permute-start.12 = (bf16[256,2048]{1,0:T(8,128)(2,1)}, bf16[256,2048]{1,0:T(8,128)(2,1)}, u32[]{:S(2)}, u32[]{:S(2)}) collective-permute-start(bf16[256,2048]{1,0:T(8,128)(2,1)} %get-tuple-element.94), channel_id=1, source_target_pairs={{0,1},{4,5},{8,9},{12,13},{16,17},{20,21},{24,25},{28,29}} | collective-permute-start | bytes 3145736 | tf_op jit(solution)/shard_map/ppermute | solution.py:176
  870.0 257.4 %reduce-scatter.16.cloned.1.call-start = ((), (), s32[]{:S(2)}) async-start(), calls=%async_computation.16 | async-start | bytes 1179648
  870.0 83.5 %collective-permute-start.24 = (bf16[256,2048]{1,0:T(8,128)(2,1)}, bf16[256,2048]{1,0:T(8,128)(2,1)}, u32[]{:S(2)}, u32[]{:S(2)}) collective-permute-start(bf16[256,2048]{1,0:T(8,128)(2,1)} %copy-done.41), channel_id=1, source_target_pairs={{0,1},{1,2},{2,3},{4,5},{5,6},{6,7},{8,9},{9,10},{10,11},{12,13},{... | collective-permute-start | bytes 3145736 | tf_op jit(solution)/shard_map/ppermute | solution.py:157
  872.4 81.9 %collective-permute-start.25 = (bf16[256,2048]{1,0:T(8,128)(2,1)}, bf16[256,2048]{1,0:T(8,128)(2,1)}, u32[]{:S(2)}, u32[]{:S(2)}) collective-permute-start(bf16[256,2048]{1,0:T(8,128)(2,1)} %copy-done.41), channel_id=1, source_target_pairs={{1,0},{2,1},{3,2},{5,4},{6,5},{7,6},{9,8},{10,9},{11,10},{13,12},{... | collective-permute-start | bytes 3145736 | tf_op jit(solution)/shard_map/ppermute | solution.py:158
  873.7 82.0 %collective-permute-start.15 = (bf16[256,2048]{1,0:T(8,128)(2,1)}, bf16[256,2048]{1,0:T(8,128)(2,1)}, u32[]{:S(2)}, u32[]{:S(2)}) collective-permute-start(bf16[256,2048]{1,0:T(8,128)(2,1)} %get-tuple-element.95), channel_id=1, source_target_pairs={{3,2},{7,6},{11,10},{15,14},{19,18},{23,22},{27,26},{31,30}} | collective-permute-start | bytes 3145736 | tf_op jit(solution)/shard_map/ppermute | solution.py:179
  911.5 85.5 %collective-permute-start.13 = (bf16[256,2048]{1,0:T(8,128)(2,1)}, bf16[256,2048]{1,0:T(8,128)(2,1)}, u32[]{:S(2)}, u32[]{:S(2)}) collective-permute-start(bf16[256,2048]{1,0:T(8,128)(2,1)} %add_convert_fusion.5), channel_id=1, source_target_pairs={{0,1},{1,2},{4,5},{5,6},{8,9},{9,10},{12,13},{13,14},{16,17},{17,1... | collective-permute-start | bytes 3145736 | tf_op jit(solution)/shard_map/ppermute | solution.py:176
  953.6 50.3 %collective-permute-start.26 = (bf16[256,2048]{1,0:T(8,128)(2,1)}, bf16[256,2048]{1,0:T(8,128)(2,1)S(1)}, u32[]{:S(2)}, u32[]{:S(2)}) collective-permute-start(bf16[256,2048]{1,0:T(8,128)(2,1)} %collective-permute-done.24), channel_id=1, source_target_pairs={{1,2},{2,3},{5,6},{6,7},{9,10},{10,11},{13,14},{14,15},{17,18},{18... | collective-permute-start | bytes 3145736 | tf_op jit(solution)/shard_map/ppermute | solution.py:157
  954.3 50.3 %collective-permute-start.27 = (bf16[256,2048]{1,0:T(8,128)(2,1)}, bf16[256,2048]{1,0:T(8,128)(2,1)S(1)}, u32[]{:S(2)}, u32[]{:S(2)}) collective-permute-start(bf16[256,2048]{1,0:T(8,128)(2,1)} %collective-permute-done.25), channel_id=1, source_target_pairs={{1,0},{2,1},{5,4},{6,5},{9,8},{10,9},{13,12},{14,13},{17,16},{18,1... | collective-permute-start | bytes 3145736 | tf_op jit(solution)/shard_map/ppermute | solution.py:158
  1004.6 28.3 %collective-permute-start.29 = (bf16[256,2048]{1,0:T(8,128)(2,1)S(1)}, bf16[256,2048]{1,0:T(8,128)(2,1)S(1)}, u32[]{:S(2)}, u32[]{:S(2)}) collective-permute-start(bf16[256,2048]{1,0:T(8,128)(2,1)S(1)} %collective-permute-done.27), channel_id=1, source_target_pairs={{1,0},{5,4},{9,8},{13,12},{17,16},{21,20},{25,24},{29,28}} | collective-permute-start | bytes 3145736 | tf_op jit(solution)/shard_map/ppermute | solution.py:158
  1007.5 31.0 %collective-permute-start.14 = (bf16[256,2048]{1,0:T(8,128)(2,1)S(1)}, bf16[256,2048]{1,0:T(8,128)(2,1)S(1)}, u32[]{:S(2)}, u32[]{:S(2)}) collective-permute-start(bf16[256,2048]{1,0:T(8,128)(2,1)S(1)} %get-tuple-element.92), channel_id=1, source_target_pairs={{0,1},{1,2},{2,3},{4,5},{5,6},{6,7},{8,9},{9,10},{10,11},{12,13},{... | collective-permute-start | bytes 3145736 | tf_op jit(solution)/shard_map/ppermute | solution.py:176
  1013.0 38.6 %collective-permute-start.17 = (bf16[256,2048]{1,0:T(8,128)(2,1)S(1)}, bf16[256,2048]{1,0:T(8,128)(2,1)S(1)}, u32[]{:S(2)}, u32[]{:S(2)}) collective-permute-start(bf16[256,2048]{1,0:T(8,128)(2,1)S(1)} %add_convert_fusion.2), channel_id=1, source_target_pairs={{1,0},{2,1},{3,2},{5,4},{6,5},{7,6},{9,8},{10,9},{11,10},{13,12},{... | collective-permute-start | bytes 3145736 | tf_op jit(solution)/shard_map/ppermute | solution.py:179
  1056.0 95.7 %reduce-scatter.14.cloned.1.call-start = ((), (), s32[]{:S(2)}) async-start(), calls=%async_computation.15 | async-start | bytes 5898240 | tf_op jit(solution)/shard_map/reduce_scatter | solution.py:484
  1065.9 23.3 %collective-permute-start.21 = (bf16[256,2048]{1,0:T(8,128)(2,1)S(1)}, bf16[256,2048]{1,0:T(8,128)(2,1)S(1)}, u32[]{:S(2)}, u32[]{:S(2)}) collective-permute-start(bf16[256,2048]{1,0:T(8,128)(2,1)S(1)} %add_convert_fusion.1), channel_id=1, source_target_pairs={{1,0},{2,1},{3,2},{5,4},{6,5},{7,6},{9,8},{10,9},{11,10},{13,12},{... | collective-permute-start | bytes 3145736 | tf_op jit(solution)/shard_map/ppermute | solution.py:158
  1067.2 23.3 %collective-permute-start.18 = (bf16[256,2048]{1,0:T(8,128)(2,1)S(1)}, bf16[256,2048]{1,0:T(8,128)(2,1)S(1)}, u32[]{:S(2)}, u32[]{:S(2)}) collective-permute-start(bf16[256,2048]{1,0:T(8,128)(2,1)S(1)} %add_convert_fusion.1), channel_id=1, source_target_pairs={{0,1},{1,2},{2,3},{4,5},{5,6},{6,7},{8,9},{9,10},{10,11},{12,13},{... | collective-permute-start | bytes 3145736 | tf_op jit(solution)/shard_map/ppermute | solution.py:157
  1112.4 28.9 %collective-permute-start.23 = (bf16[256,2048]{1,0:T(8,128)(2,1)}, bf16[256,2048]{1,0:T(8,128)(2,1)}, u32[]{:S(2)}, u32[]{:S(2)}) collective-permute-start(bf16[256,2048]{1,0:T(8,128)(2,1)} %collective-permute-done.22), channel_id=1, source_target_pairs={{1,0},{5,4},{9,8},{13,12},{17,16},{21,20},{25,24},{29,28}} | collective-permute-start | bytes 3145736 | tf_op jit(solution)/shard_map/ppermute | solution.py:158
  1113.7 27.6 %collective-permute-start.20 = (bf16[256,2048]{1,0:T(8,128)(2,1)}, bf16[256,2048]{1,0:T(8,128)(2,1)}, u32[]{:S(2)}, u32[]{:S(2)}) collective-permute-start(bf16[256,2048]{1,0:T(8,128)(2,1)} %collective-permute-done.19), channel_id=1, source_target_pairs={{2,3},{6,7},{10,11},{14,15},{18,19},{22,23},{26,27},{30,31}} | collective-permute-start | bytes 3145736 | tf_op jit(solution)/shard_map/ppermute | solution.py:157
  (97 other events, 1653.2 us)
Sparse Core Ops, SparseCore 0:
  10.1 83.4 all-gather.3
  95.2 18.3 all-gather.5
  380.0 154.1 reduce-scatter.7
  539.5 119.5 reduce-scatter.9
  839.0 6.5 reduce-scatter.11
  870.1 133.5 all-gather.7
  1056.1 35.6 reduce-scatter.15
  1095.2 56.3 reduce-scatter.13

commit v3 on v2

--- a/solution.py
+++ b/solution.py
@@ -150,38 +150,49 @@
     return chunk_of
 
 
-def line_hops(share, count):
-    arrived = {0: share}
-    forward = backward = share
-    for step in range(1, count):
-        forward = lax.ppermute(forward, "tensor", [(i, i + 1) for i in range(step - 1, count - 1)])
-        backward = lax.ppermute(backward, "tensor", [(i, i - 1) for i in range(1, count - step + 1)])
-        arrived[-step] = forward
-        arrived[step] = backward
-    return arrived
-
-
-def line_sum(part_at, count):
-    from_left = from_right = None
-    for distance in range(count - 1, 0, -1):
-        to_right = part_at(distance)
-        to_left = part_at(-distance)
-        if from_left is not None:
-            to_right = (to_right.astype(jnp.float32) + from_left.astype(jnp.float32)).astype(
-                jnp.bfloat16
-            )
-            to_left = (to_left.astype(jnp.float32) + from_right.astype(jnp.float32)).astype(
-                jnp.bfloat16
-            )
-        from_left = lax.ppermute(
-            to_right, "tensor", [(i, i + 1) for i in range(0, count - distance)]
-        )
-        from_right = lax.ppermute(to_left, "tensor", [(i, i - 1) for i in range(distance, count)])
+def hop_step(forward, backward, step, count):
     return (
-        part_at(0).astype(jnp.float32)
-        + from_left.astype(jnp.float32)
-        + from_right.astype(jnp.float32)
-    )
+        lax.ppermute(forward, "tensor", [(i, i + 1) for i in range(step - 1, count - 1)]),
+        lax.ppermute(backward, "tensor", [(i, i - 1) for i in range(1, count - step + 1)]),
+    )
+
+
+def added(first, second):
+    return (first.astype(jnp.float32) + second.astype(jnp.float32)).astype(jnp.bfloat16)
+
+
+def sum_step(state, part_at, distance, count):
+    to_right = part_at(distance)
+    to_left = part_at(-distance)
+    if state is not None:
+        to_right = added(to_right, state[0])
+        to_left = added(to_left, state[1])
+    return (
+        lax.ppermute(to_right, "tensor", [(i, i + 1) for i in range(0, count - distance)]),
+        lax.ppermute(to_left, "tensor", [(i, i - 1) for i in range(distance, count)]),
+    )
+
+
+def sum_end(state, part_at):
+    return sum(part.astype(jnp.float32) for part in (part_at(0), *state))
+
+
+def tied(*values):
+    return lax.optimization_barrier(values)
+
+
+def exchanged(me, send_block, count):
+    received = {0: send_block(me)}
+    for shift in range(1, count):
+        received[shift] = lax.ppermute(
+            send_block(lax.rem(me + shift, count)),
+            "tensor",
+            [(i, (i + shift) % count) for i in range(count)],
+        )
+    return [
+        picked(me, received, {i: (i - source) % count for i in range(count)})
+        for source in range(count)
+    ]
 
 
 def shards(
@@ -212,6 +223,8 @@
     share_rows = total_rows // count
     share_start = me * share_rows
     head_half = w_out.shape[0] // 2
+    kv_heads = key_weight.shape[1] // HEAD_WIDTH
+    group_width = w_out.shape[0] // kv_heads
     order = slot_tables(count)
     slot_chunks = [
         picked(me, {i: jnp.int32(i) for i in range(count)}, {i: order[i][s] for i in range(count)})
@@ -234,15 +247,20 @@
             axis=0,
         )
 
-    def slots_from(share):
-        arrived = line_hops(share, count)
+    def slots_from(arrived):
         return [
             picked(me, arrived, {i: order[i][s] - i for i in range(count)}) for s in range(count)
         ]
 
+    def slot_part(parts):
+        return lambda distance: picked(
+            me,
+            parts,
+            {i: slot_of[i][i + distance] for i in range(count) if 0 <= i + distance < count},
+        )
+
     own_out_half = lax.dynamic_slice_in_dim(w_out, ctx_index * head_half, head_half, 0)
-    half_out = lax.all_gather(own_out_half, "tensor", axis=0, tiled=True)
-    full_out = lax.all_gather(half_out, "ctx", axis=0, tiled=True)
+    full_out = lax.all_gather(own_out_half, ("tensor", "ctx"), axis=0, tiled=True)
     all_rows = jnp.concatenate([prompt_in[0], cont_in[0].reshape(cont_rows, width)], axis=0).astype(
         jnp.float32
     )
@@ -285,37 +303,53 @@
     )
     cont_keys = jnp.concatenate([shared_prompt_keys, joined_keys[own_rows:]], axis=0)
     cont_values = jnp.concatenate([shared_prompt_values, joined_values[own_rows:]], axis=0)
-    block_index = 0
-    block_queries = query_rows[block_index * block_rows : (block_index + 1) * block_rows]
-    mixed_block, total_block = attend_forward(
-        block_queries, shared_prompt_keys, shared_prompt_values, block_masks[block_index]
-    )
-    mixed_list = [mixed_block]
-    total_list = [total_block]
-    mixed_cont, total_cont = attend_forward(
-        query_rows[own_rows:], cont_keys, cont_values, cont_mask
-    )
-    mixed_heads = jnp.concatenate(mixed_list + [mixed_cont], axis=0).astype(jnp.bfloat16)
+    prompt_mask = block_masks[0]
+
+    def head_inputs(head, prompt):
+        wide = slice(head * group_width, (head + 1) * group_width)
+        thin = slice(head * HEAD_WIDTH, (head + 1) * HEAD_WIDTH)
+        if prompt:
+            return (
+                query_rows[:own_rows, wide],
+                shared_prompt_keys[:, thin],
+                shared_prompt_values[:, thin],
+                prompt_mask,
+            )
+        return (query_rows[own_rows:, wide], cont_keys[:, thin], cont_values[:, thin], cont_mask)
+
+    mixed_list = []
+    totals = {}
+    share_list = []
+    for head in range(kv_heads):
+        mixed_prompt, totals[head, True] = attend_forward(*head_inputs(head, True))
+        mixed_cont, totals[head, False] = attend_forward(*head_inputs(head, False))
+        mixed = jnp.concatenate([mixed_prompt, mixed_cont], axis=0).astype(jnp.bfloat16)
+        mixed_list.append(mixed)
+        share_list.append(
+            exchanged(
+                me,
+                lambda target: lax.dynamic_slice_in_dim(mixed, target * share_rows, share_rows, 0),
+                count,
+            )
+        )
+    upstream = jnp.concatenate([prompt_cot[0], cont_cot[0].reshape(cont_rows, width)], axis=0)
+    grad_mlp = slot_order((branch_scale * upstream.astype(jnp.float32)).astype(jnp.bfloat16))
+    mixed_list[-1], grad_mlp = tied(mixed_list[-1], grad_mlp)
+    grad_hidden = jnp.einsum("rd,fd->rf", grad_mlp, w_down, preferred_element_type=jnp.float32)
+    share_list[-1], grad_hidden = tied(share_list[-1], grad_hidden)
+    mixed_heads = jnp.concatenate(mixed_list, axis=1)
     mixed_share = jnp.concatenate(
-        [
-            lax.all_to_all(
-                mixed_heads[:, h * head_half : (h + 1) * head_half],
-                "tensor",
-                split_axis=0,
-                concat_axis=1,
-                tiled=True,
-            )
-            for h in range(2)
-        ],
-        axis=1,
+        [share_list[head][source] for source in range(count) for head in range(kv_heads)], axis=1
     )
     attn_share = jnp.dot(mixed_share, full_out, preferred_element_type=jnp.float32)
     hidden_share = input_share + branch_scale * attn_share
     act_b_share = norm_rows(hidden_share, gain_mlp).astype(jnp.bfloat16)
-    upstream = jnp.concatenate([prompt_cot[0], cont_cot[0].reshape(cont_rows, width)], axis=0)
-    grad_mlp = slot_order((branch_scale * upstream.astype(jnp.float32)).astype(jnp.bfloat16))
-    grad_hidden = jnp.einsum("rd,fd->rf", grad_mlp, w_down, preferred_element_type=jnp.float32)
-    act_b_slots = slots_from(act_b_share)
+    forward, backward = (act_b_share, act_b_share)
+    arrived = {0: act_b_share}
+    for step in range(1, count):
+        forward, backward = hop_step(forward, backward, step, count)
+        arrived[-step], arrived[step] = (forward, backward)
+    act_b_slots = slots_from(arrived)
     hidden_list, gate_list, up_list, part_list = ([], [], [], [])
     for s in range(count):
         gate_proj = jnp.dot(act_b_slots[s], w_gate, preferred_element_type=jnp.float32)
@@ -323,120 +357,155 @@
         sigmoid_gate = jax.nn.sigmoid(gate_proj)
         silu_gate = gate_proj * sigmoid_gate
         grad_slot = grad_hidden[s * share_rows : (s + 1) * share_rows]
-        hidden_list.append((silu_gate * up_proj).astype(jnp.bfloat16))
-        gate_list.append(
-            (grad_slot * up_proj * sigmoid_gate * (1.0 + gate_proj * (1.0 - sigmoid_gate))).astype(
-                jnp.bfloat16
+        hidden = (silu_gate * up_proj).astype(jnp.bfloat16)
+        grad_gate_slot = (
+            grad_slot * up_proj * sigmoid_gate * (1.0 + gate_proj * (1.0 - sigmoid_gate))
+        ).astype(jnp.bfloat16)
+        grad_up_slot = (grad_slot * silu_gate).astype(jnp.bfloat16)
+        part = (
+            jnp.einsum("rf,df->rd", grad_gate_slot, w_gate, preferred_element_type=jnp.float32)
+            + jnp.einsum("rf,df->rd", grad_up_slot, w_up, preferred_element_type=jnp.float32)
+        ).astype(jnp.bfloat16)
+        if s + 1 < count:
+            hidden, grad_gate_slot, grad_up_slot, part, act_b_slots[s + 1] = tied(
+                hidden, grad_gate_slot, grad_up_slot, part, act_b_slots[s + 1]
             )
-        )
-        up_list.append((grad_slot * silu_gate).astype(jnp.bfloat16))
-        part_list.append(
-            (
-                jnp.einsum("rf,df->rd", gate_list[s], w_gate, preferred_element_type=jnp.float32)
-                + jnp.einsum("rf,df->rd", up_list[s], w_up, preferred_element_type=jnp.float32)
-            ).astype(jnp.bfloat16)
-        )
-
-    def slot_part(distance):
-        return picked(
-            me,
-            part_list,
-            {
-                i: slot_of[i][i + distance]
-                for i in range(count)
-                if 0 <= i + distance < count
-            },
-        )
-
-    normed_share = line_sum(slot_part, count)
+        hidden_list.append(hidden)
+        gate_list.append(grad_gate_slot)
+        up_list.append(grad_up_slot)
+        part_list.append(part)
+    last = count - 1
+    part_list[last], hidden_list[last], gate_list[last], up_list[last] = tied(
+        part_list[last], hidden_list[last], gate_list[last], up_list[last]
+    )
+    act_b = jnp.concatenate(act_b_slots, axis=0)
+    hidden_act = jnp.concatenate(hidden_list, axis=0)
+    grad_gate_act = jnp.concatenate(gate_list, axis=0)
+    grad_up_act = jnp.concatenate(up_list, axis=0)
+
+    def over_tokens(values):
+        return lax.psum_scatter(
+            values.astype(jnp.bfloat16), ("dp", "ctx"), scatter_dimension=0, tiled=True
+        )
+
+    fillers = [
+        lambda: jnp.einsum(
+            "rd,rf->df",
+            act_b,
+            jnp.concatenate([grad_gate_act, grad_up_act], axis=1),
+            preferred_element_type=jnp.float32,
+        ),
+        lambda: jnp.einsum("rf,rd->df", hidden_act, grad_mlp, preferred_element_type=jnp.float32),
+        lambda: jnp.dot(hidden_act, w_down, preferred_element_type=jnp.float32),
+    ]
+    filled = []
+    state = None
+    for distance in range(count - 1, 0, -1):
+        state = sum_step(state, slot_part(part_list), distance, count)
+        if fillers:
+            filled.append(fillers.pop(0)().astype(jnp.bfloat16))
+            state, filled[-1] = tied(state, filled[-1])
+    filled.extend(filler().astype(jnp.bfloat16) for filler in fillers)
+    wide_sum = over_tokens(filled[0])
+    down_sum = over_tokens(filled[1])
+    mlp_part = filled[2]
+    normed_share = sum_end(state, slot_part(part_list))
     through_mlp, gain_mlp_part = norm_back(hidden_share, gain_mlp, normed_share)
     res_share = share_of(upstream).astype(jnp.float32) + through_mlp
     grad_attn_share = (branch_scale * res_share).astype(jnp.bfloat16)
     mixed_grad = jnp.einsum(
         "rd,qd->rq", grad_attn_share, full_out, preferred_element_type=jnp.float32
     ).astype(jnp.bfloat16)
-    grad_mixed = jnp.concatenate(
+    grad_list = []
+    for head in range(kv_heads):
+        grad_list.append(
+            jnp.concatenate(
+                exchanged(
+                    me,
+                    lambda target: lax.dynamic_slice_in_dim(
+                        mixed_grad,
+                        target * (kv_heads * group_width) + head * group_width,
+                        group_width,
+                        1,
+                    ),
+                    count,
+                ),
+                axis=0,
+            )
+        )
+    mlp_slots = slot_part(
+        [mlp_part[s * share_rows : (s + 1) * share_rows] for s in range(count)]
+    )
+    pieces = [(head, prompt) for head in range(kv_heads) for prompt in (True, False)]
+    upstream_pieces = {
+        (head, prompt): grad_list[head][:own_rows] if prompt else grad_list[head][own_rows:]
+        for head, prompt in pieces
+    }
+    piece_grads = {}
+    upstream_pieces[pieces[0]], gather_start = tied(upstream_pieces[pieces[0]], grad_attn_share)
+    arrived = {0: grad_attn_share}
+    forward, backward = (gather_start, gather_start)
+    mlp_state = None
+    for place in range(max(count, len(pieces))):
+        moved = []
+        if place < count - 1:
+            forward, backward = hop_step(forward, backward, place + 1, count)
+            moved += [forward, backward]
+        if 1 <= place < count:
+            mlp_state = sum_step(mlp_state, mlp_slots, count - place, count)
+            moved += mlp_state
+        if place < len(pieces):
+            query_piece, keys_piece, values_piece, mask_piece = head_inputs(*pieces[place])
+            piece_grads[pieces[place]] = attend_backward(
+                query_piece,
+                keys_piece,
+                values_piece,
+                mask_piece,
+                totals[pieces[place]],
+                upstream_pieces[pieces[place]],
+            )
+        if place + 1 < len(pieces):
+            following = pieces[place + 1]
+            moved, piece_grads[pieces[place]], upstream_pieces[following] = tied(
+                moved, piece_grads[pieces[place]], upstream_pieces[following]
+            )
+        if place < count - 1:
+            forward, backward, *moved = moved
+            arrived[-place - 1], arrived[place + 1] = (forward, backward)
+        if 1 <= place < count:
+            mlp_state = tuple(moved)
+    mlp_share = sum_end(mlp_state, mlp_slots)
+    result_share = (hidden_share + branch_scale * mlp_share).astype(jnp.bfloat16)
+    grad_attn = jnp.concatenate(slots_from(arrived), axis=0)
+    grad_out = jnp.einsum(
+        "rq,rd->dq", slot_order(mixed_heads), grad_attn, preferred_element_type=jnp.float32
+    )
+    query_grad_rows = jnp.concatenate(
         [
-            lax.all_to_all(
-                mixed_grad[:, h * count * head_half : (h + 1) * count * head_half],
-                "tensor",
-                split_axis=1,
-                concat_axis=0,
-                tiled=True,
-            )
-            for h in range(2)
+            jnp.concatenate([piece_grads[head, True][0], piece_grads[head, False][0]], axis=0)
+            for head in range(kv_heads)
         ],
         axis=1,
     )
-    act_b = jnp.concatenate(act_b_slots, axis=0)
-    hidden_act = jnp.concatenate(hidden_list, axis=0)
-    grad_gate_act = jnp.concatenate(gate_list, axis=0)
-    grad_up_act = jnp.concatenate(up_list, axis=0)
-    grad_down = jnp.einsum("rf,rd->df", hidden_act, grad_mlp, preferred_element_type=jnp.float32)
-    grad_gate = jnp.einsum("rd,rf->df", act_b, grad_gate_act, preferred_element_type=jnp.float32)
-    grad_up = jnp.einsum("rd,rf->df", act_b, grad_up_act, preferred_element_type=jnp.float32)
-    mlp_sum = lax.psum_scatter(
-        jnp.concatenate([grad_gate, grad_up, grad_down], axis=1).astype(jnp.bfloat16),
-        ("dp", "ctx"),
-        scatter_dimension=0,
-        tiled=True,
-    )
-    mlp_part = jnp.dot(hidden_act, w_down, preferred_element_type=jnp.float32).astype(jnp.bfloat16)
-    mlp_part, mlp_sum = lax.optimization_barrier((mlp_part, mlp_sum))
-    mlp_natural = jnp.concatenate(
+    prompt_pairs_grad = jnp.concatenate(
         [
-            lax.dynamic_slice_in_dim(
-                mlp_part,
-                picked(
-                    me,
-                    {s: jnp.int32(s * share_rows) for s in range(count)},
-                    {i: slot_of[i][c] for i in range(count)},
-                ),
-                share_rows,
-                0,
-            )
-            for c in range(count)
+            piece_grads[head, True][which] + piece_grads[head, False][which][:prompt_total]
+            for which in (1, 2)
+            for head in range(kv_heads)
         ],
-        axis=0,
-    )
-    mlp_share = lax.psum_scatter(
-        mlp_natural, "tensor", scatter_dimension=0, tiled=True
-    ).astype(jnp.float32)
-    result_share = (hidden_share + branch_scale * mlp_share).astype(jnp.bfloat16)
-    result = lax.all_gather(result_share, "tensor", axis=0, tiled=True)
-    prompt_out = result[:own_rows][None]
-    cont_out = result[own_rows:].reshape(1, cont_count, CONT_LENGTH, width)
-    grad_attn = jnp.concatenate(slots_from(grad_attn_share), axis=0)
-    grad_out = jnp.einsum(
-        "rq,rd->dq", slot_order(mixed_heads), grad_attn, preferred_element_type=jnp.float32
-    )
-    query_grads = []
-    block_index = 0
-    low_row = block_index * block_rows
-    block_queries = query_rows[low_row : low_row + block_rows]
-    block_grad = grad_mixed[low_row : low_row + block_rows]
-    grad_query_block, grad_key_block, grad_value_block = attend_backward(
-        block_queries,
-        shared_prompt_keys,
-        shared_prompt_values,
-        block_masks[block_index],
-        total_list[block_index],
-        block_grad,
-    )
-    query_grads.append(grad_query_block)
-    prompt_key_grad = grad_key_block
-    prompt_value_grad = grad_value_block
-    grad_query_cont, grad_key_cont, grad_value_cont = attend_backward(
-        query_rows[own_rows:], cont_keys, cont_values, cont_mask, total_cont, grad_mixed[own_rows:]
-    )
-    query_grads.append(grad_query_cont)
-    prompt_key_grad = prompt_key_grad + grad_key_cont[:prompt_total]
-    prompt_value_grad = prompt_value_grad + grad_value_cont[:prompt_total]
-    pair_grads = lax.psum_scatter(
-        jnp.concatenate([prompt_key_grad, prompt_value_grad], axis=1),
+        axis=1,
+    )
+    grad_key_cont, grad_value_cont = (
+        jnp.concatenate([piece_grads[head, False][which] for head in range(kv_heads)], axis=1)
+        for which in (1, 2)
+    )
+    other_pairs = lax.ppermute(
+        lax.dynamic_slice_in_dim(prompt_pairs_grad, (1 - ctx_index) * own_rows, own_rows, 0),
         "ctx",
-        scatter_dimension=0,
-        tiled=True,
+        [(0, 1), (1, 0)],
+    )
+    pair_grads = other_pairs + lax.dynamic_slice_in_dim(
+        prompt_pairs_grad, ctx_index * own_rows, own_rows, 0
     )
     key_grad_rows = jnp.concatenate(
         [pair_grads[:, :key_width], grad_key_cont[prompt_total:]], axis=0
@@ -444,7 +513,6 @@
     value_grad_rows = jnp.concatenate(
         [pair_grads[:, key_width:], grad_value_cont[prompt_total:]], axis=0
     )
-    query_grad_rows = jnp.concatenate(query_grads, axis=0)
     grad_query_lin = rotate(query_grad_rows, cos_table, -sin_table).astype(jnp.bfloat16)
     grad_key_lin = rotate(key_grad_rows, cos_table, -sin_table).astype(jnp.bfloat16)
     grad_value_lin = value_grad_rows.astype(jnp.bfloat16)
@@ -462,15 +530,36 @@
         place = jnp.clip(me + distance, 0, count - 1) * share_rows
         return lax.dynamic_slice_in_dim(input_part, place, share_rows, 0)
 
-    input_grad_share = line_sum(row_part, count)
+    state = None
+    forward, backward = hop_step(result_share, result_share, 1, count)
+    forward, backward, input_part, wide_sum = tied(forward, backward, input_part, wide_sum)
+    result_arrived = {0: result_share, -1: forward, 1: backward}
+    for distance in range(count - 1, 0, -1):
+        state = sum_step(state, row_part, distance, count)
+        step = count - distance + 1
+        if step < count:
+            forward, backward = hop_step(forward, backward, step, count)
+            state, forward, backward, down_sum = tied(state, forward, backward, down_sum)
+            result_arrived[-step], result_arrived[step] = (forward, backward)
+    input_grad_share = sum_end(state, row_part)
+
+    def rows_from(arrived):
+        chunks = [picked(me, arrived, {i: c - i for i in range(count)}) for c in range(count)]
+        gathered = jnp.concatenate(chunks, axis=0)
+        return (
+            gathered[:own_rows][None],
+            gathered[own_rows:].reshape(1, cont_count, CONT_LENGTH, width),
+        )
+
+    prompt_out, cont_out = rows_from(result_arrived)
     through_attn, gain_attn_part = norm_back(input_share, gain_attn, input_grad_share)
-    arrived = line_hops((res_share + through_attn).astype(jnp.bfloat16), count)
-    grad_chunks = [
-        picked(me, arrived, {i: c - i for i in range(count)}) for c in range(count)
-    ]
-    grad_input = jnp.concatenate(grad_chunks, axis=0)
-    prompt_grad = grad_input[:own_rows][None]
-    cont_grad = grad_input[own_rows:].reshape(1, cont_count, CONT_LENGTH, width)
+    grad_share = (res_share + through_attn).astype(jnp.bfloat16)
+    forward, backward = (grad_share, grad_share)
+    arrived = {0: grad_share}
+    for step in range(1, count):
+        forward, backward = hop_step(forward, backward, step, count)
+        arrived[-step], arrived[step] = (forward, backward)
+    prompt_grad, cont_grad = rows_from(arrived)
     gain_own = lax.psum(
         lax.psum_scatter(
             jnp.stack([gain_attn_part, gain_mlp_part]),
@@ -480,15 +569,14 @@
         ),
         "tensor",
     )
-    mlp_sum = mlp_sum.astype(jnp.float32)
     attn_sum = lax.psum_scatter(
         jnp.concatenate([grad_query, grad_key, grad_value, grad_out], axis=1).astype(jnp.bfloat16),
         ("dp", "ctx"),
         scatter_dimension=0,
         tiled=True,
     ).astype(jnp.float32)
-    ff = grad_gate.shape[1]
     qw = grad_query.shape[1]
+    ff = w_gate.shape[1]
     summed = (
         gain_own[0],
         attn_sum[:, :qw],
@@ -496,9 +584,9 @@
         attn_sum[:, qw + key_width : qw + 2 * key_width],
         attn_sum[:, qw + 2 * key_width :].T,
         gain_own[1],
-        mlp_sum[:, :ff],
-        mlp_sum[:, ff : 2 * ff],
-        mlp_sum[:, 2 * ff :].T,
+        wide_sum[:, :ff].astype(jnp.float32),
+        wide_sum[:, ff:].astype(jnp.float32),
+        down_sum.astype(jnp.float32).T,
     )
     return (
         prompt_out,

time: 1170 us -> 864 us (0.74)
  waiting for transfers between devices: 529 us -> 224 us
  starting transfers between devices: 77.1 us -> 122 us
  matrix products: 314 us -> 271 us
  blocking collectives: 32.5 us -> 14.4 us
    reduce_scatter x3 -> x2, waiting for transfers between devices: 136 us -> 0.02 us  [over_tokens(): lax.psum_scatter(values.astype(jnp.bfloat16), ('dp', 'ctx'), scatter_dime...]
    ppermute x30 -> x55, waiting for transfers between devices: 309 us -> 189 us  [the longest x12 77.3 us: hop_step(): lax.ppermute(backward, 'tensor', [(i, i - 1) for i in range(1, count - st...]
    ppermute x30 -> x55, starting transfers between devices: 60.8 us -> 121 us  [the longest x9 40.6 us: sum_step(): lax.ppermute(to_right, 'tensor', [(i, i + 1) for i in range(0, count - di...]
    all_gather x3 -> x1, waiting for transfers between devices: 47.1 us -> 0.01 us  [shards(): lax.all_gather(own_out_half, ('tensor', 'ctx'), axis=0, tiled=True)]
    unnamed x9 -> x6, waiting for transfers between devices: 0.13 us -> 35.3 us
    all_to_all x3 -> x0, waiting for transfers between devices: 32.3 us -> none  [the longest x2 25.9 us: shards(): lax.all_to_all(mixed_grad[:, h * count * head_half:(h + 1) * count * head...]
    another operation x4 -> x9, other arithmetic: 0.8 us -> 20.7 us
    all_to_all x1 -> x0, blocking collectives: 18 us -> none  [shards(): lax.all_to_all(mixed_heads[:, h * head_half:(h + 1) * head_half], 'tensor...]
  transfers between devices with their start and end apart: 41 -> 60, of which waited for: 21 -> 21; matrix products, arithmetic and copies ran while one was open for 23% -> 44% of each run, Pallas kernels for 0% -> 0%
where the time goes in v3:
time: 864 us; the launch traced here: 855 us
  matrix products  271 us (31%)
  waiting for transfers between devices  224 us (26%)
  other arithmetic  147 us (17%)
  starting transfers between devices  122 us (14%)
  local copies, waits for them, and re-layouts  59.4 us (7%)
  between operations  17.2 us (2%)
  blocking collectives  14.4 us (2%)
    ppermute x12, waiting for transfers between devices, hop_step(): lax.ppermute(backward, 'tensor', [(i, i - 1) for i in range(1, count - st...  77.3 us
    ppermute x9, starting transfers between devices, sum_step(): lax.ppermute(to_right, 'tensor', [(i, i + 1) for i in range(0, count - di...  40.6 us
    ppermute x9, waiting for transfers between devices, sum_step(): lax.ppermute(to_right, 'tensor', [(i, i + 1) for i in range(0, count - di...  38.8 us
    unnamed x6, waiting for transfers between devices  35.3 us
    dot_general x4, matrix products, attend_backward(): jnp.einsum('bhgd,khd->hgbk', grad_heads, value_head_rows, preferred_eleme...  32.9 us
    unnamed x280, local copies, waits for them, and re-layouts  31.1 us
    ppermute x12, starting transfers between devices, hop_step(): lax.ppermute(forward, 'tensor', [(i, i + 1) for i in range(step - 1, coun...  30.2 us
    ppermute x12, waiting for transfers between devices, hop_step(): lax.ppermute(forward, 'tensor', [(i, i + 1) for i in range(step - 1, coun...  28.4 us
  transfers between devices with their start and end apart: 60, of which 21 were waited for; matrix products, arithmetic and copies ran while one was open for 44% of the time, Pallas kernels for 0%

profile of v3, /device:TPU:0, one launch (start us, length us, event | category | flops | bytes accessed | tf_op | source)
XLA Modules:
  0.0 854.6 jit_solution(7748369297286258198)
XLA Ops:
  70.1 6.4 convolution_convert_fusion.7
  102.4 11.1 %fusion.157 = f32[1024,2048]{1,0:T(8,128)} fusion(bf16[1024,2048]{1,0:T(8,128)(2,1)S(1)} %pad_maximum_fusion.2, bf16[2048,2048]{1,0:T(8,128)(2,1)S(1)} %bitcast.493), kind=kOutput, calls=%fused_computation.378 | convolution fusion | flops 8589934592 | bytes 20971520 | tf_op jit(solution)/shard_map/rd,fd->rf/dot_general | solution.py:338
  132.3 6.7 multiply_reduce_fusion.6
  150.1 12.2 %collective-permute-done.6 = bf16[256,2048]{1,0:T(8,128)(2,1)} collective-permute-done((bf16[256,2048]{1,0:T(8,128)(2,1)S(1)}, bf16[256,2048]{1,0:T(8,128)(2,1)}, u32[]{:S(2)}, u32[]{:S(2)}) %collective-permute-start.6) | collective-permute-done | bytes 1048608 | tf_op jit(solution)/shard_map/ppermute | solution.py:155
  169.0 8.1 multiply_convert_fusion.12
  177.9 14.2 %collective-permute-done.9 = bf16[256,2048]{1,0:T(8,128)(2,1)S(1)} collective-permute-done((bf16[256,2048]{1,0:T(8,128)(2,1)}, bf16[256,2048]{1,0:T(8,128)(2,1)S(1)}, u32[]{:S(2)}, u32[]{:S(2)}) %collective-permute-start.9) | collective-permute-done | bytes 1048608 | tf_op jit(solution)/shard_map/ppermute | solution.py:156
  201.9 13.3 %collective-permute-done.11 = bf16[256,2048]{1,0:T(8,128)(2,1)S(1)} collective-permute-done((bf16[256,2048]{1,0:T(8,128)(2,1)S(1)}, bf16[256,2048]{1,0:T(8,128)(2,1)S(1)}, u32[]{:S(2)}, u32[]{:S(2)}) %collective-permute-start.11) | collective-permute-done | bytes 1048608 | tf_op jit(solution)/shard_map/ppermute | solution.py:156
  216.8 6.9 fusion.160
  231.8 6.9 fusion.61
  252.5 6.7 fusion.62
  273.3 6.7 fusion.63
  284.7 25.8 %convolution_convert_fusion = bf16[2048,4096]{1,0:T(8,128)(2,1)} fusion(bf16[256,2048]{1,0:T(8,128)(2,1)} %copy-done.111, bf16[256,2048]{1,0:T(8,128)(2,1)} %copy-done.110, bf16[256,2048]{1,0:T(8,128)(2,1)} %copy-done.109, bf16[256,2048]{1,0:T(8,128)(2,1)} %copy-done.108, bf16[256,2048]{1,0:T(8,128)(2,1)} %copy-done.115, bf16[256,2048]{1,0:T(8,128)(2,1)} %copy-done.114, ...), kind=kOutput, calls=%fused_computation | convolution fusion | flops 17272143872 | bytes 29360128 | tf_op jit(solution)/shard_map/rd,rf->df/dot_general | solution.py:392
  325.3 11.5 %convolution_convert_fusion.1 = bf16[2048,2048]{1,0:T(8,128)(2,1)} fusion(bf16[1024,2048]{1,0:T(8,128)(2,1)S(1)} %copy-done.26, bf16[1024,2048]{1,0:T(8,128)(2,1)S(1)} %constant_dynamic-update-slice_fusion.4), kind=kOutput, calls=%fused_computation.54 | convolution fusion | flops 8594128896 | bytes 16777216 | tf_op jit(solution)/shard_map/rf,rd->df/dot_general | solution.py:398
  350.7 13.0 %convolution_convert_fusion.2 = bf16[1024,2048]{1,0:T(8,128)(2,1)} fusion(bf16[1024,2048]{1,0:T(8,128)(2,1)S(1)} %copy-done.91, bf16[2048,2048]{1,0:T(8,128)(2,1)} %param.25), kind=kOutput, calls=%fused_computation.88 | convolution fusion | flops 8592031744 | bytes 16777216 | tf_op jit(solution)/shard_map/dot_general | solution.py:399
  400.3 18.3 %collective-permute-done.20 = bf16[256,256]{1,0:T(8,128)(2,1)S(1)} collective-permute-done((bf16[256,256]{1,0:T(8,128)(2,1)S(1)}, bf16[256,256]{1,0:T(8,128)(2,1)S(1)}, u32[]{:S(2)}, u32[]{:S(2)}) %collective-permute-start.20) | collective-permute-done | bytes 131104 | tf_op jit(solution)/shard_map/ppermute | solution.py:187
  452.0 11.5 %fusion.3 = (f32[4,512]{1,0:T(4,128)S(1)}, f32[1536,512,4]{1,0,2:T(8,128)}) fusion(f32[1,4,512,1536]{2,3,1,0:T(8,128)} %copy-done.2, f32[4,512]{1,0:T(4,128)S(1)} %copy-done.95, bf16[512,4,64]{0,2,1:T(8,128)(2,1)} %bitcast.454, bf16[512,128]{1,0:T(8,128)(2,1)S(1)} %copy-done.32, bf16[1024,128]{1,0:T(8,128)(2,1)S(1)} %copy-done.23), kind=kOutput, calls=%fused_computation.10 | convolution fusion | flops 412481536 | bytes 25837568 | tf_op jit(solution)/shard_map/bhgd,khd->hgbk/dot_general | solution.py:95
  465.6 7.1 fusion.33
  487.0 7.7 collective-permute-start.32
  526.3 6.6 convolution_bitcast_fusion
  533.0 10.7 %fusion = (f32[4,512]{1,0:T(4,128)S(1)}, f32[1536,512,4]{1,0,2:T(8,128)}) fusion(f32[1,4,512,1536]{2,3,1,0:T(8,128)} %copy-done.1, f32[4,512]{1,0:T(4,128)S(1)} %copy-done.93, bf16[512,4,64]{0,2,1:T(8,128)(2,1)S(1)} %bitcast.457, bf16[512,128]{1,0:T(8,128)(2,1)S(1)} %copy-done.32, bf16[1024,128]{1,0:T(8,128)(2,1)S(1)} %copy-done.23), kind=kOutput, calls=%fused_computation.5 | convolution fusion | flops 412481536 | bytes 25837568 | tf_op jit(solution)/shard_map/bhgd,khd->hgbk/dot_general | solution.py:95
  545.5 7.0 fusion.34
  574.9 10.2 %pad_maximum_fusion = bf16[2048,1280]{0,1:T(8,128)(2,1)} fusion(bf16[2048,512]{0,1:T(8,128)(2,1)S(1)} %fusion.56, bf16[2048,128]{0,1:T(8,128)(2,1)S(1)} %convolution_convert_fusion.5, bf16[2048,128]{0,1:T(8,128)(2,1)S(1)} %convolution_convert_fusion.6, bf16[2048,512]{0,1:T(8,128)(2,1)S(1)} %convolution_convert_fusion.3), kind=kLoop, calls=%fused_computation.61 | loop fusion | flops 20971520 | bytes 10485760 | tf_op jit(solution)/shard_map/concatenate | solution.py:573
  598.6 16.2 %collective-permute-done.36 = bf16[256,2048]{1,0:T(8,128)(2,1)} collective-permute-done((bf16[256,2048]{1,0:T(8,128)(2,1)S(1)}, bf16[256,2048]{1,0:T(8,128)(2,1)}, u32[]{:S(2)}, u32[]{:S(2)}) %collective-permute-start.36) | collective-permute-done | bytes 1048608 | tf_op jit(solution)/shard_map/ppermute | solution.py:155
  633.0 16.6 %collective-permute-done.39 = bf16[256,2048]{1,0:T(8,128)(2,1)} collective-permute-done((bf16[256,2048]{1,0:T(8,128)(2,1)}, bf16[256,2048]{1,0:T(8,128)(2,1)}, u32[]{:S(2)}, u32[]{:S(2)}) %collective-permute-start.39) | collective-permute-done | bytes 1048608 | tf_op jit(solution)/shard_map/ppermute | solution.py:171
  649.6 8.4 collective-permute-done.42
  670.2 15.7 %collective-permute-done.43 = bf16[256,2048]{1,0:T(8,128)(2,1)} collective-permute-done((bf16[256,2048]{1,0:T(8,128)(2,1)}, bf16[256,2048]{1,0:T(8,128)(2,1)}, u32[]{:S(2)}, u32[]{:S(2)}) %collective-permute-start.43) | collective-permute-done | bytes 1048608 | tf_op jit(solution)/shard_map/ppermute | solution.py:171
  685.8 8.5 collective-permute-done.46
  707.5 15.8 %collective-permute-done.48 = bf16[256,2048]{1,0:T(8,128)(2,1)} collective-permute-done((bf16[256,2048]{1,0:T(8,128)(2,1)}, bf16[256,2048]{1,0:T(8,128)(2,1)}, u32[]{:S(2)}, u32[]{:S(2)}) %collective-permute-start.48) | collective-permute-done | bytes 1048608 | tf_op jit(solution)/shard_map/ppermute | solution.py:172
  748.2 8.5 collective-permute-done.52
  766.3 13.8 %collective-permute-done.53 = bf16[256,2048]{1,0:T(8,128)(2,1)} collective-permute-done((bf16[256,2048]{1,0:T(8,128)(2,1)}, bf16[256,2048]{1,0:T(8,128)(2,1)}, u32[]{:S(2)}, u32[]{:S(2)}) %collective-permute-start.53) | collective-permute-done | bytes 1048608 | tf_op jit(solution)/shard_map/ppermute | solution.py:156
  793.2 35.2 %reduce-scatter.13.cloned.1.call-done = f32[256,2]{1,0:T(8,128)} async-done(((f32[2048,2]{1,0:T(8,128)}), f32[256,2]{1,0:T(8,128)}) %reduce-scatter.13.cloned.1.call-update) | async-done | bytes 2064
  829.4 11.7 %psum.7 = f32[2,256]{1,0:T(2,128)S(1)} all-reduce(f32[2,256]{1,0:T(2,128)S(1)} %copy.218), channel_id=1, replica_groups=mesh['dp'=4,'ctx'=2,'tensor'=4] {'tensor'}, use_global_device_ids=true, to_apply=%region_22.23 | all-reduce | flops 512 | bytes 4096 | tf_op jit(solution)/shard_map/psum | solution.py:563
  (561 shorter events, 458.6 us)
Async XLA Ops:
  7.2 125.1 %all-gather.2.cloned.1.call-start = ((), (), s32[]{:S(2)}) async-start(), calls=%async_computation.4 | async-start | bytes 9437184 | tf_op jit(solution)/shard_map/all_gather | solution.py:263
  9.7 610.8 %reduce-scatter.7.cloned.1.call-start = ((), (), s32[]{:S(2)}) async-start(), calls=%async_computation.5 | async-start | bytes 18874368 | tf_op jit(solution)/shard_map/reduce_scatter | solution.py:387
  64.7 54.3 %collective-permute-start = (bf16[256,256]{1,0:T(8,128)(2,1)}, bf16[256,256]{1,0:T(8,128)(2,1)}, u32[]{:S(2)}, u32[]{:S(2)}) collective-permute-start(bf16[256,256]{1,0:T(8,128)(2,1)} %get-tuple-element.297), channel_id=1, source_target_pairs={{0,3},{1,0},{2,1},{3,2},{4,7},{5,4},{6,5},{7,6},{8,11},{9,8},{10,9... | collective-permute-start | bytes 393224 | tf_op jit(solution)/shard_map/ppermute | solution.py:187
  70.0 49.0 %collective-permute-start.1 = (bf16[256,256]{1,0:T(8,128)(2,1)}, bf16[256,256]{1,0:T(8,128)(2,1)}, u32[]{:S(2)}, u32[]{:S(2)}) collective-permute-start(bf16[256,256]{1,0:T(8,128)(2,1)} %get-tuple-element.298), channel_id=1, source_target_pairs={{0,2},{1,3},{2,0},{3,1},{4,6},{5,7},{6,4},{7,5},{8,10},{9,11},{10,... | collective-permute-start | bytes 393224 | tf_op jit(solution)/shard_map/ppermute | solution.py:187
  90.0 27.7 %collective-permute-start.5 = (bf16[256,256]{1,0:T(8,128)(2,1)S(1)}, bf16[256,256]{1,0:T(8,128)(2,1)S(1)}, u32[]{:S(2)}, u32[]{:S(2)}) collective-permute-start(bf16[256,256]{1,0:T(8,128)(2,1)S(1)} %get-tuple-element.293), channel_id=1, source_target_pairs={{0,1},{1,2},{2,3},{3,0},{4,5},{5,6},{6,7},{7,4},{8,9},{9,10},{10,1... | collective-permute-start | bytes 393224 | tf_op jit(solution)/shard_map/ppermute | solution.py:187
  91.0 26.8 %collective-permute-start.3 = (bf16[256,256]{1,0:T(8,128)(2,1)}, bf16[256,256]{1,0:T(8,128)(2,1)S(1)}, u32[]{:S(2)}, u32[]{:S(2)}) collective-permute-start(bf16[256,256]{1,0:T(8,128)(2,1)} %get-tuple-element.294), channel_id=1, source_target_pairs={{0,3},{1,0},{2,1},{3,2},{4,7},{5,4},{6,5},{7,6},{8,11},{9,8},{10,9... | collective-permute-start | bytes 393224 | tf_op jit(solution)/shard_map/ppermute | solution.py:187
  142.9 24.8 %collective-permute-start.7 = (bf16[256,2048]{1,0:T(8,128)(2,1)S(1)}, bf16[256,2048]{1,0:T(8,128)(2,1)}, u32[]{:S(2)}, u32[]{:S(2)}) collective-permute-start(bf16[256,2048]{1,0:T(8,128)(2,1)S(1)} %multiply_convert_fusion.15), channel_id=1, source_target_pairs={{1,0},{2,1},{3,2},{5,4},{6,5},{7,6},{9,8},{10,9},{11,10},{13,12},{... | collective-permute-start | bytes 3145736 | tf_op jit(solution)/shard_map/ppermute | solution.py:156
  177.2 24.8 %collective-permute-start.10 = (bf16[256,2048]{1,0:T(8,128)(2,1)S(1)}, bf16[256,2048]{1,0:T(8,128)(2,1)S(1)}, u32[]{:S(2)}, u32[]{:S(2)}) collective-permute-start(bf16[256,2048]{1,0:T(8,128)(2,1)S(1)} %collective-permute-done.8), channel_id=1, source_target_pairs={{2,3},{6,7},{10,11},{14,15},{18,19},{22,23},{26,27},{30,31}} | collective-permute-start | bytes 3145736 | tf_op jit(solution)/shard_map/ppermute | solution.py:155
  280.0 30.5 %collective-permute-start.12 = (bf16[256,2048]{1,0:T(8,128)(2,1)}, bf16[256,2048]{1,0:T(8,128)(2,1)}, u32[]{:S(2)}, u32[]{:S(2)}) collective-permute-start(bf16[256,2048]{1,0:T(8,128)(2,1)} %fusion.63), channel_id=1, source_target_pairs={{0,1},{4,5},{8,9},{12,13},{16,17},{20,21},{24,25},{28,29}} | collective-permute-start | bytes 3145736 | tf_op jit(solution)/shard_map/ppermute | solution.py:171
  282.8 27.7 %collective-permute-start.13 = (bf16[256,2048]{1,0:T(8,128)(2,1)}, bf16[256,2048]{1,0:T(8,128)(2,1)}, u32[]{:S(2)}, u32[]{:S(2)}) collective-permute-start(bf16[256,2048]{1,0:T(8,128)(2,1)} %fusion.63), channel_id=1, source_target_pairs={{3,2},{7,6},{11,10},{15,14},{19,18},{23,22},{27,26},{31,30}} | collective-permute-start | bytes 3145736 | tf_op jit(solution)/shard_map/ppermute | solution.py:172
  310.6 322.4 %reduce-scatter.9.cloned.1.call-start = ((), (), s32[]{:S(2)}) async-start(), calls=%async_computation.6 | async-start | bytes 9437184 | tf_op jit(solution)/shard_map/reduce_scatter | solution.py:387
  385.6 354.2 %reduce-scatter.11.cloned.1.call-start = ((), (), s32[]{:S(2)}) async-start(), calls=%async_computation.7 | async-start | bytes 5898240 | tf_op jit(solution)/shard_map/reduce_scatter | solution.py:572
  388.0 92.3 %collective-permute-start.25 = (bf16[256,2048]{1,0:T(8,128)(2,1)}, bf16[256,2048]{1,0:T(8,128)(2,1)}, u32[]{:S(2)}, u32[]{:S(2)}) collective-permute-start(bf16[256,2048]{1,0:T(8,128)(2,1)} %slice.227), channel_id=1, source_target_pairs={{0,1},{4,5},{8,9},{12,13},{16,17},{20,21},{24,25},{28,29}} | collective-permute-start | bytes 3145736 | tf_op jit(solution)/shard_map/ppermute | solution.py:171
  391.5 88.8 %collective-permute-start.26 = (bf16[256,2048]{1,0:T(8,128)(2,1)}, bf16[256,2048]{1,0:T(8,128)(2,1)}, u32[]{:S(2)}, u32[]{:S(2)}) collective-permute-start(bf16[256,2048]{1,0:T(8,128)(2,1)} %slice.227), channel_id=1, source_target_pairs={{3,2},{7,6},{11,10},{15,14},{19,18},{23,22},{27,26},{31,30}} | collective-permute-start | bytes 3145736 | tf_op jit(solution)/shard_map/ppermute | solution.py:172
  421.0 25.7 %collective-permute-start.21 = (bf16[256,2048]{1,0:T(8,128)(2,1)}, bf16[256,2048]{1,0:T(8,128)(2,1)}, u32[]{:S(2)}, u32[]{:S(2)}) collective-permute-start(bf16[256,2048]{1,0:T(8,128)(2,1)} %get-tuple-element.118), channel_id=1, source_target_pairs={{0,1},{1,2},{2,3},{4,5},{5,6},{6,7},{8,9},{9,10},{10,11},{12,13},{... | collective-permute-start | bytes 3145736 | tf_op jit(solution)/shard_map/ppermute | solution.py:155
  447.0 33.3 %collective-permute-start.23 = (bf16[256,2048]{1,0:T(8,128)(2,1)}, bf16[256,2048]{1,0:T(8,128)(2,1)}, u32[]{:S(2)}, u32[]{:S(2)}) collective-permute-start(bf16[256,2048]{1,0:T(8,128)(2,1)} %collective-permute-done.21), channel_id=1, source_target_pairs={{1,2},{2,3},{5,6},{6,7},{9,10},{10,11},{13,14},{14,15},{17,18},{18... | collective-permute-start | bytes 3145736 | tf_op jit(solution)/shard_map/ppermute | solution.py:155
  448.6 31.7 %collective-permute-start.24 = (bf16[256,2048]{1,0:T(8,128)(2,1)}, bf16[256,2048]{1,0:T(8,128)(2,1)}, u32[]{:S(2)}, u32[]{:S(2)}) collective-permute-start(bf16[256,2048]{1,0:T(8,128)(2,1)} %collective-permute-done.22), channel_id=1, source_target_pairs={{1,0},{2,1},{5,4},{6,5},{9,8},{10,9},{13,12},{14,13},{17,16},{18,1... | collective-permute-start | bytes 3145736 | tf_op jit(solution)/shard_map/ppermute | solution.py:156
  480.4 35.2 %collective-permute-start.30 = (bf16[256,2048]{1,0:T(8,128)(2,1)}, bf16[256,2048]{1,0:T(8,128)(2,1)}, u32[]{:S(2)}, u32[]{:S(2)}) collective-permute-start(bf16[256,2048]{1,0:T(8,128)(2,1)} %collective-permute-done.23), channel_id=1, source_target_pairs={{2,3},{6,7},{10,11},{14,15},{18,19},{22,23},{26,27},{30,31}} | collective-permute-start | bytes 3145736 | tf_op jit(solution)/shard_map/ppermute | solution.py:155
  482.0 33.6 %collective-permute-start.31 = (bf16[256,2048]{1,0:T(8,128)(2,1)}, bf16[256,2048]{1,0:T(8,128)(2,1)}, u32[]{:S(2)}, u32[]{:S(2)}) collective-permute-start(bf16[256,2048]{1,0:T(8,128)(2,1)} %collective-permute-done.24), channel_id=1, source_target_pairs={{1,0},{5,4},{9,8},{13,12},{17,16},{21,20},{25,24},{29,28}} | collective-permute-start | bytes 3145736 | tf_op jit(solution)/shard_map/ppermute | solution.py:156
  487.0 28.6 %collective-permute-start.32 = (bf16[256,2048]{1,0:T(8,128)(2,1)}, bf16[256,2048]{1,0:T(8,128)(2,1)}, u32[]{:S(2)}, u32[]{:S(2)}) collective-permute-start(bf16[256,2048]{1,0:T(8,128)(2,1)} %get-tuple-element.233), channel_id=1, source_target_pairs={{0,1},{1,2},{4,5},{5,6},{8,9},{9,10},{12,13},{13,14},{16,17},{17,1... | collective-permute-start | bytes 3145736 | tf_op jit(solution)/shard_map/ppermute | solution.py:171
  519.3 65.9 %collective-permute-start.35 = (bf16[256,2048]{1,0:T(8,128)(2,1)}, bf16[256,2048]{1,0:T(8,128)(2,1)}, u32[]{:S(2)}, u32[]{:S(2)}) collective-permute-start(bf16[256,2048]{1,0:T(8,128)(2,1)} %get-tuple-element.231), channel_id=1, source_target_pairs={{1,0},{2,1},{3,2},{5,4},{6,5},{7,6},{9,8},{10,9},{11,10},{13,12},{... | collective-permute-start | bytes 3145736 | tf_op jit(solution)/shard_map/ppermute | solution.py:172
  520.6 64.6 %collective-permute-start.34 = (bf16[256,2048]{1,0:T(8,128)(2,1)}, bf16[256,2048]{1,0:T(8,128)(2,1)}, u32[]{:S(2)}, u32[]{:S(2)}) collective-permute-start(bf16[256,2048]{1,0:T(8,128)(2,1)} %get-tuple-element.230), channel_id=1, source_target_pairs={{0,1},{1,2},{2,3},{4,5},{5,6},{6,7},{8,9},{9,10},{10,11},{12,13},{... | collective-permute-start | bytes 3145736 | tf_op jit(solution)/shard_map/ppermute | solution.py:171
  585.1 243.2 %reduce-scatter.13.cloned.1.call-start = ((), (), s32[]{:S(2)}) async-start(), calls=%async_computation.8 | async-start | bytes 1179648
  588.5 26.2 %collective-permute-start.36 = (bf16[256,2048]{1,0:T(8,128)(2,1)S(1)}, bf16[256,2048]{1,0:T(8,128)(2,1)}, u32[]{:S(2)}, u32[]{:S(2)}) collective-permute-start(bf16[256,2048]{1,0:T(8,128)(2,1)S(1)} %add_convert_fusion.6), channel_id=1, source_target_pairs={{0,1},{1,2},{2,3},{4,5},{5,6},{6,7},{8,9},{9,10},{10,11},{12,13},{... | collective-permute-start | bytes 3145736 | tf_op jit(solution)/shard_map/ppermute | solution.py:155
  592.7 27.9 %collective-permute-start.37 = (bf16[256,2048]{1,0:T(8,128)(2,1)S(1)}, bf16[256,2048]{1,0:T(8,128)(2,1)}, u32[]{:S(2)}, u32[]{:S(2)}) collective-permute-start(bf16[256,2048]{1,0:T(8,128)(2,1)S(1)} %add_convert_fusion.6), channel_id=1, source_target_pairs={{1,0},{2,1},{3,2},{5,4},{6,5},{7,6},{9,8},{10,9},{11,10},{13,12},{... | collective-permute-start | bytes 3145736 | tf_op jit(solution)/shard_map/ppermute | solution.py:156
  623.8 25.8 %collective-permute-start.39 = (bf16[256,2048]{1,0:T(8,128)(2,1)}, bf16[256,2048]{1,0:T(8,128)(2,1)}, u32[]{:S(2)}, u32[]{:S(2)}) collective-permute-start(bf16[256,2048]{1,0:T(8,128)(2,1)} %get-tuple-element.229), channel_id=1, source_target_pairs={{0,1},{4,5},{8,9},{12,13},{16,17},{20,21},{24,25},{28,29}} | collective-permute-start | bytes 3145736 | tf_op jit(solution)/shard_map/ppermute | solution.py:171
  631.7 26.3 %collective-permute-start.42 = (bf16[256,2048]{1,0:T(8,128)(2,1)}, bf16[256,2048]{1,0:T(8,128)(2,1)}, u32[]{:S(2)}, u32[]{:S(2)}) collective-permute-start(bf16[256,2048]{1,0:T(8,128)(2,1)} %collective-permute-done.37), channel_id=1, source_target_pairs={{1,0},{2,1},{5,4},{6,5},{9,8},{10,9},{13,12},{14,13},{17,16},{18,1... | collective-permute-start | bytes 3145736 | tf_op jit(solution)/shard_map/ppermute | solution.py:156
  668.9 25.5 %collective-permute-start.46 = (bf16[256,2048]{1,0:T(8,128)(2,1)}, bf16[256,2048]{1,0:T(8,128)(2,1)}, u32[]{:S(2)}, u32[]{:S(2)}) collective-permute-start(bf16[256,2048]{1,0:T(8,128)(2,1)} %collective-permute-done.42), channel_id=1, source_target_pairs={{1,0},{5,4},{9,8},{13,12},{17,16},{21,20},{25,24},{29,28}} | collective-permute-start | bytes 3145736 | tf_op jit(solution)/shard_map/ppermute | solution.py:156
  698.7 24.6 %collective-permute-start.48 = (bf16[256,2048]{1,0:T(8,128)(2,1)}, bf16[256,2048]{1,0:T(8,128)(2,1)}, u32[]{:S(2)}, u32[]{:S(2)}) collective-permute-start(bf16[256,2048]{1,0:T(8,128)(2,1)} %get-tuple-element.225), channel_id=1, source_target_pairs={{1,0},{2,1},{3,2},{5,4},{6,5},{7,6},{9,8},{10,9},{11,10},{13,12},{... | collective-permute-start | bytes 3145736 | tf_op jit(solution)/shard_map/ppermute | solution.py:172
  700.0 24.5 %collective-permute-start.47 = (bf16[256,2048]{1,0:T(8,128)(2,1)}, bf16[256,2048]{1,0:T(8,128)(2,1)}, u32[]{:S(2)}, u32[]{:S(2)}) collective-permute-start(bf16[256,2048]{1,0:T(8,128)(2,1)} %get-tuple-element.224), channel_id=1, source_target_pairs={{0,1},{1,2},{2,3},{4,5},{5,6},{6,7},{8,9},{9,10},{10,11},{12,13},{... | collective-permute-start | bytes 3145736 | tf_op jit(solution)/shard_map/ppermute | solution.py:171
  780.0 61.6 %collective-permute-start.54 = (bf16[256,2048]{1,0:T(8,128)(2,1)}, bf16[256,2048]{1,0:T(8,128)(2,1)}, u32[]{:S(2)}, u32[]{:S(2)}) collective-permute-start(bf16[256,2048]{1,0:T(8,128)(2,1)} %collective-permute-done.53), channel_id=1, source_target_pairs={{1,0},{5,4},{9,8},{13,12},{17,16},{21,20},{25,24},{29,28}} | collective-permute-start | bytes 3145736 | tf_op jit(solution)/shard_map/ppermute | solution.py:156
  781.3 60.3 %collective-permute-start.51 = (bf16[256,2048]{1,0:T(8,128)(2,1)}, bf16[256,2048]{1,0:T(8,128)(2,1)}, u32[]{:S(2)}, u32[]{:S(2)}) collective-permute-start(bf16[256,2048]{1,0:T(8,128)(2,1)} %collective-permute-done.50), channel_id=1, source_target_pairs={{2,3},{6,7},{10,11},{14,15},{18,19},{22,23},{26,27},{30,31}} | collective-permute-start | bytes 3145736 | tf_op jit(solution)/shard_map/ppermute | solution.py:155
  (162 other events, 2005.1 us)
Sparse Core Ops, SparseCore 0:
  10.2 104.0 all-gather.1
  310.7 114.5 reduce-scatter.6
  428.8 71.4 reduce-scatter.8
  585.3 58.6 reduce-scatter.10
  787.7 40.6 reduce-scatter.12

commit v4 on v3

--- a/solution.py
+++ b/solution.py
@@ -193,6 +193,20 @@
         picked(me, received, {i: (i - source) % count for i in range(count)})
         for source in range(count)
     ]
+
+
+def pair_stages():
+    return [
+        (axis, 1 << bit)
+        for axis in ("ctx", "tensor", "dp")
+        for bit in range(lax.axis_size(axis).bit_length() - 1)
+    ]
+
+
+def pair_sum(values, axis, distance):
+    return values + lax.ppermute(
+        values, axis, [(i, i ^ distance) for i in range(lax.axis_size(axis))]
+    )
 
 
 def shards(
@@ -346,12 +360,14 @@
     act_b_share = norm_rows(hidden_share, gain_mlp).astype(jnp.bfloat16)
     forward, backward = (act_b_share, act_b_share)
     arrived = {0: act_b_share}
-    for step in range(1, count):
-        forward, backward = hop_step(forward, backward, step, count)
-        arrived[-step], arrived[step] = (forward, backward)
-    act_b_slots = slots_from(arrived)
+    act_b_slots = []
     hidden_list, gate_list, up_list, part_list = ([], [], [], [])
     for s in range(count):
+        act_b_slots.append(
+            picked(me, arrived, {i: order[i][s] - i for i in range(count)})
+        )
+        if s + 1 < count:
+            forward, backward = hop_step(forward, backward, s + 1, count)
         gate_proj = jnp.dot(act_b_slots[s], w_gate, preferred_element_type=jnp.float32)
         up_proj = jnp.dot(act_b_slots[s], w_up, preferred_element_type=jnp.float32)
         sigmoid_gate = jax.nn.sigmoid(gate_proj)
@@ -366,18 +382,14 @@
             jnp.einsum("rf,df->rd", grad_gate_slot, w_gate, preferred_element_type=jnp.float32)
             + jnp.einsum("rf,df->rd", grad_up_slot, w_up, preferred_element_type=jnp.float32)
         ).astype(jnp.bfloat16)
-        if s + 1 < count:
-            hidden, grad_gate_slot, grad_up_slot, part, act_b_slots[s + 1] = tied(
-                hidden, grad_gate_slot, grad_up_slot, part, act_b_slots[s + 1]
-            )
+        forward, backward, hidden, grad_gate_slot, grad_up_slot, part = tied(
+            forward, backward, hidden, grad_gate_slot, grad_up_slot, part
+        )
+        arrived[-s - 1], arrived[s + 1] = (forward, backward)
         hidden_list.append(hidden)
         gate_list.append(grad_gate_slot)
         up_list.append(grad_up_slot)
         part_list.append(part)
-    last = count - 1
-    part_list[last], hidden_list[last], gate_list[last], up_list[last] = tied(
-        part_list[last], hidden_list[last], gate_list[last], up_list[last]
-    )
     act_b = jnp.concatenate(act_b_slots, axis=0)
     hidden_act = jnp.concatenate(hidden_list, axis=0)
     grad_gate_act = jnp.concatenate(gate_list, axis=0)
@@ -389,14 +401,9 @@
         )
 
     fillers = [
-        lambda: jnp.einsum(
-            "rd,rf->df",
-            act_b,
-            jnp.concatenate([grad_gate_act, grad_up_act], axis=1),
-            preferred_element_type=jnp.float32,
-        ),
+        lambda: jnp.einsum("rd,rf->df", act_b, grad_gate_act, preferred_element_type=jnp.float32),
+        lambda: jnp.einsum("rd,rf->df", act_b, grad_up_act, preferred_element_type=jnp.float32),
         lambda: jnp.einsum("rf,rd->df", hidden_act, grad_mlp, preferred_element_type=jnp.float32),
-        lambda: jnp.dot(hidden_act, w_down, preferred_element_type=jnp.float32),
     ]
     filled = []
     state = None
@@ -406,9 +413,7 @@
             filled.append(fillers.pop(0)().astype(jnp.bfloat16))
             state, filled[-1] = tied(state, filled[-1])
     filled.extend(filler().astype(jnp.bfloat16) for filler in fillers)
-    wide_sum = over_tokens(filled[0])
-    down_sum = over_tokens(filled[1])
-    mlp_part = filled[2]
+    gate_sum, up_sum, down_sum = (over_tokens(product) for product in filled)
     normed_share = sum_end(state, slot_part(part_list))
     through_mlp, gain_mlp_part = norm_back(hidden_share, gain_mlp, normed_share)
     res_share = share_of(upstream).astype(jnp.float32) + through_mlp
@@ -416,29 +421,28 @@
     mixed_grad = jnp.einsum(
         "rd,qd->rq", grad_attn_share, full_out, preferred_element_type=jnp.float32
     ).astype(jnp.bfloat16)
-    grad_list = []
-    for head in range(kv_heads):
-        grad_list.append(
-            jnp.concatenate(
-                exchanged(
-                    me,
-                    lambda target: lax.dynamic_slice_in_dim(
-                        mixed_grad,
-                        target * (kv_heads * group_width) + head * group_width,
-                        group_width,
-                        1,
-                    ),
-                    count,
-                ),
-                axis=0,
-            )
-        )
+    grad_mixed = jnp.concatenate(
+        exchanged(
+            me,
+            lambda target: lax.dynamic_slice_in_dim(
+                mixed_grad, target * w_out.shape[0], w_out.shape[0], 1
+            ),
+            count,
+        ),
+        axis=0,
+    )
+    hidden_act, mixed_grad = tied(hidden_act, mixed_grad)
+    mlp_part = jnp.dot(hidden_act, w_down, preferred_element_type=jnp.float32).astype(jnp.bfloat16)
+    grad_mixed, mlp_part = tied(grad_mixed, mlp_part)
     mlp_slots = slot_part(
         [mlp_part[s * share_rows : (s + 1) * share_rows] for s in range(count)]
     )
     pieces = [(head, prompt) for head in range(kv_heads) for prompt in (True, False)]
     upstream_pieces = {
-        (head, prompt): grad_list[head][:own_rows] if prompt else grad_list[head][own_rows:]
+        (head, prompt): grad_mixed[
+            (slice(0, own_rows) if prompt else slice(own_rows, total_rows)),
+            head * group_width : (head + 1) * group_width,
+        ]
         for head, prompt in pieces
     }
     piece_grads = {}
@@ -469,6 +473,8 @@
             moved, piece_grads[pieces[place]], upstream_pieces[following] = tied(
                 moved, piece_grads[pieces[place]], upstream_pieces[following]
             )
+        elif place < len(pieces):
+            moved, piece_grads[pieces[place]] = tied(moved, piece_grads[pieces[place]])
         if place < count - 1:
             forward, backward, *moved = moved
             arrived[-place - 1], arrived[place + 1] = (forward, backward)
@@ -532,7 +538,9 @@
 
     state = None
     forward, backward = hop_step(result_share, result_share, 1, count)
-    forward, backward, input_part, wide_sum = tied(forward, backward, input_part, wide_sum)
+    forward, backward, input_part, gate_sum, up_sum = tied(
+        forward, backward, input_part, gate_sum, up_sum
+    )
     result_arrived = {0: result_share, -1: forward, 1: backward}
     for distance in range(count - 1, 0, -1):
         state = sum_step(state, row_part, distance, count)
@@ -556,19 +564,19 @@
     grad_share = (res_share + through_attn).astype(jnp.bfloat16)
     forward, backward = (grad_share, grad_share)
     arrived = {0: grad_share}
+    gain_parts = jnp.stack([gain_attn_part, gain_mlp_part])
+    stages = pair_stages()
+    per_hop = -(-len(stages) // (count - 1))
     for step in range(1, count):
         forward, backward = hop_step(forward, backward, step, count)
+        for axis, distance in stages[(step - 1) * per_hop : step * per_hop]:
+            gain_parts = pair_sum(gain_parts, axis, distance)
+        forward, backward, gain_parts = tied(forward, backward, gain_parts)
         arrived[-step], arrived[step] = (forward, backward)
     prompt_grad, cont_grad = rows_from(arrived)
-    gain_own = lax.psum(
-        lax.psum_scatter(
-            jnp.stack([gain_attn_part, gain_mlp_part]),
-            ("dp", "ctx"),
-            scatter_dimension=1,
-            tiled=True,
-        ),
-        "tensor",
-    )
+    gain_rows = width // (lax.axis_size("dp") * lax.axis_size("ctx"))
+    gain_place = (lax.axis_index("dp") * lax.axis_size("ctx") + ctx_index) * gain_rows
+    gain_own = lax.dynamic_slice_in_dim(gain_parts, gain_place, gain_rows, 1)
     attn_sum = lax.psum_scatter(
         jnp.concatenate([grad_query, grad_key, grad_value, grad_out], axis=1).astype(jnp.bfloat16),
         ("dp", "ctx"),
@@ -576,7 +584,6 @@
         tiled=True,
     ).astype(jnp.float32)
     qw = grad_query.shape[1]
-    ff = w_gate.shape[1]
     summed = (
         gain_own[0],
         attn_sum[:, :qw],
@@ -584,8 +591,8 @@
         attn_sum[:, qw + key_width : qw + 2 * key_width],
         attn_sum[:, qw + 2 * key_width :].T,
         gain_own[1],
-        wide_sum[:, :ff].astype(jnp.float32),
-        wide_sum[:, ff:].astype(jnp.float32),
+        gate_sum.astype(jnp.float32),
+        up_sum.astype(jnp.float32),
         down_sum.astype(jnp.float32).T,
     )
     return (

time: 864 us -> 769 us (0.89)
  waiting for transfers between devices: 224 us -> 158 us
  matrix products: 271 us -> 257 us
  starting transfers between devices: 122 us -> 135 us
  blocking collectives: 14.4 us -> 2.6 us
  local copies, waits for them, and re-layouts: 59.4 us -> 50.3 us
    unnamed x6 -> x5, waiting for transfers between devices: 35.3 us -> 0.08 us
    ppermute x12, waiting for transfers between devices: 77.3 us -> 48.8 us  [hop_step(): lax.ppermute(backward, 'tensor', [(i, i - 1) for i in range(1, count - st...]
    ppermute x0 -> x5, waiting for transfers between devices: none -> 20.7 us  [pair_sum(): lax.ppermute(values, axis, [(i, i ^ distance) for i in range(lax.axis_siz...]
    ppermute x12 -> x9, waiting for transfers between devices: 24 us -> 6.19 us  [exchanged(): lax.ppermute(send_block(lax.rem(me + shift, count)), 'tensor', [(i, (i +...]
    ppermute x9, waiting for transfers between devices: 38.8 us -> 54 us  [sum_step(): lax.ppermute(to_right, 'tensor', [(i, i + 1) for i in range(0, count - di...]
    psum x1 -> x0, blocking collectives: 11.7 us -> none  [shards(): lax.psum(lax.psum_scatter(jnp.stack([gain_attn_part, gain_mlp_part]), ('d...]
    ppermute x12, waiting for transfers between devices: 28.4 us -> 17.6 us  [hop_step(): lax.ppermute(forward, 'tensor', [(i, i + 1) for i in range(step - 1, coun...]
    ppermute x9, waiting for transfers between devices: 20.3 us -> 10.4 us  [sum_step(): lax.ppermute(to_left, 'tensor', [(i, i - 1) for i in range(distance, coun...]
  transfers between devices with their start and end apart: 60 -> 62, of which waited for: 21 -> 25; matrix products, arithmetic and copies ran while one was open for 44% -> 51% of each run, Pallas kernels for 0% -> 0%
where the time goes in v4:
time: 769 us; the launch traced here: 762 us
  matrix products  257 us (33%)
  waiting for transfers between devices  158 us (21%)
  other arithmetic  141 us (18%)
  starting transfers between devices  135 us (18%)
  local copies, waits for them, and re-layouts  50.3 us (7%)
  between operations  17.5 us (2%)
    ppermute x9, waiting for transfers between devices, sum_step(): lax.ppermute(to_right, 'tensor', [(i, i + 1) for i in range(0, count - di...  54 us
    ppermute x12, waiting for transfers between devices, hop_step(): lax.ppermute(backward, 'tensor', [(i, i - 1) for i in range(1, count - st...  48.8 us
    ppermute x9, starting transfers between devices, sum_step(): lax.ppermute(to_right, 'tensor', [(i, i + 1) for i in range(0, count - di...  45.9 us
    dot_general x4, matrix products, attend_backward(): jnp.einsum('bhgd,khd->hgbk', grad_heads, value_head_rows, preferred_eleme...  33.6 us
    ppermute x12, starting transfers between devices, hop_step(): lax.ppermute(forward, 'tensor', [(i, i + 1) for i in range(step - 1, coun...  32.1 us
    unnamed x290, local copies, waits for them, and re-layouts  27.8 us
    dot_general x4, matrix products, shards(): jnp.einsum('rf,df->rd', grad_up_slot, w_up, preferred_element_type=jnp.fl...  26 us
    convert_element_type x6, other arithmetic, added(): (first.astype(jnp.float32) + second.astype(jnp.float32)).astype(jnp.bfloa...  25.9 us
  transfers between devices with their start and end apart: 62, of which 25 were waited for; matrix products, arithmetic and copies ran while one was open for 51% of the time, Pallas kernels for 0%

profile of v4, /device:TPU:0, one launch (start us, length us, event | category | flops | bytes accessed | tf_op | source)
XLA Modules:
  0.0 761.6 jit_solution(7044443360591161077)
XLA Ops:
  40.6 6.4 fusion.21
  92.8 11.2 %fusion.151 = f32[1024,2048]{1,0:T(8,128)} fusion(bf16[1024,2048]{1,0:T(8,128)(2,1)S(1)} %pad_maximum_fusion.2, bf16[2048,2048]{1,0:T(8,128)(2,1)S(1)} %bitcast.494), kind=kOutput, calls=%fused_computation.362 | convolution fusion | flops 8589934592 | bytes 20971520 | tf_op jit(solution)/shard_map/rd,fd->rf/dot_general | solution.py:352
  117.9 6.4 multiply_reduce_fusion.6
  156.6 6.1 fusion.154
  170.8 6.8 fusion.53
  198.6 6.7 fusion.54
  208.3 6.1 fusion.158
  214.4 6.2 multiply_convert_fusion.3
  223.0 6.8 fusion.55
  234.2 11.2 %convolution_convert_fusion.2 = bf16[2048,2048]{1,0:T(8,128)(2,1)} fusion(bf16[256,2048]{1,0:T(8,128)(2,1)S(1)} %get-tuple-element.126, bf16[256,2048]{1,0:T(8,128)(2,1)S(1)} %copy-done.121, bf16[256,2048]{1,0:T(8,128)(2,1)S(1)} %get-tuple-element.124, bf16[256,2048]{1,0:T(8,128)(2,1)S(1)} %get-tuple-element.123, ...), kind=kOutput, calls=%fused_computation.40 | convolution fusion | flops 8627683328 | bytes 16777216 | tf_op jit(solution)/shard_map/rd,rf->df/dot_general | solution.py:404
  245.4 8.3 %collective-permute-done.12 = bf16[256,2048]{1,0:T(8,128)(2,1)} collective-permute-done((bf16[256,2048]{1,0:T(8,128)(2,1)}, bf16[256,2048]{1,0:T(8,128)(2,1)}, u32[]{:S(2)}, u32[]{:S(2)}) %collective-permute-start.12) | collective-permute-done | bytes 1048608 | tf_op jit(solution)/shard_map/ppermute | solution.py:171
  265.4 12.5 %convolution_convert_fusion.1 = bf16[2048,2048]{1,0:T(8,128)(2,1)} fusion(bf16[256,2048]{1,0:T(8,128)(2,1)} %copy-done.119, bf16[256,2048]{1,0:T(8,128)(2,1)} %copy-done.118, bf16[256,2048]{1,0:T(8,128)(2,1)S(1)} %copy-done.117, bf16[256,2048]{1,0:T(8,128)(2,1)S(1)} %copy-done.115, bf16[256,2048]{1,0:T(8,128)(2,1)S(1)} %copy-done.79, ...), kind=kOutput, calls=%fused_computation.39 | convolution fusion | flops 8627683328 | bytes 16777216 | tf_op jit(solution)/shard_map/rd,rf->df/dot_general | solution.py:405
  295.1 6.1 collective-permute-start.16
  301.2 11.4 %convolution_convert_fusion = bf16[2048,2048]{1,0:T(8,128)(2,1)} fusion(bf16[1024,2048]{1,0:T(8,128)(2,1)S(1)} %copy-done.23, bf16[1024,2048]{1,0:T(8,128)(2,1)S(1)} %constant_dynamic-update-slice_fusion.4), kind=kOutput, calls=%fused_computation.38 | convolution fusion | flops 8594128896 | bytes 16777216 | tf_op jit(solution)/shard_map/rf,rd->df/dot_general | solution.py:406
  340.9 10.4 %convolution_convert_fusion.3 = bf16[1024,2048]{1,0:T(8,128)(2,1)} fusion(bf16[1024,2048]{1,0:T(8,128)(2,1)S(1)} %copy-done.96, bf16[2048,2048]{1,0:T(8,128)(2,1)S(1)} %bitcast.496), kind=kOutput, calls=%fused_computation.82 | convolution fusion | flops 8592031744 | bytes 16777216 | tf_op jit(solution)/shard_map/dot_general | solution.py:435
  358.7 8.1 %collective-permute-start.25 = (bf16[256,2048]{1,0:T(8,128)(2,1)}, bf16[256,2048]{1,0:T(8,128)(2,1)}, u32[]{:S(2)}, u32[]{:S(2)}) collective-permute-start(bf16[256,2048]{1,0:T(8,128)(2,1)} %slice.221), channel_id=1, source_target_pairs={{0,1},{4,5},{8,9},{12,13},{16,17},{20,21},{24,25},{28,29}} | collective-permute-start | bytes 3145736 | tf_op jit(solution)/shard_map/ppermute | solution.py:171
  394.1 16.4 %collective-permute-done.21 = bf16[256,2048]{1,0:T(8,128)(2,1)} collective-permute-done((bf16[256,2048]{1,0:T(8,128)(2,1)}, bf16[256,2048]{1,0:T(8,128)(2,1)}, u32[]{:S(2)}, u32[]{:S(2)}) %collective-permute-start.21) | collective-permute-done | bytes 1048608 | tf_op jit(solution)/shard_map/ppermute | solution.py:155
  415.7 11.7 %fusion.3 = (f32[4,512]{1,0:T(4,128)S(1)}, f32[1536,512,4]{1,0,2:T(8,128)}) fusion(f32[1,4,512,1536]{2,3,1,0:T(8,128)} %copy-done.2, f32[4,512]{1,0:T(4,128)S(1)} %copy-done.100, bf16[512,4,64]{0,2,1:T(8,128)(2,1)} %bitcast.452, bf16[512,128]{1,0:T(8,128)(2,1)S(1)} %copy-done.26, bf16[1024,128]{1,0:T(8,128)(2,1)S(1)} %copy-done.21), kind=kOutput, calls=%fused_computation.9 | convolution fusion | flops 412481536 | bytes 25837568 | tf_op jit(solution)/shard_map/bhgd,khd->hgbk/dot_general | solution.py:95
  430.5 7.1 fusion.18
  478.0 6.3 collective-permute-done.28
  494.7 10.7 %fusion = (f32[4,512]{1,0:T(4,128)S(1)}, f32[1536,512,4]{1,0,2:T(8,128)}) fusion(f32[1,4,512,1536]{2,3,1,0:T(8,128)} %copy-done.1, f32[4,512]{1,0:T(4,128)S(1)} %copy-done.98, bf16[512,4,64]{0,2,1:T(8,128)(2,1)S(1)} %bitcast.450, bf16[512,128]{1,0:T(8,128)(2,1)S(1)} %copy-done.26, bf16[1024,128]{1,0:T(8,128)(2,1)S(1)} %copy-done.21), kind=kOutput, calls=%fused_computation.4 | convolution fusion | flops 412481536 | bytes 25837568 | tf_op jit(solution)/shard_map/bhgd,khd->hgbk/dot_general | solution.py:95
  507.3 6.8 fusion.19
  542.7 10.4 %pad_maximum_fusion = bf16[2048,1280]{0,1:T(8,128)(2,1)} fusion(bf16[2048,512]{0,1:T(8,128)(2,1)S(1)} %fusion.48, bf16[2048,128]{0,1:T(8,128)(2,1)S(1)} %convolution_convert_fusion.6, bf16[2048,128]{0,1:T(8,128)(2,1)S(1)} %convolution_convert_fusion.7, bf16[2048,512]{0,1:T(8,128)(2,1)S(1)} %convolution_convert_fusion.4), kind=kLoop, calls=%fused_computation.47 | loop fusion | flops 20971520 | bytes 10485760 | tf_op jit(solution)/shard_map/concatenate | solution.py:581
  574.9 14.8 %collective-permute-done.39 = bf16[256,2048]{1,0:T(8,128)(2,1)} collective-permute-done((bf16[256,2048]{1,0:T(8,128)(2,1)}, bf16[256,2048]{1,0:T(8,128)(2,1)}, u32[]{:S(2)}, u32[]{:S(2)}) %collective-permute-start.39) | collective-permute-done | bytes 1048608 | tf_op jit(solution)/shard_map/ppermute | solution.py:156
  589.8 6.0 collective-permute-done.36
  610.2 16.7 %collective-permute-done.40 = bf16[256,2048]{1,0:T(8,128)(2,1)} collective-permute-done((bf16[256,2048]{1,0:T(8,128)(2,1)}, bf16[256,2048]{1,0:T(8,128)(2,1)}, u32[]{:S(2)}, u32[]{:S(2)}) %collective-permute-start.40) | collective-permute-done | bytes 1048608 | tf_op jit(solution)/shard_map/ppermute | solution.py:171
  626.9 6.8 collective-permute-done.43
  643.9 15.2 %collective-permute-done.44 = bf16[256,2048]{1,0:T(8,128)(2,1)} collective-permute-done((bf16[256,2048]{1,0:T(8,128)(2,1)}, bf16[256,2048]{1,0:T(8,128)(2,1)}, u32[]{:S(2)}, u32[]{:S(2)}) %collective-permute-start.44) | collective-permute-done | bytes 1048608 | tf_op jit(solution)/shard_map/ppermute | solution.py:171
  687.1 9.3 %collective-permute-done.49 = f32[2,2048]{1,0:T(2,128)S(1)} collective-permute-done((f32[2,2048]{1,0:T(2,128)S(1)}, f32[2,2048]{1,0:T(2,128)S(1)}, u32[]{:S(2)}, u32[]{:S(2)}) %collective-permute-start.49) | collective-permute-done | bytes 16416 | tf_op jit(solution)/shard_map/ppermute | solution.py:207
  700.3 7.2 collective-permute-start.52
  713.7 10.0 %collective-permute-done.52 = f32[2,2048]{1,0:T(2,128)S(1)} collective-permute-done((f32[2,2048]{1,0:T(2,128)S(1)}, f32[2,2048]{1,0:T(2,128)S(1)}, u32[]{:S(2)}, u32[]{:S(2)}) %collective-permute-start.52) | collective-permute-done | bytes 16416 | tf_op jit(solution)/shard_map/ppermute | solution.py:207
  738.3 9.7 %collective-permute-done.55 = bf16[256,2048]{1,0:T(8,128)(2,1)} collective-permute-done((bf16[256,2048]{1,0:T(8,128)(2,1)}, bf16[256,2048]{1,0:T(8,128)(2,1)}, u32[]{:S(2)}, u32[]{:S(2)}) %collective-permute-start.55) | collective-permute-done | bytes 1048608 | tf_op jit(solution)/shard_map/ppermute | solution.py:156
  (576 shorter events, 448.3 us)
Async XLA Ops:
  7.2 110.7 %all-gather.2.cloned.1.call-start = ((), (), s32[]{:S(2)}) async-start(), calls=%async_computation.4 | async-start | bytes 9437184 | tf_op jit(solution)/shard_map/all_gather | solution.py:277
  9.7 551.8 %reduce-scatter.5.cloned.1.call-start = ((), (), s32[]{:S(2)}) async-start(), calls=%async_computation.5 | async-start | bytes 9437184 | tf_op jit(solution)/shard_map/reduce_scatter | solution.py:399
  59.8 48.3 %collective-permute-start.5 = (bf16[256,256]{0,1:T(8,128)(2,1)}, bf16[256,256]{0,1:T(8,128)(2,1)}, u32[]{:S(2)}, u32[]{:S(2)}) collective-permute-start(bf16[256,256]{0,1:T(8,128)(2,1)} %get-tuple-element.314), channel_id=1, source_target_pairs={{0,1},{1,2},{2,3},{3,0},{4,5},{5,6},{6,7},{7,4},{8,9},{9,10},{10,1... | collective-permute-start | bytes 393224 | tf_op jit(solution)/shard_map/ppermute | solution.py:187
  62.8 45.6 %collective-permute-start.3 = (bf16[256,256]{0,1:T(8,128)(2,1)}, bf16[256,256]{0,1:T(8,128)(2,1)}, u32[]{:S(2)}, u32[]{:S(2)}) collective-permute-start(bf16[256,256]{0,1:T(8,128)(2,1)} %get-tuple-element.315), channel_id=1, source_target_pairs={{0,3},{1,0},{2,1},{3,2},{4,7},{5,4},{6,5},{7,6},{8,11},{9,8},{10,9... | collective-permute-start | bytes 393224 | tf_op jit(solution)/shard_map/ppermute | solution.py:187
  64.9 43.5 %collective-permute-start.4 = (bf16[256,256]{0,1:T(8,128)(2,1)}, bf16[256,256]{0,1:T(8,128)(2,1)}, u32[]{:S(2)}, u32[]{:S(2)}) collective-permute-start(bf16[256,256]{0,1:T(8,128)(2,1)} %get-tuple-element.316), channel_id=1, source_target_pairs={{0,2},{1,3},{2,0},{3,1},{4,6},{5,7},{6,4},{7,5},{8,10},{9,11},{10,... | collective-permute-start | bytes 393224 | tf_op jit(solution)/shard_map/ppermute | solution.py:187
  81.4 29.1 %collective-permute-start.2 = (bf16[256,256]{0,1:T(8,128)(2,1)S(1)}, bf16[256,256]{0,1:T(8,128)(2,1)S(1)}, u32[]{:S(2)}, u32[]{:S(2)}) collective-permute-start(bf16[256,256]{0,1:T(8,128)(2,1)S(1)} %get-tuple-element.317), channel_id=1, source_target_pairs={{0,1},{1,2},{2,3},{3,0},{4,5},{5,6},{6,7},{7,4},{8,9},{9,10},{10,1... | collective-permute-start | bytes 393224 | tf_op jit(solution)/shard_map/ppermute | solution.py:187
  83.0 27.5 %collective-permute-start = (bf16[256,256]{0,1:T(8,128)(2,1)S(1)}, bf16[256,256]{0,1:T(8,128)(2,1)S(1)}, u32[]{:S(2)}, u32[]{:S(2)}) collective-permute-start(bf16[256,256]{0,1:T(8,128)(2,1)S(1)} %get-tuple-element.318), channel_id=1, source_target_pairs={{0,3},{1,0},{2,1},{3,2},{4,7},{5,4},{6,5},{7,6},{8,11},{9,8},{10,9... | collective-permute-start | bytes 393224 | tf_op jit(solution)/shard_map/ppermute | solution.py:187
  125.9 26.8 %collective-permute-start.7 = (bf16[256,2048]{1,0:T(8,128)(2,1)S(1)}, bf16[256,2048]{1,0:T(8,128)(2,1)S(1)}, u32[]{:S(2)}, u32[]{:S(2)}) collective-permute-start(bf16[256,2048]{1,0:T(8,128)(2,1)S(1)} %multiply_convert_fusion.15), channel_id=1, source_target_pairs={{1,0},{2,1},{3,2},{5,4},{6,5},{7,6},{9,8},{10,9},{11,10},{13,12},{... | collective-permute-start | bytes 3145736 | tf_op jit(solution)/shard_map/ppermute | solution.py:156
  127.5 26.4 %collective-permute-start.6 = (bf16[256,2048]{1,0:T(8,128)(2,1)S(1)}, bf16[256,2048]{1,0:T(8,128)(2,1)S(1)}, u32[]{:S(2)}, u32[]{:S(2)}) collective-permute-start(bf16[256,2048]{1,0:T(8,128)(2,1)S(1)} %multiply_convert_fusion.15), channel_id=1, source_target_pairs={{0,1},{1,2},{2,3},{4,5},{5,6},{6,7},{8,9},{9,10},{10,11},{12,13},{... | collective-permute-start | bytes 3145736 | tf_op jit(solution)/shard_map/ppermute | solution.py:155
  154.7 27.7 %collective-permute-start.9 = (bf16[256,2048]{1,0:T(8,128)(2,1)S(1)}, bf16[256,2048]{1,0:T(8,128)(2,1)S(1)}, u32[]{:S(2)}, u32[]{:S(2)}) collective-permute-start(bf16[256,2048]{1,0:T(8,128)(2,1)S(1)} %collective-permute-done.7), channel_id=1, source_target_pairs={{1,0},{2,1},{5,4},{6,5},{9,8},{10,9},{13,12},{14,13},{17,16},{18,1... | collective-permute-start | bytes 3145736 | tf_op jit(solution)/shard_map/ppermute | solution.py:156
  183.3 24.8 %collective-permute-start.11 = (bf16[256,2048]{1,0:T(8,128)(2,1)S(1)}, bf16[256,2048]{1,0:T(8,128)(2,1)S(1)}, u32[]{:S(2)}, u32[]{:S(2)}) collective-permute-start(bf16[256,2048]{1,0:T(8,128)(2,1)S(1)} %collective-permute-done.9), channel_id=1, source_target_pairs={{1,0},{5,4},{9,8},{13,12},{17,16},{21,20},{25,24},{29,28}} | collective-permute-start | bytes 3145736 | tf_op jit(solution)/shard_map/ppermute | solution.py:156
  253.7 307.8 %reduce-scatter.7.cloned.1.call-start = ((), (), s32[]{:S(2)}) async-start(), calls=%async_computation.6 | async-start | bytes 9437184 | tf_op jit(solution)/shard_map/reduce_scatter | solution.py:399
  283.8 291.1 %reduce-scatter.9.cloned.1.call-start = ((), (), s32[]{:S(2)}) async-start(), calls=%async_computation.7 | async-start | bytes 9437184 | tf_op jit(solution)/shard_map/reduce_scatter | solution.py:399
  351.3 334.7 %reduce-scatter.11.cloned.1.call-start = ((), (), s32[]{:S(2)}) async-start(), calls=%async_computation.8 | async-start | bytes 5898240 | tf_op jit(solution)/shard_map/reduce_scatter | solution.py:580
  357.0 88.1 %collective-permute-start.26 = (bf16[256,2048]{1,0:T(8,128)(2,1)}, bf16[256,2048]{1,0:T(8,128)(2,1)}, u32[]{:S(2)}, u32[]{:S(2)}) collective-permute-start(bf16[256,2048]{1,0:T(8,128)(2,1)} %slice.221), channel_id=1, source_target_pairs={{3,2},{7,6},{11,10},{15,14},{19,18},{23,22},{27,26},{31,30}} | collective-permute-start | bytes 3145736 | tf_op jit(solution)/shard_map/ppermute | solution.py:172
  358.7 86.4 %collective-permute-start.25 = (bf16[256,2048]{1,0:T(8,128)(2,1)}, bf16[256,2048]{1,0:T(8,128)(2,1)}, u32[]{:S(2)}, u32[]{:S(2)}) collective-permute-start(bf16[256,2048]{1,0:T(8,128)(2,1)} %slice.221), channel_id=1, source_target_pairs={{0,1},{4,5},{8,9},{12,13},{16,17},{20,21},{24,25},{28,29}} | collective-permute-start | bytes 3145736 | tf_op jit(solution)/shard_map/ppermute | solution.py:171
  367.8 26.3 %collective-permute-start.22 = (bf16[256,2048]{1,0:T(8,128)(2,1)}, bf16[256,2048]{1,0:T(8,128)(2,1)}, u32[]{:S(2)}, u32[]{:S(2)}) collective-permute-start(bf16[256,2048]{1,0:T(8,128)(2,1)} %get-tuple-element.144), channel_id=1, source_target_pairs={{1,0},{2,1},{3,2},{5,4},{6,5},{7,6},{9,8},{10,9},{11,10},{13,12},{... | collective-permute-start | bytes 3145736 | tf_op jit(solution)/shard_map/ppermute | solution.py:156
  369.1 41.4 %collective-permute-start.21 = (bf16[256,2048]{1,0:T(8,128)(2,1)}, bf16[256,2048]{1,0:T(8,128)(2,1)}, u32[]{:S(2)}, u32[]{:S(2)}) collective-permute-start(bf16[256,2048]{1,0:T(8,128)(2,1)} %get-tuple-element.144), channel_id=1, source_target_pairs={{0,1},{1,2},{2,3},{4,5},{5,6},{6,7},{8,9},{9,10},{10,11},{12,13},{... | collective-permute-start | bytes 3145736 | tf_op jit(solution)/shard_map/ppermute | solution.py:155
  412.3 32.8 %collective-permute-start.23 = (bf16[256,2048]{1,0:T(8,128)(2,1)}, bf16[256,2048]{1,0:T(8,128)(2,1)}, u32[]{:S(2)}, u32[]{:S(2)}) collective-permute-start(bf16[256,2048]{1,0:T(8,128)(2,1)} %collective-permute-done.21), channel_id=1, source_target_pairs={{1,2},{2,3},{5,6},{6,7},{9,10},{10,11},{13,14},{14,15},{17,18},{18... | collective-permute-start | bytes 3145736 | tf_op jit(solution)/shard_map/ppermute | solution.py:155
  414.0 31.2 %collective-permute-start.24 = (bf16[256,2048]{1,0:T(8,128)(2,1)}, bf16[256,2048]{1,0:T(8,128)(2,1)}, u32[]{:S(2)}, u32[]{:S(2)}) collective-permute-start(bf16[256,2048]{1,0:T(8,128)(2,1)} %collective-permute-done.22), channel_id=1, source_target_pairs={{1,0},{2,1},{5,4},{6,5},{9,8},{10,9},{13,12},{14,13},{17,16},{18,1... | collective-permute-start | bytes 3145736 | tf_op jit(solution)/shard_map/ppermute | solution.py:156
  450.1 27.3 %collective-permute-start.30 = (bf16[256,2048]{1,0:T(8,128)(2,1)S(1)}, bf16[256,2048]{1,0:T(8,128)(2,1)S(1)}, u32[]{:S(2)}, u32[]{:S(2)}) collective-permute-start(bf16[256,2048]{1,0:T(8,128)(2,1)S(1)} %get-tuple-element.261), channel_id=1, source_target_pairs={{2,1},{3,2},{6,5},{7,6},{10,9},{11,10},{14,13},{15,14},{18,17},{19... | collective-permute-start | bytes 3145736 | tf_op jit(solution)/shard_map/ppermute | solution.py:172
  450.9 27.1 %collective-permute-start.29 = (bf16[256,2048]{1,0:T(8,128)(2,1)S(1)}, bf16[256,2048]{1,0:T(8,128)(2,1)S(1)}, u32[]{:S(2)}, u32[]{:S(2)}) collective-permute-start(bf16[256,2048]{1,0:T(8,128)(2,1)S(1)} %get-tuple-element.262), channel_id=1, source_target_pairs={{0,1},{1,2},{4,5},{5,6},{8,9},{9,10},{12,13},{13,14},{16,17},{17,1... | collective-permute-start | bytes 3145736 | tf_op jit(solution)/shard_map/ppermute | solution.py:171
  457.8 26.6 %collective-permute-start.28 = (bf16[256,2048]{1,0:T(8,128)(2,1)}, bf16[256,2048]{1,0:T(8,128)(2,1)}, u32[]{:S(2)}, u32[]{:S(2)}) collective-permute-start(bf16[256,2048]{1,0:T(8,128)(2,1)} %collective-permute-done.24), channel_id=1, source_target_pairs={{1,0},{5,4},{9,8},{13,12},{17,16},{21,20},{25,24},{29,28}} | collective-permute-start | bytes 3145736 | tf_op jit(solution)/shard_map/ppermute | solution.py:156
  487.6 38.4 %collective-permute-start.32 = (bf16[256,2048]{1,0:T(8,128)(2,1)S(1)}, bf16[256,2048]{1,0:T(8,128)(2,1)S(1)}, u32[]{:S(2)}, u32[]{:S(2)}) collective-permute-start(bf16[256,2048]{1,0:T(8,128)(2,1)S(1)} %get-tuple-element.259), channel_id=1, source_target_pairs={{1,0},{2,1},{3,2},{5,4},{6,5},{7,6},{9,8},{10,9},{11,10},{13,12},{... | collective-permute-start | bytes 3145736 | tf_op jit(solution)/shard_map/ppermute | solution.py:172
  488.9 37.1 %collective-permute-start.31 = (bf16[256,2048]{1,0:T(8,128)(2,1)S(1)}, bf16[256,2048]{1,0:T(8,128)(2,1)}, u32[]{:S(2)}, u32[]{:S(2)}) collective-permute-start(bf16[256,2048]{1,0:T(8,128)(2,1)S(1)} %get-tuple-element.260), channel_id=1, source_target_pairs={{0,1},{1,2},{2,3},{4,5},{5,6},{6,7},{8,9},{9,10},{10,11},{12,13},{... | collective-permute-start | bytes 3145736 | tf_op jit(solution)/shard_map/ppermute | solution.py:171
  528.4 33.2 %collective-permute-start.34 = (bf16[256,2048]{1,0:T(8,128)(2,1)S(1)}, bf16[256,2048]{1,0:T(8,128)(2,1)}, u32[]{:S(2)}, u32[]{:S(2)}) collective-permute-start(bf16[256,2048]{1,0:T(8,128)(2,1)S(1)} %add_convert_fusion.6), channel_id=1, source_target_pairs={{1,0},{2,1},{3,2},{5,4},{6,5},{7,6},{9,8},{10,9},{11,10},{13,12},{... | collective-permute-start | bytes 3145736 | tf_op jit(solution)/shard_map/ppermute | solution.py:156
  529.8 31.7 %collective-permute-start.33 = (bf16[256,2048]{1,0:T(8,128)(2,1)S(1)}, bf16[256,2048]{1,0:T(8,128)(2,1)}, u32[]{:S(2)}, u32[]{:S(2)}) collective-permute-start(bf16[256,2048]{1,0:T(8,128)(2,1)S(1)} %add_convert_fusion.6), channel_id=1, source_target_pairs={{0,1},{1,2},{2,3},{4,5},{5,6},{6,7},{8,9},{9,10},{10,11},{12,13},{... | collective-permute-start | bytes 3145736 | tf_op jit(solution)/shard_map/ppermute | solution.py:155
  563.2 26.5 %collective-permute-start.39 = (bf16[256,2048]{1,0:T(8,128)(2,1)}, bf16[256,2048]{1,0:T(8,128)(2,1)}, u32[]{:S(2)}, u32[]{:S(2)}) collective-permute-start(bf16[256,2048]{1,0:T(8,128)(2,1)} %collective-permute-done.34), channel_id=1, source_target_pairs={{1,0},{2,1},{5,4},{6,5},{9,8},{10,9},{13,12},{14,13},{17,16},{18,1... | collective-permute-start | bytes 3145736 | tf_op jit(solution)/shard_map/ppermute | solution.py:156
  569.4 26.4 %collective-permute-start.36 = (bf16[256,2048]{1,0:T(8,128)(2,1)}, bf16[256,2048]{1,0:T(8,128)(2,1)}, u32[]{:S(2)}, u32[]{:S(2)}) collective-permute-start(bf16[256,2048]{1,0:T(8,128)(2,1)} %get-tuple-element.258), channel_id=1, source_target_pairs={{0,1},{4,5},{8,9},{12,13},{16,17},{20,21},{24,25},{28,29}} | collective-permute-start | bytes 3145736 | tf_op jit(solution)/shard_map/ppermute | solution.py:171
  608.9 24.8 %collective-permute-start.43 = (bf16[256,2048]{1,0:T(8,128)(2,1)}, bf16[256,2048]{1,0:T(8,128)(2,1)}, u32[]{:S(2)}, u32[]{:S(2)}) collective-permute-start(bf16[256,2048]{1,0:T(8,128)(2,1)} %collective-permute-done.39), channel_id=1, source_target_pairs={{1,0},{5,4},{9,8},{13,12},{17,16},{21,20},{25,24},{29,28}} | collective-permute-start | bytes 3145736 | tf_op jit(solution)/shard_map/ppermute | solution.py:156
  696.5 31.0 %collective-permute-start.50 = (bf16[256,2048]{1,0:T(8,128)(2,1)}, bf16[256,2048]{1,0:T(8,128)(2,1)}, u32[]{:S(2)}, u32[]{:S(2)}) collective-permute-start(bf16[256,2048]{1,0:T(8,128)(2,1)} %collective-permute-done.46), channel_id=1, source_target_pairs={{1,2},{2,3},{5,6},{6,7},{9,10},{10,11},{13,14},{14,15},{17,18},{18... | collective-permute-start | bytes 3145736 | tf_op jit(solution)/shard_map/ppermute | solution.py:155
  698.2 29.4 %collective-permute-start.51 = (bf16[256,2048]{1,0:T(8,128)(2,1)}, bf16[256,2048]{1,0:T(8,128)(2,1)}, u32[]{:S(2)}, u32[]{:S(2)}) collective-permute-start(bf16[256,2048]{1,0:T(8,128)(2,1)} %collective-permute-done.47), channel_id=1, source_target_pairs={{1,0},{2,1},{5,4},{6,5},{9,8},{10,9},{13,12},{14,13},{17,16},{18,1... | collective-permute-start | bytes 3145736 | tf_op jit(solution)/shard_map/ppermute | solution.py:156
  (170 other events, 2128.6 us)
Sparse Core Ops, SparseCore 0:
  10.2 103.0 all-gather.1
  253.9 71.1 reduce-scatter.4
  328.5 71.4 reduce-scatter.6
  403.4 71.4 reduce-scatter.8
  553.3 54.1 reduce-scatter.10

commit v5 on v4

--- a/solution.py
+++ b/solution.py
@@ -5,6 +5,8 @@
 import jax
 import jax.numpy as jnp
 from jax import lax
+from jax.experimental import pallas as pl
+from jax.experimental.pallas import tpu as pltpu
 from jax.sharding import PartitionSpec as P
 
 QUERY_HEADS = 32
@@ -41,83 +43,198 @@
 
 
 def rotate(inputs, cos_table, sin_table):
-    halves = inputs.reshape(inputs.shape[0], -1, 2, HEAD_WIDTH // 2)
-    first_half = halves[:, :, 0]
-    second_half = halves[:, :, 1]
-    cos_rows = cos_table[:, None, :]
-    sin_rows = sin_table[:, None, :]
+    rows = inputs.shape[1]
+    halves = inputs.reshape(-1, 2, HEAD_WIDTH // 2, rows)
+    first_half = halves[:, 0]
+    second_half = halves[:, 1]
     turned = jnp.stack(
         [
-            first_half * cos_rows - second_half * sin_rows,
-            second_half * cos_rows + first_half * sin_rows,
+            first_half * cos_table[None] - second_half * sin_table[None],
+            second_half * cos_table[None] + first_half * sin_table[None],
         ],
-        axis=2,
+        axis=1,
     )
     return turned.reshape(inputs.shape)
 
 
-def score_block(query_rows, joined_keys, allowed):
-    query_total = query_rows.shape[0]
-    key_total = joined_keys.shape[0]
-    key_value_heads = joined_keys.shape[1] // HEAD_WIDTH
-    query_head_rows = query_rows.reshape(
-        query_total, key_value_heads, QUERY_HEADS // KEY_VALUE_HEADS, HEAD_WIDTH
-    )
-    key_head_rows = joined_keys.reshape(key_total, key_value_heads, HEAD_WIDTH)
-    scores = (
-        jnp.einsum(
-            "bhgd,khd->hgbk", query_head_rows, key_head_rows, preferred_element_type=jnp.float32
-        )
-        * score_scale
-    )
-    return (jnp.where(allowed[None, None], scores, masked_score), query_head_rows, key_head_rows)
-
-
-def attend_forward(query_rows, joined_keys, joined_values, allowed):
-    scores, query_head_rows, key_head_rows = score_block(query_rows, joined_keys, allowed)
-    highest_score = jnp.max(scores, axis=-1, keepdims=True)
-    log_total = highest_score + jnp.log(
-        jnp.sum(jnp.exp(scores - highest_score), axis=-1, keepdims=True)
-    )
-    weights = jnp.exp(scores - log_total).astype(jnp.bfloat16)
-    value_head_rows = joined_values.reshape(key_head_rows.shape)
-    mixed_heads = jnp.einsum(
-        "hgbk,khd->bhgd", weights, value_head_rows, preferred_element_type=jnp.float32
-    )
-    return (mixed_heads.reshape(query_rows.shape[0], -1), log_total)
-
-
-def attend_backward(query_rows, joined_keys, joined_values, allowed, log_total, upstream):
-    scores, query_head_rows, key_head_rows = score_block(query_rows, joined_keys, allowed)
-    weights = jnp.exp(scores - log_total)
-    value_head_rows = joined_values.reshape(key_head_rows.shape)
-    grad_heads = upstream.reshape(query_head_rows.shape)
-    grad_weights = jnp.einsum(
-        "bhgd,khd->hgbk", grad_heads, value_head_rows, preferred_element_type=jnp.float32
-    )
-    grad_scores = (
-        weights * (grad_weights - jnp.sum(grad_weights * weights, axis=-1, keepdims=True))
-    ).astype(jnp.bfloat16)
-    grad_query = (
-        jnp.einsum("hgbk,khd->bhgd", grad_scores, key_head_rows, preferred_element_type=jnp.float32)
-        * score_scale
-    )
-    grad_key = (
-        jnp.einsum(
-            "hgbk,bhgd->khd", grad_scores, query_head_rows, preferred_element_type=jnp.float32
-        )
-        * score_scale
-    )
-    grad_value = jnp.einsum(
-        "hgbk,bhgd->khd",
-        weights.astype(jnp.bfloat16),
-        grad_heads,
-        preferred_element_type=jnp.float32,
-    )
-    return (
-        grad_query.reshape(query_rows.shape[0], -1),
-        grad_key.reshape(joined_keys.shape[0], -1),
-        grad_value.reshape(joined_keys.shape[0], -1),
+HEAD_GROUP = QUERY_HEADS // KEY_VALUE_HEADS
+BLOCK = CONT_LENGTH
+
+
+def lanes_from_heads(block):
+    return jnp.concatenate(
+        [block[g * HEAD_WIDTH : (g + 1) * HEAD_WIDTH] for g in range(HEAD_GROUP)], axis=1
+    )
+
+
+def heads_from_lanes(block):
+    return jnp.concatenate(
+        [block[:, g * BLOCK : (g + 1) * BLOCK] for g in range(HEAD_GROUP)], axis=0
+    )
+
+
+def inner(first, second):
+    return jnp.dot(first, second, preferred_element_type=jnp.float32)
+
+
+def across(first, second):
+    return lax.dot_general(
+        first, second, (((1,), (1,)), ((), ())), preferred_element_type=jnp.float32
+    )
+
+
+def scaled_queries(query_ref):
+    return lanes_from_heads(query_ref[...].astype(jnp.float32) * score_scale).astype(jnp.bfloat16)
+
+
+def block_scores(meta_ref, keys, own_keys, queries):
+    lanes = HEAD_GROUP * BLOCK
+    scores = inner(keys, queries)
+    place = lax.broadcasted_iota(jnp.int32, scores.shape, 0)
+    if own_keys is None:
+        row = lax.broadcasted_iota(jnp.int32, (1, lanes), 1) % BLOCK
+        limit = jnp.minimum(row + (meta_ref[1] + pl.program_id(0) * BLOCK + 1), meta_ref[0])
+        return [jnp.where(place < limit, scores, masked_score)]
+    own = inner(own_keys, queries)
+    own_place = lax.broadcasted_iota(jnp.int32, own.shape, 0)
+    own_row = lax.broadcasted_iota(jnp.int32, own.shape, 1) % BLOCK
+    return [
+        jnp.where(place < meta_ref[0], scores, masked_score),
+        jnp.where(own_place <= own_row, own, masked_score),
+    ]
+
+
+def forward_kernel(meta_ref, query_ref, *refs):
+    *key_refs, mixed_ref, total_ref = refs
+    keys, values_t = key_refs[:2]
+    own_keys, own_values_t = key_refs[2:] if len(key_refs) > 2 else (None, None)
+    queries = scaled_queries(query_ref)
+    parts = block_scores(
+        meta_ref, keys[...], None if own_keys is None else own_keys[...], queries
+    )
+    highest = functools.reduce(
+        jnp.maximum, [jnp.max(part, axis=0, keepdims=True) for part in parts]
+    )
+    weights = [jnp.exp(part - highest) for part in parts]
+    total = sum(jnp.sum(weight, axis=0, keepdims=True) for weight in weights)
+    mixed = sum(
+        inner(ref[...], weight.astype(jnp.bfloat16))
+        for ref, weight in zip((values_t, own_values_t), weights)
+    )
+    mixed_ref[...] = heads_from_lanes(mixed * (1.0 / total)).astype(jnp.bfloat16)
+    total_ref[0] = highest + jnp.log(total)
+
+
+def backward_kernel(meta_ref, query_ref, grad_ref, total_ref, *refs):
+    own = len(refs) > 6
+    keys, keys_t, values = refs[:3]
+    own_keys, own_keys_t, own_values = refs[3:6] if own else (None, None, None)
+    query_out, key_out, value_out, *own_out = refs[6:] if own else refs[3:]
+    queries = scaled_queries(query_ref)
+    grads = lanes_from_heads(grad_ref[...].astype(jnp.float32)).astype(jnp.bfloat16)
+    parts = block_scores(meta_ref, keys[...], own_keys[...] if own else None, queries)
+    weights = [jnp.exp(part - total_ref[0]) for part in parts]
+    grad_weights = [inner(ref[...], grads) for ref, _ in zip((values, own_values), parts)]
+    mean = sum(
+        jnp.sum(weight * grad, axis=0, keepdims=True)
+        for weight, grad in zip(weights, grad_weights)
+    )
+    grad_scores = [
+        (weight * (grad - mean)).astype(jnp.bfloat16)
+        for weight, grad in zip(weights, grad_weights)
+    ]
+    query_grad = sum(inner(ref[...], part) for ref, part in zip((keys_t, own_keys_t), grad_scores))
+    query_out[...] = heads_from_lanes(query_grad * score_scale)
+
+    @pl.when(pl.program_id(0) == 0)
+    def _():
+        key_out[...] = jnp.zeros_like(key_out)
+        value_out[...] = jnp.zeros_like(value_out)
+
+    key_out[...] += across(grad_scores[0], queries)
+    value_out[...] += across(weights[0].astype(jnp.bfloat16), grads)
+    if own:
+        own_out[0][...] = across(grad_scores[1], queries)
+        own_out[1][...] = across(weights[1].astype(jnp.bfloat16), grads)
+
+
+def attention_call(kernel, meta, moving, keys, own, outs, products):
+    rows = moving[0].shape[1]
+    lanes = HEAD_GROUP * BLOCK
+    tall = HEAD_GROUP * HEAD_WIDTH
+    kinds = {
+        "rows": pl.BlockSpec((tall, BLOCK), lambda i, meta: (0, i)),
+        "total": pl.BlockSpec((1, 1, lanes), lambda i, meta: (i, 0, 0)),
+        "own": pl.BlockSpec((BLOCK, HEAD_WIDTH), lambda i, meta: (i, 0)),
+        "own_t": pl.BlockSpec((HEAD_WIDTH, BLOCK), lambda i, meta: (0, i)),
+    }
+
+    def whole(shape):
+        return pl.BlockSpec(shape, lambda i, meta: (0, 0))
+
+    in_specs = [kinds["total"] if array.ndim == 3 else kinds["rows"] for array in moving]
+    in_specs += [whole(array.shape) for array in keys]
+    in_specs += [kinds["own" if array.shape[1] == HEAD_WIDTH else "own_t"] for array in own]
+    out_specs = [
+        whole(out.shape) if kind == "whole" else kinds[kind] for kind, out in outs
+    ]
+    key_total = keys[0].shape[0] + (BLOCK if own else 0)
+    work = HEAD_GROUP * rows * key_total
+    return pl.pallas_call(
+        kernel,
+        out_shape=[out for _, out in outs],
+        grid_spec=pltpu.PrefetchScalarGridSpec(
+            num_scalar_prefetch=1,
+            grid=(rows // BLOCK,),
+            in_specs=in_specs,
+            out_specs=out_specs,
+        ),
+        compiler_params=pltpu.CompilerParams(
+            dimension_semantics=("arbitrary",), vmem_limit_bytes=40 * 1024 * 1024
+        ),
+        cost_estimate=pl.CostEstimate(
+            flops=2 * products * work * HEAD_WIDTH,
+            bytes_accessed=2 * (sum(array.size for array in moving) + 4 * keys[0].size),
+            transcendentals=work,
+        ),
+    )(meta, *moving, *keys, *own)
+
+
+def attend_forward(meta, queries, keys, values, own_keys, own_values):
+    rows = queries.shape[1]
+    own = [] if own_keys is None else [own_keys, own_values.T]
+    return attention_call(
+        forward_kernel,
+        meta,
+        [queries],
+        [keys, values.T],
+        own,
+        [
+            ("rows", jax.ShapeDtypeStruct(queries.shape, jnp.bfloat16)),
+            (
+                "total",
+                jax.ShapeDtypeStruct((rows // BLOCK, 1, HEAD_GROUP * BLOCK), jnp.float32),
+            ),
+        ],
+        2,
+    )
+
+
+def attend_backward(meta, queries, keys, values, own_keys, own_values, totals, upstream):
+    own = [] if own_keys is None else [own_keys, own_keys.T, own_values]
+    key_shape = jax.ShapeDtypeStruct(keys.shape, jnp.float32)
+    outs = [("rows", jax.ShapeDtypeStruct(queries.shape, jnp.float32))]
+    outs += [("whole", key_shape), ("whole", key_shape)]
+    if own:
+        outs += [("own", jax.ShapeDtypeStruct(own_keys.shape, jnp.float32))] * 2
+    return attention_call(
+        backward_kernel,
+        meta,
+        [queries, upstream, totals],
+        [keys, keys.T, values],
+        own,
+        outs,
+        5,
     )
 
 
@@ -280,56 +397,47 @@
     )
     input_share = share_of(all_rows)
     within = jnp.arange(cont_rows, dtype=jnp.int32) % CONT_LENGTH
-    owner = jnp.arange(cont_rows, dtype=jnp.int32) // CONT_LENGTH
     positions = jnp.concatenate(
         [ctx_index * own_rows + jnp.arange(own_rows, dtype=jnp.int32), token_length + within]
     )
-    cos_table, sin_table = angle_tables(positions)
+    cos_table, sin_table = (table.T for table in angle_tables(positions))
     act_a = norm_rows(all_rows, gain_attn).astype(jnp.bfloat16)
     query_rows = rotate(
-        jnp.dot(act_a, w_query, preferred_element_type=jnp.float32), cos_table, sin_table
+        jnp.einsum("rd,dq->qr", act_a, w_query, preferred_element_type=jnp.float32),
+        cos_table,
+        sin_table,
     ).astype(jnp.bfloat16)
-    joined_keys = rotate(
-        jnp.dot(act_a, key_weight, preferred_element_type=jnp.float32), cos_table, sin_table
-    ).astype(jnp.bfloat16)
+    joined_keys = (
+        rotate(
+            jnp.einsum("rd,dq->qr", act_a, key_weight, preferred_element_type=jnp.float32),
+            cos_table,
+            sin_table,
+        )
+        .astype(jnp.bfloat16)
+        .T
+    )
     joined_values = jnp.dot(act_a, value_weight, preferred_element_type=jnp.float32).astype(
         jnp.bfloat16
     )
     local_pairs = jnp.concatenate([joined_keys[:own_rows], joined_values[:own_rows]], axis=1)
     prompt_pairs = lax.all_gather(local_pairs, "ctx", axis=0, tiled=True)
-    prompt_total = prompt_pairs.shape[0]
     shared_prompt_keys = prompt_pairs[:, :key_width]
     shared_prompt_values = prompt_pairs[:, key_width:]
-    key_place = jnp.arange(prompt_total, dtype=jnp.int32)
-    key_valid = key_place < token_length
-    block_rows = min(512, own_rows)
-    block_index = 0
-    query_place = (
-        ctx_index * own_rows + block_index * block_rows + jnp.arange(block_rows, dtype=jnp.int32)
-    )
-    block_masks = [(key_place[None, :] <= query_place[:, None]) & key_valid[None, :]]
-    cont_mask = jnp.concatenate(
-        [
-            jnp.broadcast_to(key_valid[None, :], (cont_rows, prompt_total)),
-            (owner[:, None] == owner[None, :]) & (within[None, :] <= within[:, None]),
-        ],
-        axis=1,
-    )
-    cont_keys = jnp.concatenate([shared_prompt_keys, joined_keys[own_rows:]], axis=0)
-    cont_values = jnp.concatenate([shared_prompt_values, joined_values[own_rows:]], axis=0)
-    prompt_mask = block_masks[0]
+    meta = jnp.stack([token_length, ctx_index * own_rows]).astype(jnp.int32)
 
     def head_inputs(head, prompt):
         wide = slice(head * group_width, (head + 1) * group_width)
         thin = slice(head * HEAD_WIDTH, (head + 1) * HEAD_WIDTH)
+        shared = (shared_prompt_keys[:, thin], shared_prompt_values[:, thin])
         if prompt:
-            return (
-                query_rows[:own_rows, wide],
-                shared_prompt_keys[:, thin],
-                shared_prompt_values[:, thin],
-                prompt_mask,
-            )
-        return (query_rows[own_rows:, wide], cont_keys[:, thin], cont_values[:, thin], cont_mask)
+            return (meta, query_rows[wide, :own_rows], *shared, None, None)
+        return (
+            meta,
+            query_rows[wide, own_rows:],
+            *shared,
+            joined_keys[own_rows:, thin],
+            joined_values[own_rows:, thin],
+        )
 
     mixed_list = []
     totals = {}
@@ -337,7 +445,7 @@
     for head in range(kv_heads):
         mixed_prompt, totals[head, True] = attend_forward(*head_inputs(head, True))
         mixed_cont, totals[head, False] = attend_forward(*head_inputs(head, False))
-        mixed = jnp.concatenate([mixed_prompt, mixed_cont], axis=0).astype(jnp.bfloat16)
+        mixed = jnp.concatenate([mixed_prompt, mixed_cont], axis=1).T
         mixed_list.append(mixed)
         share_list.append(
             exchanged(
@@ -434,15 +542,13 @@
     hidden_act, mixed_grad = tied(hidden_act, mixed_grad)
     mlp_part = jnp.dot(hidden_act, w_down, preferred_element_type=jnp.float32).astype(jnp.bfloat16)
     grad_mixed, mlp_part = tied(grad_mixed, mlp_part)
-    mlp_slots = slot_part(
-        [mlp_part[s * share_rows : (s + 1) * share_rows] for s in range(count)]
-    )
+    mlp_parts = [mlp_part[s * share_rows : (s + 1) * share_rows] for s in range(count)]
     pieces = [(head, prompt) for head in range(kv_heads) for prompt in (True, False)]
     upstream_pieces = {
         (head, prompt): grad_mixed[
             (slice(0, own_rows) if prompt else slice(own_rows, total_rows)),
             head * group_width : (head + 1) * group_width,
-        ]
+        ].T
         for head, prompt in pieces
     }
     piece_grads = {}
@@ -456,22 +562,16 @@
             forward, backward = hop_step(forward, backward, place + 1, count)
             moved += [forward, backward]
         if 1 <= place < count:
-            mlp_state = sum_step(mlp_state, mlp_slots, count - place, count)
+            mlp_state = sum_step(mlp_state, slot_part(mlp_parts), count - place, count)
             moved += mlp_state
         if place < len(pieces):
-            query_piece, keys_piece, values_piece, mask_piece = head_inputs(*pieces[place])
             piece_grads[pieces[place]] = attend_backward(
-                query_piece,
-                keys_piece,
-                values_piece,
-                mask_piece,
-                totals[pieces[place]],
-                upstream_pieces[pieces[place]],
+                *head_inputs(*pieces[place]), totals[pieces[place]], upstream_pieces[pieces[place]]
             )
         if place + 1 < len(pieces):
             following = pieces[place + 1]
-            moved, piece_grads[pieces[place]], upstream_pieces[following] = tied(
-                moved, piece_grads[pieces[place]], upstream_pieces[following]
+            moved, piece_grads[pieces[place]], upstream_pieces[following], mlp_parts = tied(
+                moved, piece_grads[pieces[place]], upstream_pieces[following], mlp_parts
             )
         elif place < len(pieces):
             moved, piece_grads[pieces[place]] = tied(moved, piece_grads[pieces[place]])
@@ -480,7 +580,7 @@
             arrived[-place - 1], arrived[place + 1] = (forward, backward)
         if 1 <= place < count:
             mlp_state = tuple(moved)
-    mlp_share = sum_end(mlp_state, mlp_slots)
+    mlp_share = sum_end(mlp_state, slot_part(mlp_parts))
     result_share = (hidden_share + branch_scale * mlp_share).astype(jnp.bfloat16)
     grad_attn = jnp.concatenate(slots_from(arrived), axis=0)
     grad_out = jnp.einsum(
@@ -488,14 +588,14 @@
     )
     query_grad_rows = jnp.concatenate(
         [
-            jnp.concatenate([piece_grads[head, True][0], piece_grads[head, False][0]], axis=0)
+            jnp.concatenate([piece_grads[head, True][0], piece_grads[head, False][0]], axis=1)
             for head in range(kv_heads)
         ],
-        axis=1,
+        axis=0,
     )
     prompt_pairs_grad = jnp.concatenate(
         [
-            piece_grads[head, True][which] + piece_grads[head, False][which][:prompt_total]
+            piece_grads[head, True][which] + piece_grads[head, False][which]
             for which in (1, 2)
             for head in range(kv_heads)
         ],
@@ -503,7 +603,7 @@
     )
     grad_key_cont, grad_value_cont = (
         jnp.concatenate([piece_grads[head, False][which] for head in range(kv_heads)], axis=1)
-        for which in (1, 2)
+        for which in (3, 4)
     )
     other_pairs = lax.ppermute(
         lax.dynamic_slice_in_dim(prompt_pairs_grad, (1 - ctx_index) * own_rows, own_rows, 0),
@@ -514,20 +614,20 @@
         prompt_pairs_grad, ctx_index * own_rows, own_rows, 0
     )
     key_grad_rows = jnp.concatenate(
-        [pair_grads[:, :key_width], grad_key_cont[prompt_total:]], axis=0
+        [pair_grads[:, :key_width], grad_key_cont], axis=0
     )
     value_grad_rows = jnp.concatenate(
-        [pair_grads[:, key_width:], grad_value_cont[prompt_total:]], axis=0
+        [pair_grads[:, key_width:], grad_value_cont], axis=0
     )
     grad_query_lin = rotate(query_grad_rows, cos_table, -sin_table).astype(jnp.bfloat16)
-    grad_key_lin = rotate(key_grad_rows, cos_table, -sin_table).astype(jnp.bfloat16)
+    grad_key_lin = rotate(key_grad_rows.T, cos_table, -sin_table).astype(jnp.bfloat16)
     grad_value_lin = value_grad_rows.astype(jnp.bfloat16)
-    grad_query = jnp.einsum("rd,rq->dq", act_a, grad_query_lin, preferred_element_type=jnp.float32)
-    grad_key = jnp.einsum("rd,rq->dq", act_a, grad_key_lin, preferred_element_type=jnp.float32)
+    grad_query = jnp.einsum("rd,qr->dq", act_a, grad_query_lin, preferred_element_type=jnp.float32)
+    grad_key = jnp.einsum("rd,qr->dq", act_a, grad_key_lin, preferred_element_type=jnp.float32)
     grad_value = jnp.einsum("rd,rq->dq", act_a, grad_value_lin, preferred_element_type=jnp.float32)
     input_grad = (
-        jnp.einsum("rq,dq->rd", grad_query_lin, w_query, preferred_element_type=jnp.float32)
-        + jnp.einsum("rq,dq->rd", grad_key_lin, key_weight, preferred_element_type=jnp.float32)
+        jnp.einsum("qr,dq->rd", grad_query_lin, w_query, preferred_element_type=jnp.float32)
+        + jnp.einsum("qr,dq->rd", grad_key_lin, key_weight, preferred_element_type=jnp.float32)
         + jnp.einsum("rq,dq->rd", grad_value_lin, value_weight, preferred_element_type=jnp.float32)
     )
     input_part = input_grad.astype(jnp.bfloat16)

time: 769 us -> 746 us (0.970)
  matrix products: 257 us -> 186 us
  Pallas kernels: 0 us -> 58.6 us
  other arithmetic: 141 us -> 107 us
  local copies, waits for them, and re-layouts: 50.3 us -> 68 us
    dot_general x30 -> x6, matrix products: 98.8 us -> 20 us  [the longest x1 4.58 us: shards(): jnp.einsum('rd,dq->qr', act_a, w_query, preferred_element_type=jnp.float32)]
    pallas_call x0 -> x8, Pallas kernels: none -> 58.6 us  [attention_call(): pl.pallas_call(kernel, out_shape=[out for _, out in outs], grid_spec=pltp...]
    another operation x14 -> x11, other arithmetic: 21.8 us -> 3.54 us
    ppermute x12, waiting for transfers between devices: 17.6 us -> 2.39 us  [hop_step(): lax.ppermute(forward, 'tensor', [(i, i + 1) for i in range(step - 1, coun...]
    transpose x0 -> x11, local copies, waits for them, and re-layouts: none -> 10.2 us  [the longest x3 3.13 us: attend_backward(): own = [] if own_keys is None else [own_keys, own_keys.T, own_values]]
    unnamed x290 -> x268, local copies, waits for them, and re-layouts: 27.8 us -> 37.2 us
    reduce_sum x3 -> x0, other arithmetic: 9.23 us -> none  [attend_forward(): jnp.sum(jnp.exp(scores - highest_score), axis=-1, keepdims=True)]
    all_gather x1, waiting for transfers between devices: 0.02 us -> 8.35 us  [shards(): lax.all_gather(own_out_half, ('tensor', 'ctx'), axis=0, tiled=True)]
  transfers between devices with their start and end apart: 62 -> 62, of which waited for: 25 -> 27; matrix products, arithmetic and copies ran while one was open for 51% -> 40% of each run, Pallas kernels for 0% -> 8%
where the time goes in v5:
time: 746 us; the launch traced here: 737 us
  matrix products  186 us (25%)
  waiting for transfers between devices  155 us (21%)
  starting transfers between devices  142 us (19%)
  other arithmetic  107 us (14%)
  local copies, waits for them, and re-layouts  68 us (9%)
  Pallas kernels  58.6 us (8%)
  between operations  17 us (2%)
    ppermute x9, waiting for transfers between devices, sum_step(): lax.ppermute(to_right, 'tensor', [(i, i + 1) for i in range(0, count - di...  59.7 us
    pallas_call x8, Pallas kernels, attention_call(): pl.pallas_call(kernel, out_shape=[out for _, out in outs], grid_spec=pltp...  58.6 us
    ppermute x12, waiting for transfers between devices, hop_step(): lax.ppermute(backward, 'tensor', [(i, i - 1) for i in range(1, count - st...  49 us
    ppermute x9, starting transfers between devices, sum_step(): lax.ppermute(to_right, 'tensor', [(i, i + 1) for i in range(0, count - di...  47.9 us
    unnamed x268, local copies, waits for them, and re-layouts  37.2 us
    ppermute x12, starting transfers between devices, hop_step(): lax.ppermute(forward, 'tensor', [(i, i + 1) for i in range(step - 1, coun...  32.7 us
    dot_general x4, matrix products, shards(): jnp.einsum('rf,df->rd', grad_up_slot, w_up, preferred_element_type=jnp.fl...  26.2 us
    convert_element_type x6, other arithmetic, added(): (first.astype(jnp.float32) + second.astype(jnp.float32)).astype(jnp.bfloa...  25.2 us
  transfers between devices with their start and end apart: 62, of which 27 were waited for; matrix products, arithmetic and copies ran while one was open for 40% of the time, Pallas kernels for 8%

profile of v5, /device:TPU:0, one launch (start us, length us, event | category | flops | bytes accessed | tf_op | source)
XLA Modules:
  0.0 736.5 jit_solution(9808574104736887834)
XLA Ops:
  82.0 11.1 %fusion.79 = f32[1024,2048]{1,0:T(8,128)} fusion(bf16[1024,2048]{1,0:T(8,128)(2,1)S(1)} %pad_maximum_fusion.2, bf16[2048,2048]{1,0:T(8,128)(2,1)S(1)} %bitcast.209), kind=kOutput, calls=%fused_computation.259 | convolution fusion | flops 8589934592 | bytes 20971520 | tf_op jit(solution)/shard_map/rd,fd->rf/dot_general | solution.py:460
  108.9 8.4 %all-gather.2.cloned.1.call-done = bf16[2048,2048]{1,0:T(8,128)(2,1)} async-done(((bf16[256,2048]{1,0:T(8,128)(2,1)}), bf16[2048,2048]{1,0:T(8,128)(2,1)}) %all-gather.2.cloned.1.call-update) | async-done | bytes 8388624 | tf_op jit(solution)/shard_map/all_gather | solution.py:394
  117.2 6.7 multiply_reduce_fusion.6
  156.5 6.1 fusion.82
  171.0 6.8 fusion.27
  199.3 6.8 fusion.28
  209.0 6.1 fusion.86
  215.1 6.3 multiply_convert_fusion.3
  223.8 6.9 fusion.29
  235.2 11.4 %convolution_convert_fusion.2 = bf16[2048,2048]{1,0:T(8,128)(2,1)} fusion(bf16[256,2048]{1,0:T(8,128)(2,1)S(1)} %get-tuple-element.169, bf16[256,2048]{1,0:T(8,128)(2,1)S(1)} %copy-done.121, bf16[256,2048]{1,0:T(8,128)(2,1)S(1)} %get-tuple-element.167, bf16[256,2048]{1,0:T(8,128)(2,1)S(1)} %get-tuple-element.166, ...), kind=kOutput, calls=%fused_computation.6 | convolution fusion | flops 8627683328 | bytes 16777216 | tf_op jit(solution)/shard_map/rd,rf->df/dot_general | solution.py:512
  246.7 8.3 %collective-permute-done.12 = bf16[256,2048]{1,0:T(8,128)(2,1)} collective-permute-done((bf16[256,2048]{1,0:T(8,128)(2,1)}, bf16[256,2048]{1,0:T(8,128)(2,1)}, u32[]{:S(2)}, u32[]{:S(2)}) %collective-permute-start.12) | collective-permute-done | bytes 1048608 | tf_op jit(solution)/shard_map/ppermute | solution.py:288
  266.6 12.8 %convolution_convert_fusion.1 = bf16[2048,2048]{1,0:T(8,128)(2,1)} fusion(bf16[256,2048]{1,0:T(8,128)(2,1)} %copy-done.119, bf16[256,2048]{1,0:T(8,128)(2,1)} %copy-done.118, bf16[256,2048]{1,0:T(8,128)(2,1)S(1)} %copy-done.117, bf16[256,2048]{1,0:T(8,128)(2,1)S(1)} %copy-done.115, bf16[256,2048]{1,0:T(8,128)(2,1)S(1)} %copy-done.93, ...), kind=kOutput, calls=%fused_computation.5 | convolution fusion | flops 8627683328 | bytes 16777216 | tf_op jit(solution)/shard_map/rd,rf->df/dot_general | solution.py:513
  295.4 6.3 collective-permute-start.16
  301.7 11.4 %convolution_convert_fusion = bf16[2048,2048]{1,0:T(8,128)(2,1)} fusion(bf16[1024,2048]{1,0:T(8,128)(2,1)S(1)} %copy-done.64, bf16[1024,2048]{1,0:T(8,128)(2,1)S(1)} %constant_dynamic-update-slice_fusion.8), kind=kOutput, calls=%fused_computation.4 | convolution fusion | flops 8594128896 | bytes 16777216 | tf_op jit(solution)/shard_map/rf,rd->df/dot_general | solution.py:514
  340.3 15.4 %convolution_convert_fusion.3 = bf16[1024,2048]{1,0:T(8,128)(2,1)} fusion(bf16[1024,2048]{1,0:T(8,128)(2,1)} %copy-done.104, bf16[2048,2048]{1,0:T(8,128)(2,1)} %param.25), kind=kOutput, calls=%fused_computation.36 | convolution fusion | flops 8592031744 | bytes 16777216 | tf_op jit(solution)/shard_map/dot_general | solution.py:543
  369.9 9.3 %shard_map.241 = (f32[256,512]{1,0:T(8,128)S(1)}, f32[1024,64]{1,0:T(8,128)S(1)}, f32[1024,64]{1,0:T(8,128)S(1)}) custom-call(s32[2]{0:T(128)S(1)} %pad_add_fusion.meta_ref, bf16[256,512]{1,0:T(8,128)(2,1)S(1)} %copy-done.27, bf16[256,512]{1,0:T(8,128)(2,1)S(1)} %copy-done.31, f32[4,1,512]{2,1,0:T(1,128)S(1)} %copy-done.43, bf16[1024,64]{1,0:T(8,128)(2,1)S(1)} %copy-done.14, ...), custom_call_target="tpu_custom_call" | custom-call | flops 1342177280 | bytes 1052672 | tf_op jit(solution)/shard_map/pallas_call | solution.py:183
  391.0 9.0 %collective-permute-start.25 = (bf16[256,2048]{1,0:T(8,128)(2,1)}, bf16[256,2048]{1,0:T(8,128)(2,1)}, u32[]{:S(2)}, u32[]{:S(2)}) collective-permute-start(bf16[256,2048]{1,0:T(8,128)(2,1)} %get-tuple-element.208), channel_id=1, source_target_pairs={{0,1},{4,5},{8,9},{12,13},{16,17},{20,21},{24,25},{28,29}} | collective-permute-start | bytes 3145736 | tf_op jit(solution)/shard_map/ppermute | solution.py:288
  408.7 9.8 %shard_map.242 = (f32[256,512]{1,0:T(8,128)S(1)}, f32[1024,64]{1,0:T(8,128)S(1)}, f32[1024,64]{1,0:T(8,128)S(1)}, f32[512,64]{1,0:T(8,128)S(1)}, f32[512,64]{1,0:T(8,128)S(1)}) custom-call(s32[2]{0:T(128)S(1)} %pad_add_fusion.meta_ref, bf16[256,512]{1,0:T(8,128)(2,1)S(1)} %copy-done.25, bf16[256,512]{1,0:T(8,128)(2,1)S(1)} %copy-done.30, ...), custom_call_target="tpu_custom_call" | custom-call | flops 1509949440 | bytes 1052672 | tf_op jit(solution)/shard_map/pallas_call | solution.py:183
  438.5 9.2 %shard_map.243 = (f32[256,512]{1,0:T(8,128)S(1)}, f32[1024,64]{1,0:T(8,128)S(1)}, f32[1024,64]{1,0:T(8,128)S(1)}) custom-call(s32[2]{0:T(128)S(1)} %pad_add_fusion.meta_ref, bf16[256,512]{1,0:T(8,128)(2,1)S(1)} %copy-done.23, bf16[256,512]{1,0:T(8,128)(2,1)S(1)} %copy-done.29, f32[4,1,512]{2,1,0:T(1,128)S(1)} %get-tuple-element.213.total_ref, ...), custom_call_target="tpu_custom_call" | custom-call | flops 1342177280 | bytes 1052672 | tf_op jit(solution)/shard_map/pallas_call | solution.py:183
  450.3 6.7 collective-permute-done.28
  467.9 9.8 %shard_map.244 = (f32[256,512]{1,0:T(8,128)S(1)}, f32[1024,64]{1,0:T(8,128)S(1)}, f32[1024,64]{1,0:T(8,128)S(1)}, f32[512,64]{1,0:T(8,128)S(1)}, f32[512,64]{1,0:T(8,128)S(1)}) custom-call(s32[2]{0:T(128)S(1)} %pad_add_fusion.meta_ref, bf16[256,512]{1,0:T(8,128)(2,1)S(1)} %copy-done.21, bf16[256,512]{1,0:T(8,128)(2,1)S(1)} %copy-done.28, ...), custom_call_target="tpu_custom_call" | custom-call | flops 1509949440 | bytes 1052672 | tf_op jit(solution)/shard_map/pallas_call | solution.py:183
  511.4 10.2 %pad_maximum_fusion = bf16[2048,1280]{0,1:T(8,128)(2,1)} fusion(bf16[2048,512]{0,1:T(8,128)(2,1)S(1)} %copy-done.72, bf16[2048,128]{0,1:T(8,128)(2,1)S(1)} %convolution_convert_fusion.7, bf16[2048,128]{0,1:T(8,128)(2,1)S(1)} %convolution_convert_fusion.6, bf16[2048,512]{0,1:T(8,128)(2,1)S(1)} %copy-done.73), kind=kLoop, calls=%fused_computation.7 | loop fusion | flops 20971520 | bytes 10485760 | tf_op jit(solution)/shard_map/concatenate | solution.py:681
  537.9 6.9 collective-permute-start.36
  544.8 15.4 %collective-permute-done.39 = bf16[256,2048]{1,0:T(8,128)(2,1)} collective-permute-done((bf16[256,2048]{1,0:T(8,128)(2,1)}, bf16[256,2048]{1,0:T(8,128)(2,1)}, u32[]{:S(2)}, u32[]{:S(2)}) %collective-permute-start.39) | collective-permute-done | bytes 1048608 | tf_op jit(solution)/shard_map/ppermute | solution.py:273
  560.2 6.1 collective-permute-done.36
  580.8 17.3 %collective-permute-done.40 = bf16[256,2048]{1,0:T(8,128)(2,1)} collective-permute-done((bf16[256,2048]{1,0:T(8,128)(2,1)}, bf16[256,2048]{1,0:T(8,128)(2,1)}, u32[]{:S(2)}, u32[]{:S(2)}) %collective-permute-start.40) | collective-permute-done | bytes 1048608 | tf_op jit(solution)/shard_map/ppermute | solution.py:288
  598.1 6.7 collective-permute-done.43
  615.1 15.8 %collective-permute-done.44 = bf16[256,2048]{1,0:T(8,128)(2,1)} collective-permute-done((bf16[256,2048]{1,0:T(8,128)(2,1)}, bf16[256,2048]{1,0:T(8,128)(2,1)}, u32[]{:S(2)}, u32[]{:S(2)}) %collective-permute-start.44) | collective-permute-done | bytes 1048608 | tf_op jit(solution)/shard_map/ppermute | solution.py:288
  657.7 11.0 %collective-permute-done.49 = f32[2,2048]{1,0:T(2,128)S(1)} collective-permute-done((f32[2,2048]{1,0:T(2,128)S(1)}, f32[2,2048]{1,0:T(2,128)S(1)}, u32[]{:S(2)}, u32[]{:S(2)}) %collective-permute-start.49) | collective-permute-done | bytes 16416 | tf_op jit(solution)/shard_map/ppermute | solution.py:324
  672.6 6.8 collective-permute-start.52
  685.6 10.9 %collective-permute-done.52 = f32[2,2048]{1,0:T(2,128)S(1)} collective-permute-done((f32[2,2048]{1,0:T(2,128)S(1)}, f32[2,2048]{1,0:T(2,128)S(1)}, u32[]{:S(2)}, u32[]{:S(2)}) %collective-permute-start.52) | collective-permute-done | bytes 16416 | tf_op jit(solution)/shard_map/ppermute | solution.py:324
  715.0 7.7 %collective-permute-done.55 = bf16[256,2048]{1,0:T(8,128)(2,1)} collective-permute-done((bf16[256,2048]{1,0:T(8,128)(2,1)}, bf16[256,2048]{1,0:T(8,128)(2,1)}, u32[]{:S(2)}, u32[]{:S(2)}) %collective-permute-start.55) | collective-permute-done | bytes 1048608 | tf_op jit(solution)/shard_map/ppermute | solution.py:273
  (524 shorter events, 420.2 us)
Async XLA Ops:
  7.2 110.0 %all-gather.2.cloned.1.call-start = ((), (), s32[]{:S(2)}) async-start(), calls=%async_computation.4 | async-start | bytes 9437184 | tf_op jit(solution)/shard_map/all_gather | solution.py:394
  9.7 520.2 %reduce-scatter.5.cloned.1.call-start = ((), (), s32[]{:S(2)}) async-start(), calls=%async_computation.5 | async-start | bytes 9437184 | tf_op jit(solution)/shard_map/reduce_scatter | solution.py:507
  52.7 40.3 %collective-permute-start.5 = (bf16[256,256]{0,1:T(8,128)(2,1)}, bf16[256,256]{0,1:T(8,128)(2,1)}, u32[]{:S(2)}, u32[]{:S(2)}) collective-permute-start(bf16[256,256]{0,1:T(8,128)(2,1)} %get-tuple-element.397), channel_id=1, source_target_pairs={{0,1},{1,2},{2,3},{3,0},{4,5},{5,6},{6,7},{7,4},{8,9},{9,10},{10,1... | collective-permute-start | bytes 393224 | tf_op jit(solution)/shard_map/ppermute | solution.py:304
  55.9 44.2 %collective-permute-start.4 = (bf16[256,256]{0,1:T(8,128)(2,1)}, bf16[256,256]{0,1:T(8,128)(2,1)}, u32[]{:S(2)}, u32[]{:S(2)}) collective-permute-start(bf16[256,256]{0,1:T(8,128)(2,1)} %get-tuple-element.398), channel_id=1, source_target_pairs={{0,2},{1,3},{2,0},{3,1},{4,6},{5,7},{6,4},{7,5},{8,10},{9,11},{10,... | collective-permute-start | bytes 393224 | tf_op jit(solution)/shard_map/ppermute | solution.py:304
  58.5 41.6 %collective-permute-start.3 = (bf16[256,256]{0,1:T(8,128)(2,1)}, bf16[256,256]{0,1:T(8,128)(2,1)}, u32[]{:S(2)}, u32[]{:S(2)}) collective-permute-start(bf16[256,256]{0,1:T(8,128)(2,1)} %get-tuple-element.399), channel_id=1, source_target_pairs={{0,3},{1,0},{2,1},{3,2},{4,7},{5,4},{6,5},{7,6},{8,11},{9,8},{10,9... | collective-permute-start | bytes 393224 | tf_op jit(solution)/shard_map/ppermute | solution.py:304
  72.8 27.3 %collective-permute-start.2 = (bf16[256,256]{0,1:T(8,128)(2,1)}, bf16[256,256]{0,1:T(8,128)(2,1)S(1)}, u32[]{:S(2)}, u32[]{:S(2)}) collective-permute-start(bf16[256,256]{0,1:T(8,128)(2,1)} %get-tuple-element.400), channel_id=1, source_target_pairs={{0,1},{1,2},{2,3},{3,0},{4,5},{5,6},{6,7},{7,4},{8,9},{9,10},{10,1... | collective-permute-start | bytes 393224 | tf_op jit(solution)/shard_map/ppermute | solution.py:304
  73.6 28.2 %collective-permute-start.1 = (bf16[256,256]{0,1:T(8,128)(2,1)}, bf16[256,256]{0,1:T(8,128)(2,1)S(1)}, u32[]{:S(2)}, u32[]{:S(2)}) collective-permute-start(bf16[256,256]{0,1:T(8,128)(2,1)} %get-tuple-element.401), channel_id=1, source_target_pairs={{0,2},{1,3},{2,0},{3,1},{4,6},{5,7},{6,4},{7,5},{8,10},{9,11},{10,... | collective-permute-start | bytes 393224 | tf_op jit(solution)/shard_map/ppermute | solution.py:304
  125.5 27.5 %collective-permute-start.7 = (bf16[256,2048]{1,0:T(8,128)(2,1)S(1)}, bf16[256,2048]{1,0:T(8,128)(2,1)S(1)}, u32[]{:S(2)}, u32[]{:S(2)}) collective-permute-start(bf16[256,2048]{1,0:T(8,128)(2,1)S(1)} %multiply_convert_fusion.15), channel_id=1, source_target_pairs={{1,0},{2,1},{3,2},{5,4},{6,5},{7,6},{9,8},{10,9},{11,10},{13,12},{... | collective-permute-start | bytes 3145736 | tf_op jit(solution)/shard_map/ppermute | solution.py:273
  127.1 27.1 %collective-permute-start.6 = (bf16[256,2048]{1,0:T(8,128)(2,1)S(1)}, bf16[256,2048]{1,0:T(8,128)(2,1)S(1)}, u32[]{:S(2)}, u32[]{:S(2)}) collective-permute-start(bf16[256,2048]{1,0:T(8,128)(2,1)S(1)} %multiply_convert_fusion.15), channel_id=1, source_target_pairs={{0,1},{1,2},{2,3},{4,5},{5,6},{6,7},{8,9},{9,10},{10,11},{12,13},{... | collective-permute-start | bytes 3145736 | tf_op jit(solution)/shard_map/ppermute | solution.py:272
  154.9 27.9 %collective-permute-start.9 = (bf16[256,2048]{1,0:T(8,128)(2,1)S(1)}, bf16[256,2048]{1,0:T(8,128)(2,1)S(1)}, u32[]{:S(2)}, u32[]{:S(2)}) collective-permute-start(bf16[256,2048]{1,0:T(8,128)(2,1)S(1)} %collective-permute-done.7), channel_id=1, source_target_pairs={{1,0},{2,1},{5,4},{6,5},{9,8},{10,9},{13,12},{14,13},{17,16},{18,1... | collective-permute-start | bytes 3145736 | tf_op jit(solution)/shard_map/ppermute | solution.py:273
  183.7 25.1 %collective-permute-start.11 = (bf16[256,2048]{1,0:T(8,128)(2,1)S(1)}, bf16[256,2048]{1,0:T(8,128)(2,1)S(1)}, u32[]{:S(2)}, u32[]{:S(2)}) collective-permute-start(bf16[256,2048]{1,0:T(8,128)(2,1)S(1)} %collective-permute-done.9), channel_id=1, source_target_pairs={{1,0},{5,4},{9,8},{13,12},{17,16},{21,20},{25,24},{29,28}} | collective-permute-start | bytes 3145736 | tf_op jit(solution)/shard_map/ppermute | solution.py:273
  255.0 275.0 %reduce-scatter.7.cloned.1.call-start = ((), (), s32[]{:S(2)}) async-start(), calls=%async_computation.6 | async-start | bytes 9437184 | tf_op jit(solution)/shard_map/reduce_scatter | solution.py:507
  285.3 259.5 %reduce-scatter.9.cloned.1.call-start = ((), (), s32[]{:S(2)}) async-start(), calls=%async_computation.7 | async-start | bytes 9437184 | tf_op jit(solution)/shard_map/reduce_scatter | solution.py:507
  339.9 316.7 %reduce-scatter.11.cloned.1.call-start = ((), (), s32[]{:S(2)}) async-start(), calls=%async_computation.8 | async-start | bytes 5898240 | tf_op jit(solution)/shard_map/reduce_scatter | solution.py:680
  358.3 26.9 %collective-permute-start.22 = (bf16[256,2048]{1,0:T(8,128)(2,1)}, bf16[256,2048]{1,0:T(8,128)(2,1)}, u32[]{:S(2)}, u32[]{:S(2)}) collective-permute-start(bf16[256,2048]{1,0:T(8,128)(2,1)} %get-tuple-element.186), channel_id=1, source_target_pairs={{1,0},{2,1},{3,2},{5,4},{6,5},{7,6},{9,8},{10,9},{11,10},{13,12},{... | collective-permute-start | bytes 3145736 | tf_op jit(solution)/shard_map/ppermute | solution.py:273
  359.6 26.8 %collective-permute-start.21 = (bf16[256,2048]{1,0:T(8,128)(2,1)}, bf16[256,2048]{1,0:T(8,128)(2,1)}, u32[]{:S(2)}, u32[]{:S(2)}) collective-permute-start(bf16[256,2048]{1,0:T(8,128)(2,1)} %get-tuple-element.186), channel_id=1, source_target_pairs={{0,1},{1,2},{2,3},{4,5},{5,6},{6,7},{8,9},{9,10},{10,11},{12,13},{... | collective-permute-start | bytes 3145736 | tf_op jit(solution)/shard_map/ppermute | solution.py:272
  386.4 32.2 %collective-permute-start.23 = (bf16[256,2048]{1,0:T(8,128)(2,1)}, bf16[256,2048]{1,0:T(8,128)(2,1)}, u32[]{:S(2)}, u32[]{:S(2)}) collective-permute-start(bf16[256,2048]{1,0:T(8,128)(2,1)} %collective-permute-done.21), channel_id=1, source_target_pairs={{1,2},{2,3},{5,6},{6,7},{9,10},{10,11},{13,14},{14,15},{17,18},{18... | collective-permute-start | bytes 3145736 | tf_op jit(solution)/shard_map/ppermute | solution.py:272
  388.0 30.6 %collective-permute-start.24 = (bf16[256,2048]{1,0:T(8,128)(2,1)}, bf16[256,2048]{1,0:T(8,128)(2,1)}, u32[]{:S(2)}, u32[]{:S(2)}) collective-permute-start(bf16[256,2048]{1,0:T(8,128)(2,1)} %collective-permute-done.22), channel_id=1, source_target_pairs={{1,0},{2,1},{5,4},{6,5},{9,8},{10,9},{13,12},{14,13},{17,16},{18,1... | collective-permute-start | bytes 3145736 | tf_op jit(solution)/shard_map/ppermute | solution.py:273
  389.3 29.3 %collective-permute-start.26 = (bf16[256,2048]{1,0:T(8,128)(2,1)}, bf16[256,2048]{1,0:T(8,128)(2,1)}, u32[]{:S(2)}, u32[]{:S(2)}) collective-permute-start(bf16[256,2048]{1,0:T(8,128)(2,1)} %get-tuple-element.208), channel_id=1, source_target_pairs={{3,2},{7,6},{11,10},{15,14},{19,18},{23,22},{27,26},{31,30}} | collective-permute-start | bytes 3145736 | tf_op jit(solution)/shard_map/ppermute | solution.py:289
  391.0 28.9 %collective-permute-start.25 = (bf16[256,2048]{1,0:T(8,128)(2,1)}, bf16[256,2048]{1,0:T(8,128)(2,1)}, u32[]{:S(2)}, u32[]{:S(2)}) collective-permute-start(bf16[256,2048]{1,0:T(8,128)(2,1)} %get-tuple-element.208), channel_id=1, source_target_pairs={{0,1},{4,5},{8,9},{12,13},{16,17},{20,21},{24,25},{28,29}} | collective-permute-start | bytes 3145736 | tf_op jit(solution)/shard_map/ppermute | solution.py:288
  425.8 24.5 %collective-permute-start.29 = (bf16[256,2048]{1,0:T(8,128)(2,1)}, bf16[256,2048]{1,0:T(8,128)(2,1)}, u32[]{:S(2)}, u32[]{:S(2)}) collective-permute-start(bf16[256,2048]{1,0:T(8,128)(2,1)} %get-tuple-element.352), channel_id=1, source_target_pairs={{0,1},{1,2},{4,5},{5,6},{8,9},{9,10},{12,13},{13,14},{16,17},{17,1... | collective-permute-start | bytes 3145736 | tf_op jit(solution)/shard_map/ppermute | solution.py:288
  432.4 24.6 %collective-permute-start.28 = (bf16[256,2048]{1,0:T(8,128)(2,1)}, bf16[256,2048]{1,0:T(8,128)(2,1)}, u32[]{:S(2)}, u32[]{:S(2)}) collective-permute-start(bf16[256,2048]{1,0:T(8,128)(2,1)} %collective-permute-done.24), channel_id=1, source_target_pairs={{1,0},{5,4},{9,8},{13,12},{17,16},{21,20},{25,24},{29,28}} | collective-permute-start | bytes 3145736 | tf_op jit(solution)/shard_map/ppermute | solution.py:273
  484.7 45.2 %collective-permute-start.34 = (bf16[256,2048]{1,0:T(8,128)(2,1)S(1)}, bf16[256,2048]{1,0:T(8,128)(2,1)}, u32[]{:S(2)}, u32[]{:S(2)}) collective-permute-start(bf16[256,2048]{1,0:T(8,128)(2,1)S(1)} %add_convert_fusion.6), channel_id=1, source_target_pairs={{1,0},{2,1},{3,2},{5,4},{6,5},{7,6},{9,8},{10,9},{11,10},{13,12},{... | collective-permute-start | bytes 3145736 | tf_op jit(solution)/shard_map/ppermute | solution.py:273
  486.0 44.0 %collective-permute-start.33 = (bf16[256,2048]{1,0:T(8,128)(2,1)S(1)}, bf16[256,2048]{1,0:T(8,128)(2,1)}, u32[]{:S(2)}, u32[]{:S(2)}) collective-permute-start(bf16[256,2048]{1,0:T(8,128)(2,1)S(1)} %add_convert_fusion.6), channel_id=1, source_target_pairs={{0,1},{1,2},{2,3},{4,5},{5,6},{6,7},{8,9},{9,10},{10,11},{12,13},{... | collective-permute-start | bytes 3145736 | tf_op jit(solution)/shard_map/ppermute | solution.py:272
  531.6 28.6 %collective-permute-start.39 = (bf16[256,2048]{1,0:T(8,128)(2,1)}, bf16[256,2048]{1,0:T(8,128)(2,1)}, u32[]{:S(2)}, u32[]{:S(2)}) collective-permute-start(bf16[256,2048]{1,0:T(8,128)(2,1)} %collective-permute-done.34), channel_id=1, source_target_pairs={{1,0},{2,1},{5,4},{6,5},{9,8},{10,9},{13,12},{14,13},{17,16},{18,1... | collective-permute-start | bytes 3145736 | tf_op jit(solution)/shard_map/ppermute | solution.py:273
  537.9 28.4 %collective-permute-start.36 = (bf16[256,2048]{1,0:T(8,128)(2,1)}, bf16[256,2048]{1,0:T(8,128)(2,1)}, u32[]{:S(2)}, u32[]{:S(2)}) collective-permute-start(bf16[256,2048]{1,0:T(8,128)(2,1)} %get-tuple-element.328), channel_id=1, source_target_pairs={{0,1},{4,5},{8,9},{12,13},{16,17},{20,21},{24,25},{28,29}} | collective-permute-start | bytes 3145736 | tf_op jit(solution)/shard_map/ppermute | solution.py:288
  572.5 25.6 %collective-permute-start.40 = (bf16[256,2048]{1,0:T(8,128)(2,1)}, bf16[256,2048]{1,0:T(8,128)(2,1)}, u32[]{:S(2)}, u32[]{:S(2)}) collective-permute-start(bf16[256,2048]{1,0:T(8,128)(2,1)} %get-tuple-element.326), channel_id=1, source_target_pairs={{0,1},{1,2},{4,5},{5,6},{8,9},{9,10},{12,13},{13,14},{16,17},{17,1... | collective-permute-start | bytes 3145736 | tf_op jit(solution)/shard_map/ppermute | solution.py:288
  579.5 25.3 %collective-permute-start.43 = (bf16[256,2048]{1,0:T(8,128)(2,1)}, bf16[256,2048]{1,0:T(8,128)(2,1)}, u32[]{:S(2)}, u32[]{:S(2)}) collective-permute-start(bf16[256,2048]{1,0:T(8,128)(2,1)} %collective-permute-done.39), channel_id=1, source_target_pairs={{1,0},{5,4},{9,8},{13,12},{17,16},{21,20},{25,24},{29,28}} | collective-permute-start | bytes 3145736 | tf_op jit(solution)/shard_map/ppermute | solution.py:273
  611.8 24.3 %collective-permute-start.45 = (bf16[256,2048]{1,0:T(8,128)(2,1)}, bf16[256,2048]{1,0:T(8,128)(2,1)}, u32[]{:S(2)}, u32[]{:S(2)}) collective-permute-start(bf16[256,2048]{1,0:T(8,128)(2,1)} %get-tuple-element.324), channel_id=1, source_target_pairs={{1,0},{2,1},{3,2},{5,4},{6,5},{7,6},{9,8},{10,9},{11,10},{13,12},{... | collective-permute-start | bytes 3145736 | tf_op jit(solution)/shard_map/ppermute | solution.py:289
  643.9 24.9 %collective-permute-start.47 = (bf16[256,2048]{1,0:T(8,128)(2,1)}, bf16[256,2048]{1,0:T(8,128)(2,1)}, u32[]{:S(2)}, u32[]{:S(2)}) collective-permute-start(bf16[256,2048]{1,0:T(8,128)(2,1)} %add_convert_fusion.1), channel_id=1, source_target_pairs={{1,0},{2,1},{3,2},{5,4},{6,5},{7,6},{9,8},{10,9},{11,10},{13,12},{... | collective-permute-start | bytes 3145736 | tf_op jit(solution)/shard_map/ppermute | solution.py:273
  668.8 31.9 %collective-permute-start.50 = (bf16[256,2048]{1,0:T(8,128)(2,1)}, bf16[256,2048]{1,0:T(8,128)(2,1)}, u32[]{:S(2)}, u32[]{:S(2)}) collective-permute-start(bf16[256,2048]{1,0:T(8,128)(2,1)} %collective-permute-done.46), channel_id=1, source_target_pairs={{1,2},{2,3},{5,6},{6,7},{9,10},{10,11},{13,14},{14,15},{17,18},{18... | collective-permute-start | bytes 3145736 | tf_op jit(solution)/shard_map/ppermute | solution.py:272
  670.5 30.3 %collective-permute-start.51 = (bf16[256,2048]{1,0:T(8,128)(2,1)}, bf16[256,2048]{1,0:T(8,128)(2,1)}, u32[]{:S(2)}, u32[]{:S(2)}) collective-permute-start(bf16[256,2048]{1,0:T(8,128)(2,1)} %collective-permute-done.47), channel_id=1, source_target_pairs={{1,0},{2,1},{5,4},{6,5},{9,8},{10,9},{13,12},{14,13},{17,16},{18,1... | collective-permute-start | bytes 3145736 | tf_op jit(solution)/shard_map/ppermute | solution.py:273
  (159 other events, 1672.7 us)
Sparse Core Ops, SparseCore 0:
  10.2 106.9 all-gather.1
  255.1 71.4 reduce-scatter.4
  330.1 71.4 reduce-scatter.6
  405.0 71.4 reduce-scatter.8
  521.8 56.9 reduce-scatter.10

commit v6 on v5

--- a/solution.py
+++ b/solution.py
@@ -288,6 +288,28 @@
         lax.ppermute(to_right, "tensor", [(i, i + 1) for i in range(0, count - distance)]),
         lax.ppermute(to_left, "tensor", [(i, i - 1) for i in range(distance, count)]),
     )
+
+
+def stream_step(states, parts, part_of, distance, count, waiting=()):
+    moved = []
+    for stream, state in enumerate(states):
+        part_at = part_of(parts, stream)
+        to_right = part_at(distance)
+        to_left = part_at(-distance)
+        if state is not None:
+            to_right = added(to_right, state[0])
+            to_left = added(to_left, state[1])
+        if stream == 0:
+            to_right, to_left, parts, waiting = tied(to_right, to_left, parts, waiting)
+        else:
+            to_right, to_left, parts = tied(to_right, to_left, parts)
+        moved.append(
+            (
+                lax.ppermute(to_right, "tensor", [(i, i + 1) for i in range(0, count - distance)]),
+                lax.ppermute(to_left, "tensor", [(i, i - 1) for i in range(distance, count)]),
+            )
+        )
+    return (moved, parts, waiting)
 
 
 def sum_end(state, part_at):
@@ -392,10 +414,9 @@
 
     own_out_half = lax.dynamic_slice_in_dim(w_out, ctx_index * head_half, head_half, 0)
     full_out = lax.all_gather(own_out_half, ("tensor", "ctx"), axis=0, tiled=True)
-    all_rows = jnp.concatenate([prompt_in[0], cont_in[0].reshape(cont_rows, width)], axis=0).astype(
-        jnp.float32
-    )
-    input_share = share_of(all_rows)
+    token_rows = jnp.concatenate([prompt_in[0], cont_in[0].reshape(cont_rows, width)], axis=0)
+    all_rows = token_rows.astype(jnp.float32)
+    input_share = share_of(token_rows).astype(jnp.float32)
     within = jnp.arange(cont_rows, dtype=jnp.int32) % CONT_LENGTH
     positions = jnp.concatenate(
         [ctx_index * own_rows + jnp.arange(own_rows, dtype=jnp.int32), token_length + within]
@@ -508,21 +529,41 @@
             values.astype(jnp.bfloat16), ("dp", "ctx"), scatter_dimension=0, tiled=True
         )
 
+    streams = (0, 1)
+    half_rows = share_rows // len(streams)
+
+    def half(values, stream):
+        return values[stream * half_rows : (stream + 1) * half_rows]
+
     fillers = [
-        lambda: jnp.einsum("rd,rf->df", act_b, grad_gate_act, preferred_element_type=jnp.float32),
-        lambda: jnp.einsum("rd,rf->df", act_b, grad_up_act, preferred_element_type=jnp.float32),
-        lambda: jnp.einsum("rf,rd->df", hidden_act, grad_mlp, preferred_element_type=jnp.float32),
+        lambda act, hidden: jnp.einsum(
+            "rd,rf->df", act, grad_gate_act, preferred_element_type=jnp.float32
+        ),
+        lambda act, hidden: jnp.einsum(
+            "rd,rf->df", act, grad_up_act, preferred_element_type=jnp.float32
+        ),
+        lambda act, hidden: jnp.einsum(
+            "rf,rd->df", hidden, grad_mlp, preferred_element_type=jnp.float32
+        ),
     ]
+
+    def half_part(parts, stream):
+        return slot_part([half(part, stream) for part in parts])
+
     filled = []
-    state = None
+    states = [None, None]
     for distance in range(count - 1, 0, -1):
-        state = sum_step(state, slot_part(part_list), distance, count)
+        states, part_list, (act_b, hidden_act) = stream_step(
+            states, part_list, half_part, distance, count, (act_b, hidden_act)
+        )
         if fillers:
-            filled.append(fillers.pop(0)().astype(jnp.bfloat16))
-            state, filled[-1] = tied(state, filled[-1])
-    filled.extend(filler().astype(jnp.bfloat16) for filler in fillers)
+            filled.append(fillers.pop(0)(act_b, hidden_act).astype(jnp.bfloat16))
+            states[1], filled[-1] = tied(states[1], filled[-1])
+    filled.extend(filler(act_b, hidden_act).astype(jnp.bfloat16) for filler in fillers)
     gate_sum, up_sum, down_sum = (over_tokens(product) for product in filled)
-    normed_share = sum_end(state, slot_part(part_list))
+    normed_share = jnp.concatenate(
+        [sum_end(states[stream], half_part(part_list, stream)) for stream in streams], axis=0
+    )
     through_mlp, gain_mlp_part = norm_back(hidden_share, gain_mlp, normed_share)
     res_share = share_of(upstream).astype(jnp.float32) + through_mlp
     grad_attn_share = (branch_scale * res_share).astype(jnp.bfloat16)
@@ -583,9 +624,6 @@
     mlp_share = sum_end(mlp_state, slot_part(mlp_parts))
     result_share = (hidden_share + branch_scale * mlp_share).astype(jnp.bfloat16)
     grad_attn = jnp.concatenate(slots_from(arrived), axis=0)
-    grad_out = jnp.einsum(
-        "rq,rd->dq", slot_order(mixed_heads), grad_attn, preferred_element_type=jnp.float32
-    )
     query_grad_rows = jnp.concatenate(
         [
             jnp.concatenate([piece_grads[head, True][0], piece_grads[head, False][0]], axis=1)
@@ -593,6 +631,7 @@
         ],
         axis=0,
     )
+    query_grad_rows, result_share = tied(query_grad_rows, result_share)
     prompt_pairs_grad = jnp.concatenate(
         [
             piece_grads[head, True][which] + piece_grads[head, False][which]
@@ -622,9 +661,6 @@
     grad_query_lin = rotate(query_grad_rows, cos_table, -sin_table).astype(jnp.bfloat16)
     grad_key_lin = rotate(key_grad_rows.T, cos_table, -sin_table).astype(jnp.bfloat16)
     grad_value_lin = value_grad_rows.astype(jnp.bfloat16)
-    grad_query = jnp.einsum("rd,qr->dq", act_a, grad_query_lin, preferred_element_type=jnp.float32)
-    grad_key = jnp.einsum("rd,qr->dq", act_a, grad_key_lin, preferred_element_type=jnp.float32)
-    grad_value = jnp.einsum("rd,rq->dq", act_a, grad_value_lin, preferred_element_type=jnp.float32)
     input_grad = (
         jnp.einsum("qr,dq->rd", grad_query_lin, w_query, preferred_element_type=jnp.float32)
         + jnp.einsum("qr,dq->rd", grad_key_lin, key_weight, preferred_element_type=jnp.float32)
@@ -632,47 +668,72 @@
     )
     input_part = input_grad.astype(jnp.bfloat16)
 
-    def row_part(distance):
-        place = jnp.clip(me + distance, 0, count - 1) * share_rows
-        return lax.dynamic_slice_in_dim(input_part, place, share_rows, 0)
-
-    state = None
+    def row_part(rows, stream):
+        def part_at(distance):
+            place = jnp.clip(me + distance, 0, count - 1) * share_rows + stream * half_rows
+            return lax.dynamic_slice_in_dim(rows, place, half_rows, 0)
+
+        return part_at
+
+    states = [None, None]
     forward, backward = hop_step(result_share, result_share, 1, count)
     forward, backward, input_part, gate_sum, up_sum = tied(
         forward, backward, input_part, gate_sum, up_sum
     )
     result_arrived = {0: result_share, -1: forward, 1: backward}
     for distance in range(count - 1, 0, -1):
-        state = sum_step(state, row_part, distance, count)
+        states, input_part, _ = stream_step(states, input_part, row_part, distance, count)
         step = count - distance + 1
         if step < count:
             forward, backward = hop_step(forward, backward, step, count)
-            state, forward, backward, down_sum = tied(state, forward, backward, down_sum)
+            states[1], forward, backward, down_sum = tied(states[1], forward, backward, down_sum)
+            if step == 2:
+                states[0], act_a, mixed_heads, grad_attn = tied(
+                    states[0], act_a, mixed_heads, grad_attn
+                )
             result_arrived[-step], result_arrived[step] = (forward, backward)
-    input_grad_share = sum_end(state, row_part)
+
+    grad_query = jnp.einsum("rd,qr->dq", act_a, grad_query_lin, preferred_element_type=jnp.float32)
+    grad_key = jnp.einsum("rd,qr->dq", act_a, grad_key_lin, preferred_element_type=jnp.float32)
+    grad_value = jnp.einsum("rd,rq->dq", act_a, grad_value_lin, preferred_element_type=jnp.float32)
+    grad_out = jnp.einsum(
+        "rq,rd->dq", slot_order(mixed_heads), grad_attn, preferred_element_type=jnp.float32
+    )
 
     def rows_from(arrived):
-        chunks = [picked(me, arrived, {i: c - i for i in range(count)}) for c in range(count)]
+        chunks = [
+            picked(me, stream, {i: c - i for i in range(count)})
+            for c in range(count)
+            for stream in arrived
+        ]
         gathered = jnp.concatenate(chunks, axis=0)
         return (
             gathered[:own_rows][None],
             gathered[own_rows:].reshape(1, cont_count, CONT_LENGTH, width),
         )
 
-    prompt_out, cont_out = rows_from(result_arrived)
-    through_attn, gain_attn_part = norm_back(input_share, gain_attn, input_grad_share)
-    grad_share = (res_share + through_attn).astype(jnp.bfloat16)
-    forward, backward = (grad_share, grad_share)
-    arrived = {0: grad_share}
+    prompt_out, cont_out = rows_from([result_arrived])
+    travelling = []
+    arrived = []
+    gain_attn_part = 0.0
+    for stream in streams:
+        through_attn, gain_half = norm_back(
+            half(input_share, stream), gain_attn, sum_end(states[stream], row_part(input_part, stream))
+        )
+        gain_attn_part = gain_attn_part + gain_half
+        grad_share = (half(res_share, stream) + through_attn).astype(jnp.bfloat16)
+        travelling.append((grad_share, grad_share))
+        arrived.append({0: grad_share})
     gain_parts = jnp.stack([gain_attn_part, gain_mlp_part])
     stages = pair_stages()
     per_hop = -(-len(stages) // (count - 1))
     for step in range(1, count):
-        forward, backward = hop_step(forward, backward, step, count)
+        travelling = [hop_step(*travelling[stream], step, count) for stream in streams]
         for axis, distance in stages[(step - 1) * per_hop : step * per_hop]:
             gain_parts = pair_sum(gain_parts, axis, distance)
-        forward, backward, gain_parts = tied(forward, backward, gain_parts)
-        arrived[-step], arrived[step] = (forward, backward)
+        *travelling[1], gain_parts = tied(*travelling[1], gain_parts)
+        for stream in streams:
+            arrived[stream][-step], arrived[stream][step] = travelling[stream]
     prompt_grad, cont_grad = rows_from(arrived)
     gain_rows = width // (lax.axis_size("dp") * lax.axis_size("ctx"))
     gain_place = (lax.axis_index("dp") * lax.axis_size("ctx") + ctx_index) * gain_rows

time: 746 us -> 749 us (level)
  waiting for transfers between devices: 155 us -> 93.4 us
  starting transfers between devices: 142 us -> 189 us
  matrix products: 186 us -> 196 us
  other arithmetic: 107 us -> 117 us
    ppermute x0 -> x24, starting transfers between devices: none -> 77.5 us  [the longest x12 62.1 us: stream_step(): lax.ppermute(to_right, 'tensor', [(i, i + 1) for i in range(0, count - di...]
    ppermute x9 -> x3, waiting for transfers between devices: 59.7 us -> 2.89 us  [sum_step(): lax.ppermute(to_right, 'tensor', [(i, i + 1) for i in range(0, count - di...]
    ppermute x9 -> x3, starting transfers between devices: 47.9 us -> 22.2 us  [sum_step(): lax.ppermute(to_right, 'tensor', [(i, i + 1) for i in range(0, count - di...]
    ppermute x0 -> x24, waiting for transfers between devices: none -> 23.7 us  [the longest x12 18.5 us: stream_step(): lax.ppermute(to_right, 'tensor', [(i, i + 1) for i in range(0, count - di...]
    ppermute x5, waiting for transfers between devices: 23.1 us -> 4.66 us  [pair_sum(): lax.ppermute(values, axis, [(i, i ^ distance) for i in range(lax.axis_siz...]
    ppermute x12 -> x15, starting transfers between devices: 32.7 us -> 43.5 us  [hop_step(): lax.ppermute(forward, 'tensor', [(i, i + 1) for i in range(step - 1, coun...]
    ppermute x9 -> x3, waiting for transfers between devices: 10.1 us -> 0.01 us  [sum_step(): lax.ppermute(to_left, 'tensor', [(i, i - 1) for i in range(distance, coun...]
    ppermute x9 -> x3, starting transfers between devices: 14 us -> 4.74 us  [sum_step(): lax.ppermute(to_left, 'tensor', [(i, i - 1) for i in range(distance, coun...]
  transfers between devices with their start and end apart: 62 -> 80, of which waited for: 27 -> 23; matrix products, arithmetic and copies ran while one was open for 40% -> 41% of each run, Pallas kernels for 8% -> 8%
where the time goes in v6:
time: 749 us; the launch traced here: 742 us
  matrix products  196 us (26%)
  starting transfers between devices  189 us (25%)
  other arithmetic  117 us (16%)
  waiting for transfers between devices  93.4 us (12%)
  local copies, waits for them, and re-layouts  69.5 us (9%)
  Pallas kernels  58.2 us (8%)
  between operations  17 us (2%)
    ppermute x12, starting transfers between devices, stream_step(): lax.ppermute(to_right, 'tensor', [(i, i + 1) for i in range(0, count - di...  62.1 us
    pallas_call x8, Pallas kernels, attention_call(): pl.pallas_call(kernel, out_shape=[out for _, out in outs], grid_spec=pltp...  58.2 us
    ppermute x15, waiting for transfers between devices, hop_step(): lax.ppermute(backward, 'tensor', [(i, i - 1) for i in range(1, count - st...  48 us
    ppermute x15, starting transfers between devices, hop_step(): lax.ppermute(forward, 'tensor', [(i, i + 1) for i in range(step - 1, coun...  43.5 us
    unnamed x255, local copies, waits for them, and re-layouts  40.1 us
    convert_element_type x10, other arithmetic, added(): (first.astype(jnp.float32) + second.astype(jnp.float32)).astype(jnp.bfloa...  28.7 us
    dot_general x4, matrix products, shards(): jnp.einsum('rf,df->rd', grad_up_slot, w_up, preferred_element_type=jnp.fl...  25.9 us
    dot_general x4, matrix products, shards(): up_proj = jnp.dot(act_b_slots[s], w_up, preferred_element_type=jnp.float32)  24.5 us
  transfers between devices with their start and end apart: 80, of which 23 were waited for; matrix products, arithmetic and copies ran while one was open for 41% of the time, Pallas kernels for 8%

profile of v6, /device:TPU:0, one launch (start us, length us, event | category | flops | bytes accessed | tf_op | source)
XLA Modules:
  0.0 742.4 jit_solution(3652457281001352000)
XLA Ops:
  14.4 6.4 fusion.2
  83.0 11.1 %fusion.71 = f32[1024,2048]{1,0:T(8,128)} fusion(bf16[1024,2048]{1,0:T(8,128)(2,1)S(1)} %pad_maximum_fusion.3, bf16[2048,2048]{1,0:T(8,128)(2,1)S(1)} %bitcast.212), kind=kOutput, calls=%fused_computation.276 | convolution fusion | flops 8589934592 | bytes 20971520 | tf_op jit(solution)/shard_map/rd,fd->rf/dot_general | solution.py:481
  110.7 6.5 all-gather.2.cloned.1.call-done
  117.2 6.7 multiply_reduce_fusion.2
  145.0 6.7 fusion.18
  169.6 6.7 fusion.19
  176.4 6.7 collective-permute-done.9
  198.8 6.7 fusion.20
  210.1 7.3 fusion.78
  238.3 11.6 %convolution_convert_fusion.2 = bf16[2048,2048]{1,0:T(8,128)(2,1)} fusion(bf16[1024,2048]{1,0:T(8,128)(2,1)S(1)} %pad_maximum_fusion.4, bf16[256,2048]{1,0:T(8,128)(2,1)S(1)} %copy-done.114, bf16[256,2048]{1,0:T(8,128)(2,1)S(1)} %copy-done.112, bf16[256,2048]{1,0:T(8,128)(2,1)S(1)} %copy-done.110, bf16[256,2048]{1,0:T(8,128)(2,1)S(1)} %copy-done.108), kind=kOutput, calls=%fused_computation.9 | convolution fusion | flops 8610906112 | bytes 16777216 | tf_op jit(solution)/shard_map/rd,rf->df/dot_general | solution.py:539
  252.5 8.3 %collective-permute-done.12 = bf16[128,2048]{1,0:T(8,128)(2,1)S(1)} collective-permute-done((bf16[128,2048]{1,0:T(8,128)(2,1)}, bf16[128,2048]{1,0:T(8,128)(2,1)S(1)}, u32[]{:S(2)}, u32[]{:S(2)}) %collective-permute-start.12) | collective-permute-done | bytes 524320 | tf_op jit(solution)/shard_map/ppermute | solution.py:308
  272.7 13.3 %convolution_convert_fusion.1 = bf16[2048,2048]{1,0:T(8,128)(2,1)} fusion(bf16[1024,2048]{1,0:T(8,128)(2,1)S(1)} %copy-done.70, bf16[256,2048]{1,0:T(8,128)(2,1)} %copy-done.106, bf16[256,2048]{1,0:T(8,128)(2,1)} %copy-done.105, bf16[256,2048]{1,0:T(8,128)(2,1)S(1)} %copy-done.104, bf16[256,2048]{1,0:T(8,128)(2,1)S(1)} %copy-done.102), kind=kOutput, calls=%fused_computation.8 | convolution fusion | flops 8610906112 | bytes 16777216 | tf_op jit(solution)/shard_map/rd,rf->df/dot_general | solution.py:542
  298.1 8.8 %collective-permute-start.20 = (bf16[128,2048]{1,0:T(8,128)(2,1)}, bf16[128,2048]{1,0:T(8,128)(2,1)}, u32[]{:S(2)}, u32[]{:S(2)}) collective-permute-start(bf16[128,2048]{1,0:T(8,128)(2,1)} %get-tuple-element.274), channel_id=1, source_target_pairs={{0,1},{1,2},{2,3},{4,5},{5,6},{6,7},{8,9},{9,10},{10,11},{12,13},{... | collective-permute-start | bytes 1572872 | tf_op jit(solution)/shard_map/ppermute | solution.py:308
  317.7 14.1 %convolution_convert_fusion = bf16[2048,2048]{1,0:T(8,128)(2,1)} fusion(bf16[1024,2048]{1,0:T(8,128)(2,1)S(1)} %copy-done.67, bf16[1024,2048]{1,0:T(8,128)(2,1)} %pad_maximum_fusion.5), kind=kOutput, calls=%fused_computation.7 | convolution fusion | flops 8594128896 | bytes 16777216 | tf_op jit(solution)/shard_map/rf,rd->df/dot_general | solution.py:545
  350.5 10.6 %convolution_convert_fusion.3 = bf16[1024,2048]{1,0:T(8,128)(2,1)} fusion(bf16[1024,2048]{1,0:T(8,128)(2,1)S(1)} %copy-done.68, bf16[2048,2048]{1,0:T(8,128)(2,1)S(1)} %bitcast.214), kind=kOutput, calls=%fused_computation.35 | convolution fusion | flops 8592031744 | bytes 16777216 | tf_op jit(solution)/shard_map/dot_general | solution.py:584
  365.9 8.2 %collective-permute-start.27 = (bf16[256,2048]{1,0:T(8,128)(2,1)}, bf16[256,2048]{1,0:T(8,128)(2,1)}, u32[]{:S(2)}, u32[]{:S(2)}) collective-permute-start(bf16[256,2048]{1,0:T(8,128)(2,1)} %get-tuple-element.283), channel_id=1, source_target_pairs={{0,1},{1,2},{2,3},{4,5},{5,6},{6,7},{8,9},{9,10},{10,11},{12,13},{... | collective-permute-start | bytes 3145736 | tf_op jit(solution)/shard_map/ppermute | solution.py:272
  378.8 9.1 %shard_map.241 = (f32[256,512]{1,0:T(8,128)S(1)}, f32[1024,64]{1,0:T(8,128)S(1)}, f32[1024,64]{1,0:T(8,128)S(1)}) custom-call(s32[2]{0:T(128)S(1)} %pad_add_fusion.meta_ref, bf16[256,512]{1,0:T(8,128)(2,1)S(1)} %copy-done.32, bf16[256,512]{1,0:T(8,128)(2,1)S(1)} %copy-done.36, f32[4,1,512]{2,1,0:T(1,128)S(1)} %copy-done.47, bf16[1024,64]{1,0:T(8,128)(2,1)S(1)} %copy-done.20, ...), custom_call_target="tpu_custom_call" | custom-call | flops 1342177280 | bytes 1052672 | tf_op jit(solution)/shard_map/pallas_call | solution.py:183
  399.2 9.0 %collective-permute-start.31 = (bf16[256,2048]{1,0:T(8,128)(2,1)}, bf16[256,2048]{1,0:T(8,128)(2,1)}, u32[]{:S(2)}, u32[]{:S(2)}) collective-permute-start(bf16[256,2048]{1,0:T(8,128)(2,1)} %get-tuple-element.307), channel_id=1, source_target_pairs={{0,1},{4,5},{8,9},{12,13},{16,17},{20,21},{24,25},{28,29}} | collective-permute-start | bytes 3145736 | tf_op jit(solution)/shard_map/ppermute | solution.py:288
  417.3 9.6 %shard_map.242 = (f32[256,512]{1,0:T(8,128)S(1)}, f32[1024,64]{1,0:T(8,128)S(1)}, f32[1024,64]{1,0:T(8,128)S(1)}, f32[512,64]{1,0:T(8,128)S(1)}, f32[512,64]{1,0:T(8,128)S(1)}) custom-call(s32[2]{0:T(128)S(1)} %pad_add_fusion.meta_ref, bf16[256,512]{1,0:T(8,128)(2,1)S(1)} %copy-done.30, bf16[256,512]{1,0:T(8,128)(2,1)S(1)} %copy-done.35, ...), custom_call_target="tpu_custom_call" | custom-call | flops 1509949440 | bytes 1052672 | tf_op jit(solution)/shard_map/pallas_call | solution.py:183
  439.4 6.2 collective-permute-start.35
  449.6 9.3 %shard_map.243 = (f32[256,512]{1,0:T(8,128)S(1)}, f32[1024,64]{1,0:T(8,128)S(1)}, f32[1024,64]{1,0:T(8,128)S(1)}) custom-call(s32[2]{0:T(128)S(1)} %pad_add_fusion.meta_ref, bf16[256,512]{1,0:T(8,128)(2,1)S(1)} %copy-done.28, bf16[256,512]{1,0:T(8,128)(2,1)S(1)} %copy-done.34, f32[4,1,512]{2,1,0:T(1,128)S(1)} %get-tuple-element.312.total_ref, ...), custom_call_target="tpu_custom_call" | custom-call | flops 1342177280 | bytes 1052672 | tf_op jit(solution)/shard_map/pallas_call | solution.py:183
  469.4 7.1 collective-permute-start.37
  483.4 9.7 %shard_map.244 = (f32[256,512]{1,0:T(8,128)S(1)}, f32[1024,64]{1,0:T(8,128)S(1)}, f32[1024,64]{1,0:T(8,128)S(1)}, f32[512,64]{1,0:T(8,128)S(1)}, f32[512,64]{1,0:T(8,128)S(1)}) custom-call(s32[2]{0:T(128)S(1)} %pad_add_fusion.meta_ref, bf16[256,512]{1,0:T(8,128)(2,1)S(1)} %copy-done.26, bf16[256,512]{1,0:T(8,128)(2,1)S(1)} %copy-done.33, ...), custom_call_target="tpu_custom_call" | custom-call | flops 1509949440 | bytes 1052672 | tf_op jit(solution)/shard_map/pallas_call | solution.py:183
  523.9 6.8 add_convert_fusion
  550.8 6.1 collective-permute-start.52
  587.8 6.2 collective-permute-start.48
  598.5 11.2 %collective-permute-start.54 = (bf16[128,2048]{1,0:T(8,128)(2,1)}, bf16[128,2048]{1,0:T(8,128)(2,1)}, u32[]{:S(2)}, u32[]{:S(2)}) collective-permute-start(bf16[128,2048]{1,0:T(8,128)(2,1)} %get-tuple-element.382), channel_id=1, source_target_pairs={{0,1},{1,2},{2,3},{4,5},{5,6},{6,7},{8,9},{9,10},{10,11},{12,13},{... | collective-permute-start | bytes 1572872 | tf_op jit(solution)/shard_map/ppermute | solution.py:308
  613.9 7.2 collective-permute-start.59
  641.0 6.1 collective-permute-start.61
  684.3 8.5 %collective-permute-done.66 = bf16[128,2048]{1,0:T(8,128)(2,1)} collective-permute-done((bf16[128,2048]{1,0:T(8,128)(2,1)}, bf16[128,2048]{1,0:T(8,128)(2,1)}, u32[]{:S(2)}, u32[]{:S(2)}) %collective-permute-start.66) | collective-permute-done | bytes 524320 | tf_op jit(solution)/shard_map/ppermute | solution.py:273
  706.1 9.2 %collective-permute-done.70 = bf16[128,2048]{1,0:T(8,128)(2,1)} collective-permute-done((bf16[128,2048]{1,0:T(8,128)(2,1)}, bf16[128,2048]{1,0:T(8,128)(2,1)}, u32[]{:S(2)}, u32[]{:S(2)}) %collective-permute-start.70) | collective-permute-done | bytes 524320 | tf_op jit(solution)/shard_map/ppermute | solution.py:273
  718.0 6.5 collective-permute-done.74
  (561 shorter events, 458.0 us)
Async XLA Ops:
  7.2 110.0 %all-gather.2.cloned.1.call-start = ((), (), s32[]{:S(2)}) async-start(), calls=%async_computation.4 | async-start | bytes 9437184 | tf_op jit(solution)/shard_map/all_gather | solution.py:416
  9.7 521.0 %reduce-scatter.5.cloned.1.call-start = ((), (), s32[]{:S(2)}) async-start(), calls=%async_computation.5 | async-start | bytes 9437184 | tf_op jit(solution)/shard_map/reduce_scatter | solution.py:528
  54.0 40.1 %collective-permute-start.5 = (bf16[256,256]{0,1:T(8,128)(2,1)}, bf16[256,256]{0,1:T(8,128)(2,1)}, u32[]{:S(2)}, u32[]{:S(2)}) collective-permute-start(bf16[256,256]{0,1:T(8,128)(2,1)} %get-tuple-element.543), channel_id=1, source_target_pairs={{0,1},{1,2},{2,3},{3,0},{4,5},{5,6},{6,7},{7,4},{8,9},{9,10},{10,1... | collective-permute-start | bytes 393224 | tf_op jit(solution)/shard_map/ppermute | solution.py:326
  56.5 44.2 %collective-permute-start.4 = (bf16[256,256]{0,1:T(8,128)(2,1)}, bf16[256,256]{0,1:T(8,128)(2,1)}, u32[]{:S(2)}, u32[]{:S(2)}) collective-permute-start(bf16[256,256]{0,1:T(8,128)(2,1)} %get-tuple-element.544), channel_id=1, source_target_pairs={{0,2},{1,3},{2,0},{3,1},{4,6},{5,7},{6,4},{7,5},{8,10},{9,11},{10,... | collective-permute-start | bytes 393224 | tf_op jit(solution)/shard_map/ppermute | solution.py:326
  59.1 41.6 %collective-permute-start.3 = (bf16[256,256]{0,1:T(8,128)(2,1)}, bf16[256,256]{0,1:T(8,128)(2,1)}, u32[]{:S(2)}, u32[]{:S(2)}) collective-permute-start(bf16[256,256]{0,1:T(8,128)(2,1)} %get-tuple-element.545), channel_id=1, source_target_pairs={{0,3},{1,0},{2,1},{3,2},{4,7},{5,4},{6,5},{7,6},{8,11},{9,8},{10,9... | collective-permute-start | bytes 393224 | tf_op jit(solution)/shard_map/ppermute | solution.py:326
  74.6 27.5 %collective-permute-start.1 = (bf16[256,256]{0,1:T(8,128)(2,1)}, bf16[256,256]{0,1:T(8,128)(2,1)S(1)}, u32[]{:S(2)}, u32[]{:S(2)}) collective-permute-start(bf16[256,256]{0,1:T(8,128)(2,1)} %get-tuple-element.547), channel_id=1, source_target_pairs={{0,2},{1,3},{2,0},{3,1},{4,6},{5,7},{6,4},{7,5},{8,10},{9,11},{10,... | collective-permute-start | bytes 393224 | tf_op jit(solution)/shard_map/ppermute | solution.py:326
  125.5 27.5 %collective-permute-start.7 = (bf16[256,2048]{1,0:T(8,128)(2,1)S(1)}, bf16[256,2048]{1,0:T(8,128)(2,1)S(1)}, u32[]{:S(2)}, u32[]{:S(2)}) collective-permute-start(bf16[256,2048]{1,0:T(8,128)(2,1)S(1)} %multiply_convert_fusion.14), channel_id=1, source_target_pairs={{1,0},{2,1},{3,2},{5,4},{6,5},{7,6},{9,8},{10,9},{11,10},{13,12},{... | collective-permute-start | bytes 3145736 | tf_op jit(solution)/shard_map/ppermute | solution.py:273
  127.1 27.1 %collective-permute-start.6 = (bf16[256,2048]{1,0:T(8,128)(2,1)S(1)}, bf16[256,2048]{1,0:T(8,128)(2,1)S(1)}, u32[]{:S(2)}, u32[]{:S(2)}) collective-permute-start(bf16[256,2048]{1,0:T(8,128)(2,1)S(1)} %multiply_convert_fusion.14), channel_id=1, source_target_pairs={{0,1},{1,2},{2,3},{4,5},{5,6},{6,7},{8,9},{9,10},{10,11},{12,13},{... | collective-permute-start | bytes 3145736 | tf_op jit(solution)/shard_map/ppermute | solution.py:272
  154.9 28.2 %collective-permute-start.9 = (bf16[256,2048]{1,0:T(8,128)(2,1)S(1)}, bf16[256,2048]{1,0:T(8,128)(2,1)S(1)}, u32[]{:S(2)}, u32[]{:S(2)}) collective-permute-start(bf16[256,2048]{1,0:T(8,128)(2,1)S(1)} %collective-permute-done.7), channel_id=1, source_target_pairs={{1,0},{2,1},{5,4},{6,5},{9,8},{10,9},{13,12},{14,13},{17,16},{18,1... | collective-permute-start | bytes 3145736 | tf_op jit(solution)/shard_map/ppermute | solution.py:273
  250.0 280.8 %reduce-scatter.7.cloned.1.call-start = ((), (), s32[]{:S(2)}) async-start(), calls=%async_computation.6 | async-start | bytes 9437184 | tf_op jit(solution)/shard_map/reduce_scatter | solution.py:528
  286.0 288.1 %reduce-scatter.9.cloned.1.call-start = ((), (), s32[]{:S(2)}) async-start(), calls=%async_computation.7 | async-start | bytes 9437184 | tf_op jit(solution)/shard_map/reduce_scatter | solution.py:528
  298.1 33.8 %collective-permute-start.20 = (bf16[128,2048]{1,0:T(8,128)(2,1)}, bf16[128,2048]{1,0:T(8,128)(2,1)}, u32[]{:S(2)}, u32[]{:S(2)}) collective-permute-start(bf16[128,2048]{1,0:T(8,128)(2,1)} %get-tuple-element.274), channel_id=1, source_target_pairs={{0,1},{1,2},{2,3},{4,5},{5,6},{6,7},{8,9},{9,10},{10,11},{12,13},{... | collective-permute-start | bytes 1572872 | tf_op jit(solution)/shard_map/ppermute | solution.py:308
  364.5 29.0 %collective-permute-start.28 = (bf16[256,2048]{1,0:T(8,128)(2,1)}, bf16[256,2048]{1,0:T(8,128)(2,1)}, u32[]{:S(2)}, u32[]{:S(2)}) collective-permute-start(bf16[256,2048]{1,0:T(8,128)(2,1)} %get-tuple-element.283), channel_id=1, source_target_pairs={{1,0},{2,1},{3,2},{5,4},{6,5},{7,6},{9,8},{10,9},{11,10},{13,12},{... | collective-permute-start | bytes 3145736 | tf_op jit(solution)/shard_map/ppermute | solution.py:273
  365.9 28.8 %collective-permute-start.27 = (bf16[256,2048]{1,0:T(8,128)(2,1)}, bf16[256,2048]{1,0:T(8,128)(2,1)}, u32[]{:S(2)}, u32[]{:S(2)}) collective-permute-start(bf16[256,2048]{1,0:T(8,128)(2,1)} %get-tuple-element.283), channel_id=1, source_target_pairs={{0,1},{1,2},{2,3},{4,5},{5,6},{6,7},{8,9},{9,10},{10,11},{12,13},{... | collective-permute-start | bytes 3145736 | tf_op jit(solution)/shard_map/ppermute | solution.py:272
  374.1 355.1 %reduce-scatter.11.cloned.1.call-start = ((), (), s32[]{:S(2)}) async-start(), calls=%async_computation.8 | async-start | bytes 5898240 | tf_op jit(solution)/shard_map/reduce_scatter | solution.py:741
  394.7 36.1 %collective-permute-start.29 = (bf16[256,2048]{1,0:T(8,128)(2,1)}, bf16[256,2048]{1,0:T(8,128)(2,1)}, u32[]{:S(2)}, u32[]{:S(2)}) collective-permute-start(bf16[256,2048]{1,0:T(8,128)(2,1)} %collective-permute-done.27), channel_id=1, source_target_pairs={{1,2},{2,3},{5,6},{6,7},{9,10},{10,11},{13,14},{14,15},{17,18},{18... | collective-permute-start | bytes 3145736 | tf_op jit(solution)/shard_map/ppermute | solution.py:272
  396.3 34.5 %collective-permute-start.30 = (bf16[256,2048]{1,0:T(8,128)(2,1)}, bf16[256,2048]{1,0:T(8,128)(2,1)}, u32[]{:S(2)}, u32[]{:S(2)}) collective-permute-start(bf16[256,2048]{1,0:T(8,128)(2,1)} %collective-permute-done.28), channel_id=1, source_target_pairs={{1,0},{2,1},{5,4},{6,5},{9,8},{10,9},{13,12},{14,13},{17,16},{18,1... | collective-permute-start | bytes 3145736 | tf_op jit(solution)/shard_map/ppermute | solution.py:273
  397.6 33.2 %collective-permute-start.32 = (bf16[256,2048]{1,0:T(8,128)(2,1)}, bf16[256,2048]{1,0:T(8,128)(2,1)}, u32[]{:S(2)}, u32[]{:S(2)}) collective-permute-start(bf16[256,2048]{1,0:T(8,128)(2,1)} %get-tuple-element.307), channel_id=1, source_target_pairs={{3,2},{7,6},{11,10},{15,14},{19,18},{23,22},{27,26},{31,30}} | collective-permute-start | bytes 3145736 | tf_op jit(solution)/shard_map/ppermute | solution.py:289
  399.2 31.5 %collective-permute-start.31 = (bf16[256,2048]{1,0:T(8,128)(2,1)}, bf16[256,2048]{1,0:T(8,128)(2,1)}, u32[]{:S(2)}, u32[]{:S(2)}) collective-permute-start(bf16[256,2048]{1,0:T(8,128)(2,1)} %get-tuple-element.307), channel_id=1, source_target_pairs={{0,1},{4,5},{8,9},{12,13},{16,17},{20,21},{24,25},{28,29}} | collective-permute-start | bytes 3145736 | tf_op jit(solution)/shard_map/ppermute | solution.py:288
  430.8 30.5 %collective-permute-start.33 = (bf16[256,2048]{1,0:T(8,128)(2,1)}, bf16[256,2048]{1,0:T(8,128)(2,1)}, u32[]{:S(2)}, u32[]{:S(2)}) collective-permute-start(bf16[256,2048]{1,0:T(8,128)(2,1)} %collective-permute-done.29), channel_id=1, source_target_pairs={{2,3},{6,7},{10,11},{14,15},{18,19},{22,23},{26,27},{30,31}} | collective-permute-start | bytes 3145736 | tf_op jit(solution)/shard_map/ppermute | solution.py:272
  432.4 28.9 %collective-permute-start.34 = (bf16[256,2048]{1,0:T(8,128)(2,1)}, bf16[256,2048]{1,0:T(8,128)(2,1)}, u32[]{:S(2)}, u32[]{:S(2)}) collective-permute-start(bf16[256,2048]{1,0:T(8,128)(2,1)} %collective-permute-done.30), channel_id=1, source_target_pairs={{1,0},{5,4},{9,8},{13,12},{17,16},{21,20},{25,24},{29,28}} | collective-permute-start | bytes 3145736 | tf_op jit(solution)/shard_map/ppermute | solution.py:273
  468.0 29.2 %collective-permute-start.38 = (bf16[256,2048]{1,0:T(8,128)(2,1)}, bf16[256,2048]{1,0:T(8,128)(2,1)}, u32[]{:S(2)}, u32[]{:S(2)}) collective-permute-start(bf16[256,2048]{1,0:T(8,128)(2,1)} %get-tuple-element.506), channel_id=1, source_target_pairs={{1,0},{2,1},{3,2},{5,4},{6,5},{7,6},{9,8},{10,9},{11,10},{13,12},{... | collective-permute-start | bytes 3145736 | tf_op jit(solution)/shard_map/ppermute | solution.py:289
  469.4 27.8 %collective-permute-start.37 = (bf16[256,2048]{1,0:T(8,128)(2,1)}, bf16[256,2048]{1,0:T(8,128)(2,1)}, u32[]{:S(2)}, u32[]{:S(2)}) collective-permute-start(bf16[256,2048]{1,0:T(8,128)(2,1)} %get-tuple-element.507), channel_id=1, source_target_pairs={{0,1},{1,2},{2,3},{4,5},{5,6},{6,7},{8,9},{9,10},{10,11},{12,13},{... | collective-permute-start | bytes 3145736 | tf_op jit(solution)/shard_map/ppermute | solution.py:288
  501.4 29.3 %collective-permute-start.40 = (bf16[256,2048]{1,0:T(8,128)(2,1)S(1)}, bf16[256,2048]{1,0:T(8,128)(2,1)}, u32[]{:S(2)}, u32[]{:S(2)}) collective-permute-start(bf16[256,2048]{1,0:T(8,128)(2,1)S(1)} %add_convert_fusion.1), channel_id=1, source_target_pairs={{1,0},{2,1},{3,2},{5,4},{6,5},{7,6},{9,8},{10,9},{11,10},{13,12},{... | collective-permute-start | bytes 3145736 | tf_op jit(solution)/shard_map/ppermute | solution.py:273
  502.8 27.9 %collective-permute-start.39 = (bf16[256,2048]{1,0:T(8,128)(2,1)S(1)}, bf16[256,2048]{1,0:T(8,128)(2,1)}, u32[]{:S(2)}, u32[]{:S(2)}) collective-permute-start(bf16[256,2048]{1,0:T(8,128)(2,1)S(1)} %add_convert_fusion.1), channel_id=1, source_target_pairs={{0,1},{1,2},{2,3},{4,5},{5,6},{6,7},{8,9},{9,10},{10,11},{12,13},{... | collective-permute-start | bytes 3145736 | tf_op jit(solution)/shard_map/ppermute | solution.py:272
  541.0 33.1 %collective-permute-start.44 = (bf16[128,2048]{1,0:T(8,128)(2,1)}, bf16[128,2048]{1,0:T(8,128)(2,1)}, u32[]{:S(2)}, u32[]{:S(2)}) collective-permute-start(bf16[128,2048]{1,0:T(8,128)(2,1)} %get-tuple-element.361), channel_id=1, source_target_pairs={{0,1},{4,5},{8,9},{12,13},{16,17},{20,21},{24,25},{28,29}} | collective-permute-start | bytes 1572872 | tf_op jit(solution)/shard_map/ppermute | solution.py:308
  543.2 31.0 %collective-permute-start.45 = (bf16[128,2048]{1,0:T(8,128)(2,1)}, bf16[128,2048]{1,0:T(8,128)(2,1)}, u32[]{:S(2)}, u32[]{:S(2)}) collective-permute-start(bf16[128,2048]{1,0:T(8,128)(2,1)} %get-tuple-element.362), channel_id=1, source_target_pairs={{3,2},{7,6},{11,10},{15,14},{19,18},{23,22},{27,26},{31,30}} | collective-permute-start | bytes 1572872 | tf_op jit(solution)/shard_map/ppermute | solution.py:309
  544.6 29.5 %collective-permute-start.46 = (bf16[256,2048]{1,0:T(8,128)(2,1)}, bf16[256,2048]{1,0:T(8,128)(2,1)}, u32[]{:S(2)}, u32[]{:S(2)}) collective-permute-start(bf16[256,2048]{1,0:T(8,128)(2,1)} %collective-permute-done.39), channel_id=1, source_target_pairs={{1,2},{2,3},{5,6},{6,7},{9,10},{10,11},{13,14},{14,15},{17,18},{18... | collective-permute-start | bytes 3145736 | tf_op jit(solution)/shard_map/ppermute | solution.py:272
  548.1 27.1 %collective-permute-start.47 = (bf16[256,2048]{1,0:T(8,128)(2,1)}, bf16[256,2048]{1,0:T(8,128)(2,1)}, u32[]{:S(2)}, u32[]{:S(2)}) collective-permute-start(bf16[256,2048]{1,0:T(8,128)(2,1)} %collective-permute-done.40), channel_id=1, source_target_pairs={{1,0},{2,1},{5,4},{6,5},{9,8},{10,9},{13,12},{14,13},{17,16},{18,1... | collective-permute-start | bytes 3145736 | tf_op jit(solution)/shard_map/ppermute | solution.py:273
  550.8 43.2 %collective-permute-start.52 = (bf16[128,2048]{1,0:T(8,128)(2,1)}, bf16[128,2048]{1,0:T(8,128)(2,1)}, u32[]{:S(2)}, u32[]{:S(2)}) collective-permute-start(bf16[128,2048]{1,0:T(8,128)(2,1)} %get-tuple-element.376), channel_id=1, source_target_pairs={{0,1},{1,2},{4,5},{5,6},{8,9},{9,10},{12,13},{13,14},{16,17},{17,1... | collective-permute-start | bytes 1572872 | tf_op jit(solution)/shard_map/ppermute | solution.py:308
  575.2 35.8 %collective-permute-start.50 = (bf16[256,2048]{1,0:T(8,128)(2,1)}, bf16[256,2048]{1,0:T(8,128)(2,1)}, u32[]{:S(2)}, u32[]{:S(2)}) collective-permute-start(bf16[256,2048]{1,0:T(8,128)(2,1)} %collective-permute-done.46), channel_id=1, source_target_pairs={{2,3},{6,7},{10,11},{14,15},{18,19},{22,23},{26,27},{30,31}} | collective-permute-start | bytes 3145736 | tf_op jit(solution)/shard_map/ppermute | solution.py:272
  576.8 34.2 %collective-permute-start.51 = (bf16[256,2048]{1,0:T(8,128)(2,1)}, bf16[256,2048]{1,0:T(8,128)(2,1)}, u32[]{:S(2)}, u32[]{:S(2)}) collective-permute-start(bf16[256,2048]{1,0:T(8,128)(2,1)} %collective-permute-done.47), channel_id=1, source_target_pairs={{1,0},{5,4},{9,8},{13,12},{17,16},{21,20},{25,24},{29,28}} | collective-permute-start | bytes 3145736 | tf_op jit(solution)/shard_map/ppermute | solution.py:273
  (171 other events, 1775.6 us)
Sparse Core Ops, SparseCore 0:
  10.2 107.0 all-gather.1
  250.1 69.5 reduce-scatter.4
  323.2 71.5 reduce-scatter.6
  398.1 71.5 reduce-scatter.8
  583.6 55.7 reduce-scatter.10

commit v7 on v6

--- a/solution.py
+++ b/solution.py
@@ -290,7 +290,7 @@
     )
 
 
-def stream_step(states, parts, part_of, distance, count, waiting=()):
+def stream_step(states, parts, part_of, distance, count, waiting):
     moved = []
     for stream, state in enumerate(states):
         part_at = part_of(parts, stream)
@@ -299,10 +299,7 @@
         if state is not None:
             to_right = added(to_right, state[0])
             to_left = added(to_left, state[1])
-        if stream == 0:
-            to_right, to_left, parts, waiting = tied(to_right, to_left, parts, waiting)
-        else:
-            to_right, to_left, parts = tied(to_right, to_left, parts)
+        to_right, to_left, parts, waiting = tied(to_right, to_left, parts, waiting)
         moved.append(
             (
                 lax.ppermute(to_right, "tensor", [(i, i + 1) for i in range(0, count - distance)]),
@@ -331,14 +328,6 @@
     return [
         picked(me, received, {i: (i - source) % count for i in range(count)})
         for source in range(count)
-    ]
-
-
-def pair_stages():
-    return [
-        (axis, 1 << bit)
-        for axis in ("ctx", "tensor", "dp")
-        for bit in range(lax.axis_size(axis).bit_length() - 1)
     ]
 
 
@@ -529,41 +518,21 @@
             values.astype(jnp.bfloat16), ("dp", "ctx"), scatter_dimension=0, tiled=True
         )
 
-    streams = (0, 1)
-    half_rows = share_rows // len(streams)
-
-    def half(values, stream):
-        return values[stream * half_rows : (stream + 1) * half_rows]
-
     fillers = [
-        lambda act, hidden: jnp.einsum(
-            "rd,rf->df", act, grad_gate_act, preferred_element_type=jnp.float32
-        ),
-        lambda act, hidden: jnp.einsum(
-            "rd,rf->df", act, grad_up_act, preferred_element_type=jnp.float32
-        ),
-        lambda act, hidden: jnp.einsum(
-            "rf,rd->df", hidden, grad_mlp, preferred_element_type=jnp.float32
-        ),
+        lambda: jnp.einsum("rd,rf->df", act_b, grad_gate_act, preferred_element_type=jnp.float32),
+        lambda: jnp.einsum("rd,rf->df", act_b, grad_up_act, preferred_element_type=jnp.float32),
+        lambda: jnp.einsum("rf,rd->df", hidden_act, grad_mlp, preferred_element_type=jnp.float32),
     ]
-
-    def half_part(parts, stream):
-        return slot_part([half(part, stream) for part in parts])
-
     filled = []
-    states = [None, None]
+    state = None
     for distance in range(count - 1, 0, -1):
-        states, part_list, (act_b, hidden_act) = stream_step(
-            states, part_list, half_part, distance, count, (act_b, hidden_act)
-        )
+        state = sum_step(state, slot_part(part_list), distance, count)
         if fillers:
-            filled.append(fillers.pop(0)(act_b, hidden_act).astype(jnp.bfloat16))
-            states[1], filled[-1] = tied(states[1], filled[-1])
-    filled.extend(filler(act_b, hidden_act).astype(jnp.bfloat16) for filler in fillers)
+            filled.append(fillers.pop(0)().astype(jnp.bfloat16))
+            state, filled[-1] = tied(state, filled[-1])
+    filled.extend(filler().astype(jnp.bfloat16) for filler in fillers)
     gate_sum, up_sum, down_sum = (over_tokens(product) for product in filled)
-    normed_share = jnp.concatenate(
-        [sum_end(states[stream], half_part(part_list, stream)) for stream in streams], axis=0
-    )
+    normed_share = sum_end(state, slot_part(part_list))
     through_mlp, gain_mlp_part = norm_back(hidden_share, gain_mlp, normed_share)
     res_share = share_of(upstream).astype(jnp.float32) + through_mlp
     grad_attn_share = (branch_scale * res_share).astype(jnp.bfloat16)
@@ -667,6 +636,15 @@
         + jnp.einsum("rq,dq->rd", grad_value_lin, value_weight, preferred_element_type=jnp.float32)
     )
     input_part = input_grad.astype(jnp.bfloat16)
+    streams = (0,)
+    half_rows = share_rows // len(streams)
+
+    def half(values, stream):
+        return values[stream * half_rows : (stream + 1) * half_rows]
+
+    scaled_rows = all_rows * lax.rsqrt(
+        jnp.mean(all_rows * all_rows, axis=-1, keepdims=True) + norm_eps
+    )
 
     def row_part(rows, stream):
         def part_at(distance):
@@ -675,30 +653,41 @@
 
         return part_at
 
-    states = [None, None]
+    states = [None]
     forward, backward = hop_step(result_share, result_share, 1, count)
-    forward, backward, input_part, gate_sum, up_sum = tied(
-        forward, backward, input_part, gate_sum, up_sum
+    forward, backward, input_part, gate_sum, up_sum, input_grad, mixed_heads, grad_attn = tied(
+        forward, backward, input_part, gate_sum, up_sum, input_grad, mixed_heads, grad_attn
     )
     result_arrived = {0: result_share, -1: forward, 1: backward}
     for distance in range(count - 1, 0, -1):
-        states, input_part, _ = stream_step(states, input_part, row_part, distance, count)
+        states, input_part, act_a = stream_step(
+            states, input_part, row_part, distance, count, act_a
+        )
+        if distance == count - 1:
+            gain_attn_part = jnp.sum(input_grad * scaled_rows, axis=0)
+            grad_out = jnp.einsum(
+                "rq,rd->dq", slot_order(mixed_heads), grad_attn, preferred_element_type=jnp.float32
+            )
+            states[0], gain_attn_part, grad_out = tied(
+                states[0], gain_attn_part, grad_out.astype(jnp.bfloat16)
+            )
+        if distance == count - 2:
+            grad_query = jnp.einsum("rd,qr->dq", act_a, grad_query_lin, preferred_element_type=jnp.float32)
+            grad_key = jnp.einsum("rd,qr->dq", act_a, grad_key_lin, preferred_element_type=jnp.float32)
+            grad_value = jnp.einsum("rd,rq->dq", act_a, grad_value_lin, preferred_element_type=jnp.float32)
+            attn_grads = jnp.concatenate(
+                [
+                    product.astype(jnp.bfloat16)
+                    for product in (grad_query, grad_key, grad_value, grad_out)
+                ],
+                axis=1,
+            )
+            states[0], attn_grads = tied(states[0], attn_grads)
         step = count - distance + 1
         if step < count:
             forward, backward = hop_step(forward, backward, step, count)
-            states[1], forward, backward, down_sum = tied(states[1], forward, backward, down_sum)
-            if step == 2:
-                states[0], act_a, mixed_heads, grad_attn = tied(
-                    states[0], act_a, mixed_heads, grad_attn
-                )
+            states[0], forward, backward, down_sum = tied(states[0], forward, backward, down_sum)
             result_arrived[-step], result_arrived[step] = (forward, backward)
-
-    grad_query = jnp.einsum("rd,qr->dq", act_a, grad_query_lin, preferred_element_type=jnp.float32)
-    grad_key = jnp.einsum("rd,qr->dq", act_a, grad_key_lin, preferred_element_type=jnp.float32)
-    grad_value = jnp.einsum("rd,rq->dq", act_a, grad_value_lin, preferred_element_type=jnp.float32)
-    grad_out = jnp.einsum(
-        "rq,rd->dq", slot_order(mixed_heads), grad_attn, preferred_element_type=jnp.float32
-    )
 
     def rows_from(arrived):
         chunks = [
@@ -715,31 +704,24 @@
     prompt_out, cont_out = rows_from([result_arrived])
     travelling = []
     arrived = []
-    gain_attn_part = 0.0
     for stream in streams:
-        through_attn, gain_half = norm_back(
+        through_attn, _ = norm_back(
             half(input_share, stream), gain_attn, sum_end(states[stream], row_part(input_part, stream))
         )
-        gain_attn_part = gain_attn_part + gain_half
         grad_share = (half(res_share, stream) + through_attn).astype(jnp.bfloat16)
         travelling.append((grad_share, grad_share))
         arrived.append({0: grad_share})
-    gain_parts = jnp.stack([gain_attn_part, gain_mlp_part])
-    stages = pair_stages()
-    per_hop = -(-len(stages) // (count - 1))
     for step in range(1, count):
         travelling = [hop_step(*travelling[stream], step, count) for stream in streams]
-        for axis, distance in stages[(step - 1) * per_hop : step * per_hop]:
-            gain_parts = pair_sum(gain_parts, axis, distance)
-        *travelling[1], gain_parts = tied(*travelling[1], gain_parts)
         for stream in streams:
             arrived[stream][-step], arrived[stream][step] = travelling[stream]
     prompt_grad, cont_grad = rows_from(arrived)
-    gain_rows = width // (lax.axis_size("dp") * lax.axis_size("ctx"))
-    gain_place = (lax.axis_index("dp") * lax.axis_size("ctx") + ctx_index) * gain_rows
-    gain_own = lax.dynamic_slice_in_dim(gain_parts, gain_place, gain_rows, 1)
+    gain_parts = jnp.stack([gain_attn_part, gain_mlp_part])
+    for bit in range(count.bit_length() - 1):
+        gain_parts = pair_sum(gain_parts, "tensor", 1 << bit)
+    gain_own = lax.psum_scatter(gain_parts, ("dp", "ctx"), scatter_dimension=1, tiled=True)
     attn_sum = lax.psum_scatter(
-        jnp.concatenate([grad_query, grad_key, grad_value, grad_out], axis=1).astype(jnp.bfloat16),
+        attn_grads,
         ("dp", "ctx"),
         scatter_dimension=0,
         tiled=True,

time: 749 us -> 732 us (0.977)
  waiting for transfers between devices: 93.4 us -> 147 us
  starting transfers between devices: 189 us -> 138 us
  other arithmetic: 117 us -> 108 us
    ppermute x12 -> x3, starting transfers between devices: 62.1 us -> 15.9 us  [stream_step(): lax.ppermute(to_right, 'tensor', [(i, i + 1) for i in range(0, count - di...]
    ppermute x15 -> x12, waiting for transfers between devices: 48 us -> 68.6 us  [hop_step(): lax.ppermute(backward, 'tensor', [(i, i - 1) for i in range(1, count - st...]
    ppermute x12 -> x3, waiting for transfers between devices: 18.5 us -> 36.4 us  [stream_step(): lax.ppermute(to_right, 'tensor', [(i, i + 1) for i in range(0, count - di...]
    ppermute x3 -> x6, waiting for transfers between devices: 2.89 us -> 19.6 us  [sum_step(): lax.ppermute(to_right, 'tensor', [(i, i + 1) for i in range(0, count - di...]
    ppermute x3 -> x6, starting transfers between devices: 22.2 us -> 35.4 us  [sum_step(): lax.ppermute(to_right, 'tensor', [(i, i + 1) for i in range(0, count - di...]
    ppermute x15 -> x12, starting transfers between devices: 43.5 us -> 31.9 us  [hop_step(): lax.ppermute(forward, 'tensor', [(i, i + 1) for i in range(step - 1, coun...]
    ppermute x12 -> x3, starting transfers between devices: 15.4 us -> 4.75 us  [stream_step(): lax.ppermute(to_left, 'tensor', [(i, i - 1) for i in range(distance, coun...]
    reduce_sum x0 -> x2, other arithmetic: none -> 8.47 us  [the longest x1 5.71 us: shards(): gain_attn_part = jnp.sum(input_grad * scaled_rows, axis=0)]
  transfers between devices with their start and end apart: 80 -> 60, of which waited for: 23 -> 24; matrix products, arithmetic and copies ran while one was open for 41% -> 41% of each run, Pallas kernels for 8% -> 8%
where the time goes in v7:
time: 732 us; the launch traced here: 724 us
  matrix products  191 us (26%)
  waiting for transfers between devices  147 us (20%)
  starting transfers between devices  138 us (19%)
  other arithmetic  108 us (15%)
  local copies, waits for them, and re-layouts  62.5 us (9%)
  Pallas kernels  58.6 us (8%)
  between operations  17.5 us (2%)
    ppermute x12, waiting for transfers between devices, hop_step(): lax.ppermute(backward, 'tensor', [(i, i - 1) for i in range(1, count - st...  68.6 us
    pallas_call x8, Pallas kernels, attention_call(): pl.pallas_call(kernel, out_shape=[out for _, out in outs], grid_spec=pltp...  58.6 us
    ppermute x3, waiting for transfers between devices, stream_step(): lax.ppermute(to_right, 'tensor', [(i, i + 1) for i in range(0, count - di...  36.4 us
    ppermute x6, starting transfers between devices, sum_step(): lax.ppermute(to_right, 'tensor', [(i, i + 1) for i in range(0, count - di...  35.4 us
    unnamed x315, local copies, waits for them, and re-layouts  33.4 us
    ppermute x12, starting transfers between devices, hop_step(): lax.ppermute(forward, 'tensor', [(i, i + 1) for i in range(step - 1, coun...  31.9 us
    dot_general x4, matrix products, shards(): jnp.einsum('rf,df->rd', grad_up_slot, w_up, preferred_element_type=jnp.fl...  26.2 us
    convert_element_type x6, other arithmetic, added(): (first.astype(jnp.float32) + second.astype(jnp.float32)).astype(jnp.bfloa...  26 us
  transfers between devices with their start and end apart: 60, of which 24 were waited for; matrix products, arithmetic and copies ran while one was open for 41% of the time, Pallas kernels for 8%

profile of v7, /device:TPU:0, one launch (start us, length us, event | category | flops | bytes accessed | tf_op | source)
XLA Modules:
  0.0 724.5 jit_solution(4778165418181092099)
XLA Ops:
  81.9 14.6 %fusion.79 = f32[1024,2048]{1,0:T(8,128)} fusion(bf16[1024,2048]{1,0:T(8,128)(2,1)} %pad_maximum_fusion.3, bf16[2048,2048]{1,0:T(8,128)(2,1)} %param.25), kind=kOutput, calls=%fused_computation.259 | convolution fusion | flops 8589934592 | bytes 20971520 | tf_op jit(solution)/shard_map/rd,fd->rf/dot_general | solution.py:470
  117.2 6.4 multiply_reduce_fusion.2
  134.3 6.0 multiply_convert_fusion.11
  156.2 6.1 fusion.82
  162.3 5.9 multiply_convert_fusion.8
  170.7 6.8 fusion.20
  190.2 5.9 multiply_convert_fusion.5
  198.5 6.8 fusion.21
  207.7 6.1 fusion.86
  213.8 6.4 multiply_convert_fusion.2
  222.6 6.9 fusion.22
  234.5 11.4 %convolution_convert_fusion.2 = bf16[2048,2048]{1,0:T(8,128)(2,1)} fusion(bf16[256,2048]{1,0:T(8,128)(2,1)S(1)} %get-tuple-element.183, bf16[256,2048]{1,0:T(8,128)(2,1)S(1)} %copy-done.140, bf16[256,2048]{1,0:T(8,128)(2,1)S(1)} %get-tuple-element.181, bf16[256,2048]{1,0:T(8,128)(2,1)S(1)} %get-tuple-element.180, ...), kind=kOutput, calls=%fused_computation.11 | convolution fusion | flops 8627683328 | bytes 16777216 | tf_op jit(solution)/shard_map/rd,rf->df/dot_general | solution.py:522
  246.0 7.8 %collective-permute-done.12 = bf16[256,2048]{1,0:T(8,128)(2,1)} collective-permute-done((bf16[256,2048]{1,0:T(8,128)(2,1)}, bf16[256,2048]{1,0:T(8,128)(2,1)}, u32[]{:S(2)}, u32[]{:S(2)}) %collective-permute-start.12) | collective-permute-done | bytes 1048608 | tf_op jit(solution)/shard_map/ppermute | solution.py:288
  265.4 12.8 %convolution_convert_fusion.1 = bf16[2048,2048]{1,0:T(8,128)(2,1)} fusion(bf16[256,2048]{1,0:T(8,128)(2,1)} %copy-done.138, bf16[256,2048]{1,0:T(8,128)(2,1)} %copy-done.137, bf16[256,2048]{1,0:T(8,128)(2,1)S(1)} %copy-done.136, bf16[256,2048]{1,0:T(8,128)(2,1)S(1)} %copy-done.134, bf16[256,2048]{1,0:T(8,128)(2,1)S(1)} %copy-done.106, ...), kind=kOutput, calls=%fused_computation.10 | convolution fusion | flops 8627683328 | bytes 16777216 | tf_op jit(solution)/shard_map/rd,rf->df/dot_general | solution.py:523
  293.8 6.0 collective-permute-start.16
  299.8 11.1 %convolution_convert_fusion = bf16[2048,2048]{1,0:T(8,128)(2,1)} fusion(bf16[1024,2048]{1,0:T(8,128)(2,1)S(1)} %copy-done.70, bf16[1024,2048]{1,0:T(8,128)(2,1)S(1)} %constant_dynamic-update-slice_fusion.8), kind=kOutput, calls=%fused_computation.9 | convolution fusion | flops 8594128896 | bytes 16777216 | tf_op jit(solution)/shard_map/rf,rd->df/dot_general | solution.py:524
  338.5 15.4 %convolution_convert_fusion.3 = bf16[1024,2048]{1,0:T(8,128)(2,1)} fusion(bf16[1024,2048]{1,0:T(8,128)(2,1)} %copy-done.118, bf16[2048,2048]{1,0:T(8,128)(2,1)} %param.25), kind=kOutput, calls=%fused_computation.36 | convolution fusion | flops 8592031744 | bytes 16777216 | tf_op jit(solution)/shard_map/dot_general | solution.py:553
  368.2 9.2 %shard_map.241 = (f32[256,512]{1,0:T(8,128)S(1)}, f32[1024,64]{1,0:T(8,128)S(1)}, f32[1024,64]{1,0:T(8,128)S(1)}) custom-call(s32[2]{0:T(128)S(1)} %pad_add_fusion.meta_ref, bf16[256,512]{1,0:T(8,128)(2,1)S(1)} %copy-done.27, bf16[256,512]{1,0:T(8,128)(2,1)S(1)} %copy-done.31, f32[4,1,512]{2,1,0:T(1,128)S(1)} %copy-done.43, bf16[1024,64]{1,0:T(8,128)(2,1)S(1)} %copy-done.14, ...), custom_call_target="tpu_custom_call" | custom-call | flops 1342177280 | bytes 1052672 | tf_op jit(solution)/shard_map/pallas_call | solution.py:183
  387.7 9.0 %collective-permute-start.25 = (bf16[256,2048]{1,0:T(8,128)(2,1)}, bf16[256,2048]{1,0:T(8,128)(2,1)}, u32[]{:S(2)}, u32[]{:S(2)}) collective-permute-start(bf16[256,2048]{1,0:T(8,128)(2,1)} %get-tuple-element.224), channel_id=1, source_target_pairs={{0,1},{4,5},{8,9},{12,13},{16,17},{20,21},{24,25},{28,29}} | collective-permute-start | bytes 3145736 | tf_op jit(solution)/shard_map/ppermute | solution.py:288
  405.5 9.8 %shard_map.242 = (f32[256,512]{1,0:T(8,128)S(1)}, f32[1024,64]{1,0:T(8,128)S(1)}, f32[1024,64]{1,0:T(8,128)S(1)}, f32[512,64]{1,0:T(8,128)S(1)}, f32[512,64]{1,0:T(8,128)S(1)}) custom-call(s32[2]{0:T(128)S(1)} %pad_add_fusion.meta_ref, bf16[256,512]{1,0:T(8,128)(2,1)S(1)} %copy-done.25, bf16[256,512]{1,0:T(8,128)(2,1)S(1)} %copy-done.30, ...), custom_call_target="tpu_custom_call" | custom-call | flops 1509949440 | bytes 1052672 | tf_op jit(solution)/shard_map/pallas_call | solution.py:183
  424.6 6.1 collective-permute-start.29
  436.2 9.2 %shard_map.243 = (f32[256,512]{1,0:T(8,128)S(1)}, f32[1024,64]{1,0:T(8,128)S(1)}, f32[1024,64]{1,0:T(8,128)S(1)}) custom-call(s32[2]{0:T(128)S(1)} %pad_add_fusion.meta_ref, bf16[256,512]{1,0:T(8,128)(2,1)S(1)} %copy-done.23, bf16[256,512]{1,0:T(8,128)(2,1)S(1)} %copy-done.29, f32[4,1,512]{2,1,0:T(1,128)S(1)} %get-tuple-element.229.total_ref, ...), custom_call_target="tpu_custom_call" | custom-call | flops 1342177280 | bytes 1052672 | tf_op jit(solution)/shard_map/pallas_call | solution.py:183
  459.0 9.8 %shard_map.244 = (f32[256,512]{1,0:T(8,128)S(1)}, f32[1024,64]{1,0:T(8,128)S(1)}, f32[1024,64]{1,0:T(8,128)S(1)}, f32[512,64]{1,0:T(8,128)S(1)}, f32[512,64]{1,0:T(8,128)S(1)}) custom-call(s32[2]{0:T(128)S(1)} %pad_add_fusion.meta_ref, bf16[256,512]{1,0:T(8,128)(2,1)S(1)} %copy-done.21, bf16[256,512]{1,0:T(8,128)(2,1)S(1)} %copy-done.28, ...), custom_call_target="tpu_custom_call" | custom-call | flops 1509949440 | bytes 1052672 | tf_op jit(solution)/shard_map/pallas_call | solution.py:183
  480.9 6.0 collective-permute-start.33
  513.9 8.5 %collective-permute-start.36 = (bf16[256,2048]{1,0:T(8,128)(2,1)S(1)}, bf16[256,2048]{1,0:T(8,128)(2,1)S(1)}, u32[]{:S(2)}, u32[]{:S(2)}) collective-permute-start(bf16[256,2048]{1,0:T(8,128)(2,1)S(1)} %get-tuple-element.272), channel_id=1, source_target_pairs={{0,1},{4,5},{8,9},{12,13},{16,17},{20,21},{24,25},{28,29}} | collective-permute-start | bytes 3145736 | tf_op jit(solution)/shard_map/ppermute | solution.py:305
  534.0 10.8 %collective-permute-done.36 = bf16[256,2048]{1,0:T(8,128)(2,1)S(1)} collective-permute-done((bf16[256,2048]{1,0:T(8,128)(2,1)S(1)}, bf16[256,2048]{1,0:T(8,128)(2,1)S(1)}, u32[]{:S(2)}, u32[]{:S(2)}) %collective-permute-start.36) | collective-permute-done | bytes 1048608 | tf_op jit(solution)/shard_map/ppermute | solution.py:305
  580.3 8.0 %collective-permute-done.40 = bf16[256,2048]{1,0:T(8,128)(2,1)} collective-permute-done((bf16[256,2048]{1,0:T(8,128)(2,1)}, bf16[256,2048]{1,0:T(8,128)(2,1)}, u32[]{:S(2)}, u32[]{:S(2)}) %collective-permute-start.40) | collective-permute-done | bytes 1048608 | tf_op jit(solution)/shard_map/ppermute | solution.py:305
  588.3 8.3 %collective-permute-done.43 = bf16[256,2048]{1,0:T(8,128)(2,1)} collective-permute-done((bf16[256,2048]{1,0:T(8,128)(2,1)}, bf16[256,2048]{1,0:T(8,128)(2,1)}, u32[]{:S(2)}, u32[]{:S(2)}) %collective-permute-start.43) | collective-permute-done | bytes 1048608 | tf_op jit(solution)/shard_map/ppermute | solution.py:273
  605.1 17.6 %collective-permute-done.44 = bf16[256,2048]{1,0:T(8,128)(2,1)} collective-permute-done((bf16[256,2048]{1,0:T(8,128)(2,1)}, bf16[256,2048]{1,0:T(8,128)(2,1)}, u32[]{:S(2)}, u32[]{:S(2)}) %collective-permute-start.44) | collective-permute-done | bytes 1048608 | tf_op jit(solution)/shard_map/ppermute | solution.py:305
  639.8 17.5 %collective-permute-done.49 = bf16[256,2048]{1,0:T(8,128)(2,1)S(1)} collective-permute-done((bf16[256,2048]{1,0:T(8,128)(2,1)S(1)}, bf16[256,2048]{1,0:T(8,128)(2,1)S(1)}, u32[]{:S(2)}, u32[]{:S(2)}) %collective-permute-start.49) | collective-permute-done | bytes 1048608 | tf_op jit(solution)/shard_map/ppermute | solution.py:273
  660.3 20.2 %collective-permute-done.50 = bf16[256,2048]{1,0:T(8,128)(2,1)} collective-permute-done((bf16[256,2048]{1,0:T(8,128)(2,1)S(1)}, bf16[256,2048]{1,0:T(8,128)(2,1)}, u32[]{:S(2)}, u32[]{:S(2)}) %collective-permute-start.50) | collective-permute-done | bytes 1048608 | tf_op jit(solution)/shard_map/ppermute | solution.py:273
  693.5 9.1 %collective-permute-done.51 = bf16[256,2048]{1,0:T(8,128)(2,1)} collective-permute-done((bf16[256,2048]{1,0:T(8,128)(2,1)}, bf16[256,2048]{1,0:T(8,128)(2,1)}, u32[]{:S(2)}, u32[]{:S(2)}) %collective-permute-start.51) | collective-permute-done | bytes 1048608 | tf_op jit(solution)/shard_map/ppermute | solution.py:273
  (569 shorter events, 405.5 us)
Async XLA Ops:
  7.2 110.0 %all-gather.2.cloned.1.call-start = ((), (), s32[]{:S(2)}) async-start(), calls=%async_computation.5 | async-start | bytes 9437184 | tf_op jit(solution)/shard_map/all_gather | solution.py:405
  9.7 499.8 %reduce-scatter.8.cloned.1.call-start = ((), (), s32[]{:S(2)}) async-start(), calls=%async_computation.6 | async-start | bytes 9437184 | tf_op jit(solution)/shard_map/reduce_scatter | solution.py:517
  52.7 45.2 %collective-permute-start.5 = (bf16[256,256]{0,1:T(8,128)(2,1)}, bf16[256,256]{0,1:T(8,128)(2,1)}, u32[]{:S(2)}, u32[]{:S(2)}) collective-permute-start(bf16[256,256]{0,1:T(8,128)(2,1)} %get-tuple-element.438), channel_id=1, source_target_pairs={{0,1},{1,2},{2,3},{3,0},{4,5},{5,6},{6,7},{7,4},{8,9},{9,10},{10,1... | collective-permute-start | bytes 393224 | tf_op jit(solution)/shard_map/ppermute | solution.py:323
  55.8 45.0 %collective-permute-start.4 = (bf16[256,256]{0,1:T(8,128)(2,1)}, bf16[256,256]{0,1:T(8,128)(2,1)}, u32[]{:S(2)}, u32[]{:S(2)}) collective-permute-start(bf16[256,256]{0,1:T(8,128)(2,1)} %get-tuple-element.439), channel_id=1, source_target_pairs={{0,2},{1,3},{2,0},{3,1},{4,6},{5,7},{6,4},{7,5},{8,10},{9,11},{10,... | collective-permute-start | bytes 393224 | tf_op jit(solution)/shard_map/ppermute | solution.py:323
  58.5 42.4 %collective-permute-start.3 = (bf16[256,256]{0,1:T(8,128)(2,1)}, bf16[256,256]{0,1:T(8,128)(2,1)}, u32[]{:S(2)}, u32[]{:S(2)}) collective-permute-start(bf16[256,256]{0,1:T(8,128)(2,1)} %get-tuple-element.440), channel_id=1, source_target_pairs={{0,3},{1,0},{2,1},{3,2},{4,7},{5,4},{6,5},{7,6},{8,11},{9,8},{10,9... | collective-permute-start | bytes 393224 | tf_op jit(solution)/shard_map/ppermute | solution.py:323
  74.4 27.7 %collective-permute-start.2 = (bf16[256,256]{0,1:T(8,128)(2,1)}, bf16[256,256]{0,1:T(8,128)(2,1)S(1)}, u32[]{:S(2)}, u32[]{:S(2)}) collective-permute-start(bf16[256,256]{0,1:T(8,128)(2,1)} %get-tuple-element.441), channel_id=1, source_target_pairs={{0,1},{1,2},{2,3},{3,0},{4,5},{5,6},{6,7},{7,4},{8,9},{9,10},{10,1... | collective-permute-start | bytes 393224 | tf_op jit(solution)/shard_map/ppermute | solution.py:323
  75.2 26.9 %collective-permute-start.1 = (bf16[256,256]{0,1:T(8,128)(2,1)}, bf16[256,256]{0,1:T(8,128)(2,1)}, u32[]{:S(2)}, u32[]{:S(2)}) collective-permute-start(bf16[256,256]{0,1:T(8,128)(2,1)} %get-tuple-element.442), channel_id=1, source_target_pairs={{0,2},{1,3},{2,0},{3,1},{4,6},{5,7},{6,4},{7,5},{8,10},{9,11},{10,... | collective-permute-start | bytes 393224 | tf_op jit(solution)/shard_map/ppermute | solution.py:323
  125.2 27.5 %collective-permute-start.7 = (bf16[256,2048]{1,0:T(8,128)(2,1)S(1)}, bf16[256,2048]{1,0:T(8,128)(2,1)S(1)}, u32[]{:S(2)}, u32[]{:S(2)}) collective-permute-start(bf16[256,2048]{1,0:T(8,128)(2,1)S(1)} %multiply_convert_fusion.14), channel_id=1, source_target_pairs={{1,0},{2,1},{3,2},{5,4},{6,5},{7,6},{9,8},{10,9},{11,10},{13,12},{... | collective-permute-start | bytes 3145736 | tf_op jit(solution)/shard_map/ppermute | solution.py:273
  126.8 27.1 %collective-permute-start.6 = (bf16[256,2048]{1,0:T(8,128)(2,1)S(1)}, bf16[256,2048]{1,0:T(8,128)(2,1)S(1)}, u32[]{:S(2)}, u32[]{:S(2)}) collective-permute-start(bf16[256,2048]{1,0:T(8,128)(2,1)S(1)} %multiply_convert_fusion.14), channel_id=1, source_target_pairs={{0,1},{1,2},{2,3},{4,5},{5,6},{6,7},{8,9},{9,10},{10,11},{12,13},{... | collective-permute-start | bytes 3145736 | tf_op jit(solution)/shard_map/ppermute | solution.py:272
  154.6 27.4 %collective-permute-start.9 = (bf16[256,2048]{1,0:T(8,128)(2,1)S(1)}, bf16[256,2048]{1,0:T(8,128)(2,1)S(1)}, u32[]{:S(2)}, u32[]{:S(2)}) collective-permute-start(bf16[256,2048]{1,0:T(8,128)(2,1)S(1)} %collective-permute-done.7), channel_id=1, source_target_pairs={{1,0},{2,1},{5,4},{6,5},{9,8},{10,9},{13,12},{14,13},{17,16},{18,1... | collective-permute-start | bytes 3145736 | tf_op jit(solution)/shard_map/ppermute | solution.py:273
  182.9 24.6 %collective-permute-start.11 = (bf16[256,2048]{1,0:T(8,128)(2,1)S(1)}, bf16[256,2048]{1,0:T(8,128)(2,1)S(1)}, u32[]{:S(2)}, u32[]{:S(2)}) collective-permute-start(bf16[256,2048]{1,0:T(8,128)(2,1)S(1)} %collective-permute-done.9), channel_id=1, source_target_pairs={{1,0},{5,4},{9,8},{13,12},{17,16},{21,20},{25,24},{29,28}} | collective-permute-start | bytes 3145736 | tf_op jit(solution)/shard_map/ppermute | solution.py:273
  253.8 255.8 %reduce-scatter.10.cloned.1.call-start = ((), (), s32[]{:S(2)}) async-start(), calls=%async_computation.7 | async-start | bytes 9437184 | tf_op jit(solution)/shard_map/reduce_scatter | solution.py:517
  283.6 262.2 %reduce-scatter.12.cloned.1.call-start = ((), (), s32[]{:S(2)}) async-start(), calls=%async_computation.8 | async-start | bytes 9437184 | tf_op jit(solution)/shard_map/reduce_scatter | solution.py:517
  338.0 348.6 %reduce-scatter.16.cloned.1.call-start = ((), (), s32[]{:S(2)}) async-start(), calls=%async_computation.10 | async-start | bytes 1179648
  356.6 25.3 %collective-permute-start.22 = (bf16[256,2048]{1,0:T(8,128)(2,1)}, bf16[256,2048]{1,0:T(8,128)(2,1)}, u32[]{:S(2)}, u32[]{:S(2)}) collective-permute-start(bf16[256,2048]{1,0:T(8,128)(2,1)} %get-tuple-element.200), channel_id=1, source_target_pairs={{1,0},{2,1},{3,2},{5,4},{6,5},{7,6},{9,8},{10,9},{11,10},{13,12},{... | collective-permute-start | bytes 3145736 | tf_op jit(solution)/shard_map/ppermute | solution.py:273
  357.9 25.2 %collective-permute-start.21 = (bf16[256,2048]{1,0:T(8,128)(2,1)}, bf16[256,2048]{1,0:T(8,128)(2,1)}, u32[]{:S(2)}, u32[]{:S(2)}) collective-permute-start(bf16[256,2048]{1,0:T(8,128)(2,1)} %get-tuple-element.200), channel_id=1, source_target_pairs={{0,1},{1,2},{2,3},{4,5},{5,6},{6,7},{8,9},{9,10},{10,11},{12,13},{... | collective-permute-start | bytes 3145736 | tf_op jit(solution)/shard_map/ppermute | solution.py:272
  383.1 32.2 %collective-permute-start.23 = (bf16[256,2048]{1,0:T(8,128)(2,1)}, bf16[256,2048]{1,0:T(8,128)(2,1)}, u32[]{:S(2)}, u32[]{:S(2)}) collective-permute-start(bf16[256,2048]{1,0:T(8,128)(2,1)} %collective-permute-done.21), channel_id=1, source_target_pairs={{1,2},{2,3},{5,6},{6,7},{9,10},{10,11},{13,14},{14,15},{17,18},{18... | collective-permute-start | bytes 3145736 | tf_op jit(solution)/shard_map/ppermute | solution.py:272
  384.7 30.6 %collective-permute-start.24 = (bf16[256,2048]{1,0:T(8,128)(2,1)}, bf16[256,2048]{1,0:T(8,128)(2,1)}, u32[]{:S(2)}, u32[]{:S(2)}) collective-permute-start(bf16[256,2048]{1,0:T(8,128)(2,1)} %collective-permute-done.22), channel_id=1, source_target_pairs={{1,0},{2,1},{5,4},{6,5},{9,8},{10,9},{13,12},{14,13},{17,16},{18,1... | collective-permute-start | bytes 3145736 | tf_op jit(solution)/shard_map/ppermute | solution.py:273
  386.0 29.3 %collective-permute-start.26 = (bf16[256,2048]{1,0:T(8,128)(2,1)}, bf16[256,2048]{1,0:T(8,128)(2,1)}, u32[]{:S(2)}, u32[]{:S(2)}) collective-permute-start(bf16[256,2048]{1,0:T(8,128)(2,1)} %get-tuple-element.224), channel_id=1, source_target_pairs={{3,2},{7,6},{11,10},{15,14},{19,18},{23,22},{27,26},{31,30}} | collective-permute-start | bytes 3145736 | tf_op jit(solution)/shard_map/ppermute | solution.py:289
  387.7 27.8 %collective-permute-start.25 = (bf16[256,2048]{1,0:T(8,128)(2,1)}, bf16[256,2048]{1,0:T(8,128)(2,1)}, u32[]{:S(2)}, u32[]{:S(2)}) collective-permute-start(bf16[256,2048]{1,0:T(8,128)(2,1)} %get-tuple-element.224), channel_id=1, source_target_pairs={{0,1},{4,5},{8,9},{12,13},{16,17},{20,21},{24,25},{28,29}} | collective-permute-start | bytes 3145736 | tf_op jit(solution)/shard_map/ppermute | solution.py:288
  415.6 29.8 %collective-permute-start.27 = (bf16[256,2048]{1,0:T(8,128)(2,1)}, bf16[256,2048]{1,0:T(8,128)(2,1)}, u32[]{:S(2)}, u32[]{:S(2)}) collective-permute-start(bf16[256,2048]{1,0:T(8,128)(2,1)} %collective-permute-done.23), channel_id=1, source_target_pairs={{2,3},{6,7},{10,11},{14,15},{18,19},{22,23},{26,27},{30,31}} | collective-permute-start | bytes 3145736 | tf_op jit(solution)/shard_map/ppermute | solution.py:272
  417.3 28.1 %collective-permute-start.28 = (bf16[256,2048]{1,0:T(8,128)(2,1)}, bf16[256,2048]{1,0:T(8,128)(2,1)}, u32[]{:S(2)}, u32[]{:S(2)}) collective-permute-start(bf16[256,2048]{1,0:T(8,128)(2,1)} %collective-permute-done.24), channel_id=1, source_target_pairs={{1,0},{5,4},{9,8},{13,12},{17,16},{21,20},{25,24},{29,28}} | collective-permute-start | bytes 3145736 | tf_op jit(solution)/shard_map/ppermute | solution.py:273
  424.6 24.6 %collective-permute-start.29 = (bf16[256,2048]{1,0:T(8,128)(2,1)}, bf16[256,2048]{1,0:T(8,128)(2,1)}, u32[]{:S(2)}, u32[]{:S(2)}) collective-permute-start(bf16[256,2048]{1,0:T(8,128)(2,1)} %get-tuple-element.393), channel_id=1, source_target_pairs={{0,1},{1,2},{4,5},{5,6},{8,9},{9,10},{12,13},{13,14},{16,17},{17,1... | collective-permute-start | bytes 3145736 | tf_op jit(solution)/shard_map/ppermute | solution.py:288
  451.9 24.1 %collective-permute-start.32 = (bf16[256,2048]{1,0:T(8,128)(2,1)S(1)}, bf16[256,2048]{1,0:T(8,128)(2,1)S(1)}, u32[]{:S(2)}, u32[]{:S(2)}) collective-permute-start(bf16[256,2048]{1,0:T(8,128)(2,1)S(1)} %get-tuple-element.405), channel_id=1, source_target_pairs={{1,0},{2,1},{3,2},{5,4},{6,5},{7,6},{9,8},{10,9},{11,10},{13,12},{... | collective-permute-start | bytes 3145736 | tf_op jit(solution)/shard_map/ppermute | solution.py:289
  479.6 29.9 %collective-permute-start.34 = (bf16[256,2048]{1,0:T(8,128)(2,1)S(1)}, bf16[256,2048]{1,0:T(8,128)(2,1)}, u32[]{:S(2)}, u32[]{:S(2)}) collective-permute-start(bf16[256,2048]{1,0:T(8,128)(2,1)S(1)} %add_convert_fusion.4), channel_id=1, source_target_pairs={{1,0},{2,1},{3,2},{5,4},{6,5},{7,6},{9,8},{10,9},{11,10},{13,12},{... | collective-permute-start | bytes 3145736 | tf_op jit(solution)/shard_map/ppermute | solution.py:273
  480.9 28.6 %collective-permute-start.33 = (bf16[256,2048]{1,0:T(8,128)(2,1)S(1)}, bf16[256,2048]{1,0:T(8,128)(2,1)}, u32[]{:S(2)}, u32[]{:S(2)}) collective-permute-start(bf16[256,2048]{1,0:T(8,128)(2,1)S(1)} %add_convert_fusion.4), channel_id=1, source_target_pairs={{0,1},{1,2},{2,3},{4,5},{5,6},{6,7},{8,9},{9,10},{10,11},{12,13},{... | collective-permute-start | bytes 3145736 | tf_op jit(solution)/shard_map/ppermute | solution.py:272
  509.6 36.2 %collective-permute-start.38 = (bf16[256,2048]{1,0:T(8,128)(2,1)}, bf16[256,2048]{1,0:T(8,128)(2,1)S(1)}, u32[]{:S(2)}, u32[]{:S(2)}) collective-permute-start(bf16[256,2048]{1,0:T(8,128)(2,1)} %collective-permute-done.33), channel_id=1, source_target_pairs={{1,2},{2,3},{5,6},{6,7},{9,10},{10,11},{13,14},{14,15},{17,18},{18... | collective-permute-start | bytes 3145736 | tf_op jit(solution)/shard_map/ppermute | solution.py:272
  510.5 35.3 %collective-permute-start.39 = (bf16[256,2048]{1,0:T(8,128)(2,1)}, bf16[256,2048]{1,0:T(8,128)(2,1)}, u32[]{:S(2)}, u32[]{:S(2)}) collective-permute-start(bf16[256,2048]{1,0:T(8,128)(2,1)} %collective-permute-done.34), channel_id=1, source_target_pairs={{1,0},{2,1},{5,4},{6,5},{9,8},{10,9},{13,12},{14,13},{17,16},{18,1... | collective-permute-start | bytes 3145736 | tf_op jit(solution)/shard_map/ppermute | solution.py:273
  513.9 30.9 %collective-permute-start.36 = (bf16[256,2048]{1,0:T(8,128)(2,1)S(1)}, bf16[256,2048]{1,0:T(8,128)(2,1)S(1)}, u32[]{:S(2)}, u32[]{:S(2)}) collective-permute-start(bf16[256,2048]{1,0:T(8,128)(2,1)S(1)} %get-tuple-element.272), channel_id=1, source_target_pairs={{0,1},{4,5},{8,9},{12,13},{16,17},{20,21},{24,25},{28,29}} | collective-permute-start | bytes 3145736 | tf_op jit(solution)/shard_map/ppermute | solution.py:305
  563.3 25.0 %collective-permute-start.40 = (bf16[256,2048]{1,0:T(8,128)(2,1)}, bf16[256,2048]{1,0:T(8,128)(2,1)}, u32[]{:S(2)}, u32[]{:S(2)}) collective-permute-start(bf16[256,2048]{1,0:T(8,128)(2,1)} %get-tuple-element.285), channel_id=1, source_target_pairs={{0,1},{1,2},{4,5},{5,6},{8,9},{9,10},{12,13},{13,14},{16,17},{17,1... | collective-permute-start | bytes 3145736 | tf_op jit(solution)/shard_map/ppermute | solution.py:305
  571.5 25.2 %collective-permute-start.43 = (bf16[256,2048]{1,0:T(8,128)(2,1)}, bf16[256,2048]{1,0:T(8,128)(2,1)}, u32[]{:S(2)}, u32[]{:S(2)}) collective-permute-start(bf16[256,2048]{1,0:T(8,128)(2,1)} %collective-permute-done.39), channel_id=1, source_target_pairs={{1,0},{5,4},{9,8},{13,12},{17,16},{21,20},{25,24},{29,28}} | collective-permute-start | bytes 3145736 | tf_op jit(solution)/shard_map/ppermute | solution.py:273
  574.2 139.1 %reduce-scatter.14.cloned.1.call-start = ((), (), s32[]{:S(2)}) async-start(), calls=%async_computation.9 | async-start | bytes 5898240 | tf_op jit(solution)/shard_map/reduce_scatter | solution.py:723
  (180 other events, 2028.3 us)
Sparse Core Ops, SparseCore 0:
  10.2 106.9 all-gather.1
  253.9 71.5 reduce-scatter.7
  329.0 71.4 reduce-scatter.9
  403.8 71.4 reduce-scatter.11
  574.3 37.2 reduce-scatter.15
  614.8 56.4 reduce-scatter.13

commit v8 on v7

--- a/solution.py
+++ b/solution.py
@@ -290,7 +290,7 @@
     )
 
 
-def stream_step(states, parts, part_of, distance, count, waiting):
+def stream_step(states, parts, part_of, distance, count):
     moved = []
     for stream, state in enumerate(states):
         part_at = part_of(parts, stream)
@@ -299,14 +299,14 @@
         if state is not None:
             to_right = added(to_right, state[0])
             to_left = added(to_left, state[1])
-        to_right, to_left, parts, waiting = tied(to_right, to_left, parts, waiting)
+        to_right, to_left, parts = tied(to_right, to_left, parts)
         moved.append(
             (
                 lax.ppermute(to_right, "tensor", [(i, i + 1) for i in range(0, count - distance)]),
                 lax.ppermute(to_left, "tensor", [(i, i - 1) for i in range(distance, count)]),
             )
         )
-    return (moved, parts, waiting)
+    return (moved, parts)
 
 
 def sum_end(state, part_at):
@@ -655,34 +655,28 @@
 
     states = [None]
     forward, backward = hop_step(result_share, result_share, 1, count)
-    forward, backward, input_part, gate_sum, up_sum, input_grad, mixed_heads, grad_attn = tied(
-        forward, backward, input_part, gate_sum, up_sum, input_grad, mixed_heads, grad_attn
+    forward, backward, input_part, gate_sum, up_sum, input_grad, mixed_heads, act_a = tied(
+        forward, backward, input_part, gate_sum, up_sum, input_grad, mixed_heads, act_a
     )
     result_arrived = {0: result_share, -1: forward, 1: backward}
     for distance in range(count - 1, 0, -1):
-        states, input_part, act_a = stream_step(
-            states, input_part, row_part, distance, count, act_a
-        )
+        states, input_part = stream_step(states, input_part, row_part, distance, count)
         if distance == count - 1:
             gain_attn_part = jnp.sum(input_grad * scaled_rows, axis=0)
             grad_out = jnp.einsum(
                 "rq,rd->dq", slot_order(mixed_heads), grad_attn, preferred_element_type=jnp.float32
             )
-            states[0], gain_attn_part, grad_out = tied(
-                states[0], gain_attn_part, grad_out.astype(jnp.bfloat16)
-            )
-        if distance == count - 2:
             grad_query = jnp.einsum("rd,qr->dq", act_a, grad_query_lin, preferred_element_type=jnp.float32)
             grad_key = jnp.einsum("rd,qr->dq", act_a, grad_key_lin, preferred_element_type=jnp.float32)
             grad_value = jnp.einsum("rd,rq->dq", act_a, grad_value_lin, preferred_element_type=jnp.float32)
-            attn_grads = jnp.concatenate(
-                [
-                    product.astype(jnp.bfloat16)
-                    for product in (grad_query, grad_key, grad_value, grad_out)
-                ],
-                axis=1,
-            )
-            states[0], attn_grads = tied(states[0], attn_grads)
+            products = [
+                product.astype(jnp.bfloat16)
+                for product in (grad_query, grad_key, grad_value, grad_out)
+            ]
+            states[0], gain_attn_part, products = tied(states[0], gain_attn_part, products)
+        if distance == count - 2:
+            attn_grads = jnp.concatenate(products, axis=1)
+            states[0], attn_grads, gain_attn_part = tied(states[0], attn_grads, gain_attn_part)
         step = count - distance + 1
         if step < count:
             forward, backward = hop_step(forward, backward, step, count)

time: 732 us -> 729 us (level)
  starting transfers between devices: 138 us -> 146 us
  waiting for transfers between devices: 147 us -> 139 us
    ppermute x12, waiting for transfers between devices: 68.6 us -> 59.2 us  [hop_step(): lax.ppermute(backward, 'tensor', [(i, i - 1) for i in range(1, count - st...]
    unnamed x315 -> x343, local copies, waits for them, and re-layouts: 33.4 us -> 37.1 us
  transfers between devices with their start and end apart: 60 -> 60, of which waited for: 24 -> 24; matrix products, arithmetic and copies ran while one was open for 41% -> 40% of each run, Pallas kernels for 8% -> 8%
where the time goes in v8:
time: 729 us; the launch traced here: 721 us
  matrix products  185 us (25%)
  starting transfers between devices  146 us (20%)
  waiting for transfers between devices  139 us (19%)
  other arithmetic  105 us (14%)
  local copies, waits for them, and re-layouts  67.2 us (9%)
  Pallas kernels  58.2 us (8%)
  between operations  17.5 us (2%)
    ppermute x12, waiting for transfers between devices, hop_step(): lax.ppermute(backward, 'tensor', [(i, i - 1) for i in range(1, count - st...  59.2 us
    pallas_call x8, Pallas kernels, attention_call(): pl.pallas_call(kernel, out_shape=[out for _, out in outs], grid_spec=pltp...  58.2 us
    unnamed x343, local copies, waits for them, and re-layouts  37.1 us
    ppermute x6, starting transfers between devices, sum_step(): lax.ppermute(to_right, 'tensor', [(i, i + 1) for i in range(0, count - di...  36.2 us
    ppermute x12, starting transfers between devices, hop_step(): lax.ppermute(forward, 'tensor', [(i, i + 1) for i in range(step - 1, coun...  34.3 us
    ppermute x3, waiting for transfers between devices, stream_step(): lax.ppermute(to_right, 'tensor', [(i, i + 1) for i in range(0, count - di...  30.2 us
    convert_element_type x6, other arithmetic, added(): (first.astype(jnp.float32) + second.astype(jnp.float32)).astype(jnp.bfloa...  27.3 us
    dot_general x4, matrix products, shards(): jnp.einsum('rf,df->rd', grad_up_slot, w_up, preferred_element_type=jnp.fl...  26 us
  transfers between devices with their start and end apart: 60, of which 24 were waited for; matrix products, arithmetic and copies ran while one was open for 40% of the time, Pallas kernels for 8%

profile of v8, /device:TPU:0, one launch (start us, length us, event | category | flops | bytes accessed | tf_op | source)
XLA Modules:
  0.0 720.9 jit_solution(2297098806142898955)
XLA Ops:
  82.0 14.6 %fusion.90 = f32[1024,2048]{1,0:T(8,128)} fusion(bf16[1024,2048]{1,0:T(8,128)(2,1)} %pad_maximum_fusion.3, bf16[2048,2048]{1,0:T(8,128)(2,1)} %param.25), kind=kOutput, calls=%fused_computation.266 | convolution fusion | flops 8589934592 | bytes 20971520 | tf_op jit(solution)/shard_map/rd,fd->rf/dot_general | solution.py:470
  117.2 6.4 multiply_reduce_fusion.2
  134.4 5.8 multiply_convert_fusion.11
  142.6 5.7 fusion.30
  156.2 6.1 fusion.93
  170.4 6.7 fusion.31
  198.3 6.7 fusion.32
  207.7 6.1 fusion.97
  213.8 6.3 multiply_convert_fusion.2
  222.5 6.8 fusion.33
  234.0 11.2 %convolution_convert_fusion.2 = bf16[2048,2048]{1,0:T(8,128)(2,1)} fusion(bf16[256,2048]{1,0:T(8,128)(2,1)S(1)} %get-tuple-element.185, bf16[256,2048]{1,0:T(8,128)(2,1)S(1)} %copy-done.152, bf16[256,2048]{1,0:T(8,128)(2,1)S(1)} %get-tuple-element.183, bf16[256,2048]{1,0:T(8,128)(2,1)S(1)} %get-tuple-element.182, ...), kind=kOutput, calls=%fused_computation.11 | convolution fusion | flops 8627683328 | bytes 16777216 | tf_op jit(solution)/shard_map/rd,rf->df/dot_general | solution.py:522
  245.2 8.0 %collective-permute-done.12 = bf16[256,2048]{1,0:T(8,128)(2,1)} collective-permute-done((bf16[256,2048]{1,0:T(8,128)(2,1)}, bf16[256,2048]{1,0:T(8,128)(2,1)}, u32[]{:S(2)}, u32[]{:S(2)}) %collective-permute-start.12) | collective-permute-done | bytes 1048608 | tf_op jit(solution)/shard_map/ppermute | solution.py:288
  264.8 12.6 %convolution_convert_fusion.1 = bf16[2048,2048]{1,0:T(8,128)(2,1)} fusion(bf16[256,2048]{1,0:T(8,128)(2,1)} %copy-done.150, bf16[256,2048]{1,0:T(8,128)(2,1)} %copy-done.149, bf16[256,2048]{1,0:T(8,128)(2,1)S(1)} %copy-done.148, bf16[256,2048]{1,0:T(8,128)(2,1)S(1)} %copy-done.146, bf16[256,2048]{1,0:T(8,128)(2,1)S(1)} %copy-done.114, ...), kind=kOutput, calls=%fused_computation.10 | convolution fusion | flops 8627683328 | bytes 16777216 | tf_op jit(solution)/shard_map/rd,rf->df/dot_general | solution.py:523
  293.4 5.9 collective-permute-start.16
  299.3 11.5 %convolution_convert_fusion = bf16[2048,2048]{1,0:T(8,128)(2,1)} fusion(bf16[1024,2048]{1,0:T(8,128)(2,1)S(1)} %copy-done.77, bf16[1024,2048]{1,0:T(8,128)(2,1)S(1)} %constant_dynamic-update-slice_fusion.8), kind=kOutput, calls=%fused_computation.9 | convolution fusion | flops 8594128896 | bytes 16777216 | tf_op jit(solution)/shard_map/rf,rd->df/dot_general | solution.py:524
  338.2 10.4 %convolution_convert_fusion.3 = bf16[1024,2048]{1,0:T(8,128)(2,1)} fusion(bf16[1024,2048]{1,0:T(8,128)(2,1)S(1)} %copy-done.131, bf16[2048,2048]{1,0:T(8,128)(2,1)S(1)} %bitcast.221), kind=kOutput, calls=%fused_computation.43 | convolution fusion | flops 8592031744 | bytes 16777216 | tf_op jit(solution)/shard_map/dot_general | solution.py:553
  354.0 8.5 %collective-permute-start.21 = (bf16[256,2048]{1,0:T(8,128)(2,1)}, bf16[256,2048]{1,0:T(8,128)(2,1)}, u32[]{:S(2)}, u32[]{:S(2)}) collective-permute-start(bf16[256,2048]{1,0:T(8,128)(2,1)} %get-tuple-element.202), channel_id=1, source_target_pairs={{0,1},{1,2},{2,3},{4,5},{5,6},{6,7},{8,9},{9,10},{10,11},{12,13},{... | collective-permute-start | bytes 3145736 | tf_op jit(solution)/shard_map/ppermute | solution.py:272
  367.3 9.2 %shard_map.241 = (f32[256,512]{1,0:T(8,128)S(1)}, f32[1024,64]{1,0:T(8,128)S(1)}, f32[1024,64]{1,0:T(8,128)S(1)}) custom-call(s32[2]{0:T(128)S(1)} %pad_add_fusion.meta_ref, bf16[256,512]{1,0:T(8,128)(2,1)S(1)} %copy-done.34, bf16[256,512]{1,0:T(8,128)(2,1)S(1)} %copy-done.38, f32[4,1,512]{2,1,0:T(1,128)S(1)} %copy-done.50, bf16[1024,64]{1,0:T(8,128)(2,1)S(1)} %copy-done.21, ...), custom_call_target="tpu_custom_call" | custom-call | flops 1342177280 | bytes 1052672 | tf_op jit(solution)/shard_map/pallas_call | solution.py:183
  387.5 9.0 %collective-permute-start.25 = (bf16[256,2048]{1,0:T(8,128)(2,1)}, bf16[256,2048]{1,0:T(8,128)(2,1)}, u32[]{:S(2)}, u32[]{:S(2)}) collective-permute-start(bf16[256,2048]{1,0:T(8,128)(2,1)} %get-tuple-element.226), channel_id=1, source_target_pairs={{0,1},{4,5},{8,9},{12,13},{16,17},{20,21},{24,25},{28,29}} | collective-permute-start | bytes 3145736 | tf_op jit(solution)/shard_map/ppermute | solution.py:288
  405.3 9.6 %shard_map.242 = (f32[256,512]{1,0:T(8,128)S(1)}, f32[1024,64]{1,0:T(8,128)S(1)}, f32[1024,64]{1,0:T(8,128)S(1)}, f32[512,64]{1,0:T(8,128)S(1)}, f32[512,64]{1,0:T(8,128)S(1)}) custom-call(s32[2]{0:T(128)S(1)} %pad_add_fusion.meta_ref, bf16[256,512]{1,0:T(8,128)(2,1)S(1)} %copy-done.32, bf16[256,512]{1,0:T(8,128)(2,1)S(1)} %copy-done.37, ...), custom_call_target="tpu_custom_call" | custom-call | flops 1509949440 | bytes 1052672 | tf_op jit(solution)/shard_map/pallas_call | solution.py:183
  424.3 6.3 collective-permute-start.29
  434.5 9.1 %shard_map.243 = (f32[256,512]{1,0:T(8,128)S(1)}, f32[1024,64]{1,0:T(8,128)S(1)}, f32[1024,64]{1,0:T(8,128)S(1)}) custom-call(s32[2]{0:T(128)S(1)} %pad_add_fusion.meta_ref, bf16[256,512]{1,0:T(8,128)(2,1)S(1)} %copy-done.30, bf16[256,512]{1,0:T(8,128)(2,1)S(1)} %copy-done.36, f32[4,1,512]{2,1,0:T(1,128)S(1)} %get-tuple-element.231.total_ref, ...), custom_call_target="tpu_custom_call" | custom-call | flops 1342177280 | bytes 1052672 | tf_op jit(solution)/shard_map/pallas_call | solution.py:183
  454.0 6.7 collective-permute-start.31
  466.0 9.7 %shard_map.244 = (f32[256,512]{1,0:T(8,128)S(1)}, f32[1024,64]{1,0:T(8,128)S(1)}, f32[1024,64]{1,0:T(8,128)S(1)}, f32[512,64]{1,0:T(8,128)S(1)}, f32[512,64]{1,0:T(8,128)S(1)}) custom-call(s32[2]{0:T(128)S(1)} %pad_add_fusion.meta_ref, bf16[256,512]{1,0:T(8,128)(2,1)S(1)} %copy-done.28, bf16[256,512]{1,0:T(8,128)(2,1)S(1)} %copy-done.35, ...), custom_call_target="tpu_custom_call" | custom-call | flops 1509949440 | bytes 1052672 | tf_op jit(solution)/shard_map/pallas_call | solution.py:183
  507.0 5.8 fusion.87
  516.9 8.8 %collective-permute-start.36 = (bf16[256,2048]{1,0:T(8,128)(2,1)S(1)}, bf16[256,2048]{1,0:T(8,128)(2,1)S(1)}, u32[]{:S(2)}, u32[]{:S(2)}) collective-permute-start(bf16[256,2048]{1,0:T(8,128)(2,1)S(1)} %get-tuple-element.272), channel_id=1, source_target_pairs={{0,1},{4,5},{8,9},{12,13},{16,17},{20,21},{24,25},{28,29}} | collective-permute-start | bytes 3145736 | tf_op jit(solution)/shard_map/ppermute | solution.py:305
  567.2 13.2 %collective-permute-done.40 = bf16[256,2048]{1,0:T(8,128)(2,1)} collective-permute-done((bf16[256,2048]{1,0:T(8,128)(2,1)}, bf16[256,2048]{1,0:T(8,128)(2,1)}, u32[]{:S(2)}, u32[]{:S(2)}) %collective-permute-start.40) | collective-permute-done | bytes 1048608 | tf_op jit(solution)/shard_map/ppermute | solution.py:305
  580.4 6.4 collective-permute-start.52
  606.0 15.9 %collective-permute-done.44 = bf16[256,2048]{1,0:T(8,128)(2,1)} collective-permute-done((bf16[256,2048]{1,0:T(8,128)(2,1)}, bf16[256,2048]{1,0:T(8,128)(2,1)}, u32[]{:S(2)}, u32[]{:S(2)}) %collective-permute-start.44) | collective-permute-done | bytes 1048608 | tf_op jit(solution)/shard_map/ppermute | solution.py:305
  638.8 17.4 %collective-permute-done.49 = bf16[256,2048]{1,0:T(8,128)(2,1)S(1)} collective-permute-done((bf16[256,2048]{1,0:T(8,128)(2,1)S(1)}, bf16[256,2048]{1,0:T(8,128)(2,1)S(1)}, u32[]{:S(2)}, u32[]{:S(2)}) %collective-permute-start.49) | collective-permute-done | bytes 1048608 | tf_op jit(solution)/shard_map/ppermute | solution.py:273
  659.2 20.2 %collective-permute-done.50 = bf16[256,2048]{1,0:T(8,128)(2,1)} collective-permute-done((bf16[256,2048]{1,0:T(8,128)(2,1)S(1)}, bf16[256,2048]{1,0:T(8,128)(2,1)}, u32[]{:S(2)}, u32[]{:S(2)}) %collective-permute-start.50) | collective-permute-done | bytes 1048608 | tf_op jit(solution)/shard_map/ppermute | solution.py:273
  692.4 6.7 collective-permute-done.51
  (597 shorter events, 410.1 us)
Async XLA Ops:
  7.2 110.0 %all-gather.2.cloned.1.call-start = ((), (), s32[]{:S(2)}) async-start(), calls=%async_computation.5 | async-start | bytes 9437184 | tf_op jit(solution)/shard_map/all_gather | solution.py:405
  9.7 503.2 %reduce-scatter.8.cloned.1.call-start = ((), (), s32[]{:S(2)}) async-start(), calls=%async_computation.6 | async-start | bytes 9437184 | tf_op jit(solution)/shard_map/reduce_scatter | solution.py:517
  52.7 45.2 %collective-permute-start.5 = (bf16[256,256]{0,1:T(8,128)(2,1)}, bf16[256,256]{0,1:T(8,128)(2,1)}, u32[]{:S(2)}, u32[]{:S(2)}) collective-permute-start(bf16[256,256]{0,1:T(8,128)(2,1)} %get-tuple-element.442), channel_id=1, source_target_pairs={{0,1},{1,2},{2,3},{3,0},{4,5},{5,6},{6,7},{7,4},{8,9},{9,10},{10,1... | collective-permute-start | bytes 393224 | tf_op jit(solution)/shard_map/ppermute | solution.py:323
  55.9 44.9 %collective-permute-start.4 = (bf16[256,256]{0,1:T(8,128)(2,1)}, bf16[256,256]{0,1:T(8,128)(2,1)}, u32[]{:S(2)}, u32[]{:S(2)}) collective-permute-start(bf16[256,256]{0,1:T(8,128)(2,1)} %get-tuple-element.443), channel_id=1, source_target_pairs={{0,2},{1,3},{2,0},{3,1},{4,6},{5,7},{6,4},{7,5},{8,10},{9,11},{10,... | collective-permute-start | bytes 393224 | tf_op jit(solution)/shard_map/ppermute | solution.py:323
  58.5 42.4 %collective-permute-start.3 = (bf16[256,256]{0,1:T(8,128)(2,1)}, bf16[256,256]{0,1:T(8,128)(2,1)}, u32[]{:S(2)}, u32[]{:S(2)}) collective-permute-start(bf16[256,256]{0,1:T(8,128)(2,1)} %get-tuple-element.444), channel_id=1, source_target_pairs={{0,3},{1,0},{2,1},{3,2},{4,7},{5,4},{6,5},{7,6},{8,11},{9,8},{10,9... | collective-permute-start | bytes 393224 | tf_op jit(solution)/shard_map/ppermute | solution.py:323
  74.4 27.7 %collective-permute-start.2 = (bf16[256,256]{0,1:T(8,128)(2,1)}, bf16[256,256]{0,1:T(8,128)(2,1)S(1)}, u32[]{:S(2)}, u32[]{:S(2)}) collective-permute-start(bf16[256,256]{0,1:T(8,128)(2,1)} %get-tuple-element.445), channel_id=1, source_target_pairs={{0,1},{1,2},{2,3},{3,0},{4,5},{5,6},{6,7},{7,4},{8,9},{9,10},{10,1... | collective-permute-start | bytes 393224 | tf_op jit(solution)/shard_map/ppermute | solution.py:323
  75.2 26.9 %collective-permute-start.1 = (bf16[256,256]{0,1:T(8,128)(2,1)}, bf16[256,256]{0,1:T(8,128)(2,1)}, u32[]{:S(2)}, u32[]{:S(2)}) collective-permute-start(bf16[256,256]{0,1:T(8,128)(2,1)} %get-tuple-element.446), channel_id=1, source_target_pairs={{0,2},{1,3},{2,0},{3,1},{4,6},{5,7},{6,4},{7,5},{8,10},{9,11},{10,... | collective-permute-start | bytes 393224 | tf_op jit(solution)/shard_map/ppermute | solution.py:323
  125.3 27.5 %collective-permute-start.7 = (bf16[256,2048]{1,0:T(8,128)(2,1)S(1)}, bf16[256,2048]{1,0:T(8,128)(2,1)S(1)}, u32[]{:S(2)}, u32[]{:S(2)}) collective-permute-start(bf16[256,2048]{1,0:T(8,128)(2,1)S(1)} %multiply_convert_fusion.14), channel_id=1, source_target_pairs={{1,0},{2,1},{3,2},{5,4},{6,5},{7,6},{9,8},{10,9},{11,10},{13,12},{... | collective-permute-start | bytes 3145736 | tf_op jit(solution)/shard_map/ppermute | solution.py:273
  126.8 27.1 %collective-permute-start.6 = (bf16[256,2048]{1,0:T(8,128)(2,1)S(1)}, bf16[256,2048]{1,0:T(8,128)(2,1)S(1)}, u32[]{:S(2)}, u32[]{:S(2)}) collective-permute-start(bf16[256,2048]{1,0:T(8,128)(2,1)S(1)} %multiply_convert_fusion.14), channel_id=1, source_target_pairs={{0,1},{1,2},{2,3},{4,5},{5,6},{6,7},{8,9},{9,10},{10,11},{12,13},{... | collective-permute-start | bytes 3145736 | tf_op jit(solution)/shard_map/ppermute | solution.py:272
  154.6 27.4 %collective-permute-start.9 = (bf16[256,2048]{1,0:T(8,128)(2,1)S(1)}, bf16[256,2048]{1,0:T(8,128)(2,1)S(1)}, u32[]{:S(2)}, u32[]{:S(2)}) collective-permute-start(bf16[256,2048]{1,0:T(8,128)(2,1)S(1)} %collective-permute-done.7), channel_id=1, source_target_pairs={{1,0},{2,1},{5,4},{6,5},{9,8},{10,9},{13,12},{14,13},{17,16},{18,1... | collective-permute-start | bytes 3145736 | tf_op jit(solution)/shard_map/ppermute | solution.py:273
  253.3 259.7 %reduce-scatter.10.cloned.1.call-start = ((), (), s32[]{:S(2)}) async-start(), calls=%async_computation.7 | async-start | bytes 9437184 | tf_op jit(solution)/shard_map/reduce_scatter | solution.py:517
  283.0 266.0 %reduce-scatter.12.cloned.1.call-start = ((), (), s32[]{:S(2)}) async-start(), calls=%async_computation.8 | async-start | bytes 9437184 | tf_op jit(solution)/shard_map/reduce_scatter | solution.py:517
  348.7 341.3 %reduce-scatter.16.cloned.1.call-start = ((), (), s32[]{:S(2)}) async-start(), calls=%async_computation.10 | async-start | bytes 1179648
  352.7 29.0 %collective-permute-start.22 = (bf16[256,2048]{1,0:T(8,128)(2,1)}, bf16[256,2048]{1,0:T(8,128)(2,1)}, u32[]{:S(2)}, u32[]{:S(2)}) collective-permute-start(bf16[256,2048]{1,0:T(8,128)(2,1)} %get-tuple-element.202), channel_id=1, source_target_pairs={{1,0},{2,1},{3,2},{5,4},{6,5},{7,6},{9,8},{10,9},{11,10},{13,12},{... | collective-permute-start | bytes 3145736 | tf_op jit(solution)/shard_map/ppermute | solution.py:273
  354.0 28.9 %collective-permute-start.21 = (bf16[256,2048]{1,0:T(8,128)(2,1)}, bf16[256,2048]{1,0:T(8,128)(2,1)}, u32[]{:S(2)}, u32[]{:S(2)}) collective-permute-start(bf16[256,2048]{1,0:T(8,128)(2,1)} %get-tuple-element.202), channel_id=1, source_target_pairs={{0,1},{1,2},{2,3},{4,5},{5,6},{6,7},{8,9},{9,10},{10,11},{12,13},{... | collective-permute-start | bytes 3145736 | tf_op jit(solution)/shard_map/ppermute | solution.py:272
  382.9 32.1 %collective-permute-start.23 = (bf16[256,2048]{1,0:T(8,128)(2,1)}, bf16[256,2048]{1,0:T(8,128)(2,1)}, u32[]{:S(2)}, u32[]{:S(2)}) collective-permute-start(bf16[256,2048]{1,0:T(8,128)(2,1)} %collective-permute-done.21), channel_id=1, source_target_pairs={{1,2},{2,3},{5,6},{6,7},{9,10},{10,11},{13,14},{14,15},{17,18},{18... | collective-permute-start | bytes 3145736 | tf_op jit(solution)/shard_map/ppermute | solution.py:272
  384.5 30.4 %collective-permute-start.24 = (bf16[256,2048]{1,0:T(8,128)(2,1)}, bf16[256,2048]{1,0:T(8,128)(2,1)}, u32[]{:S(2)}, u32[]{:S(2)}) collective-permute-start(bf16[256,2048]{1,0:T(8,128)(2,1)} %collective-permute-done.22), channel_id=1, source_target_pairs={{1,0},{2,1},{5,4},{6,5},{9,8},{10,9},{13,12},{14,13},{17,16},{18,1... | collective-permute-start | bytes 3145736 | tf_op jit(solution)/shard_map/ppermute | solution.py:273
  385.8 29.2 %collective-permute-start.26 = (bf16[256,2048]{1,0:T(8,128)(2,1)}, bf16[256,2048]{1,0:T(8,128)(2,1)}, u32[]{:S(2)}, u32[]{:S(2)}) collective-permute-start(bf16[256,2048]{1,0:T(8,128)(2,1)} %get-tuple-element.226), channel_id=1, source_target_pairs={{3,2},{7,6},{11,10},{15,14},{19,18},{23,22},{27,26},{31,30}} | collective-permute-start | bytes 3145736 | tf_op jit(solution)/shard_map/ppermute | solution.py:289
  387.5 27.9 %collective-permute-start.25 = (bf16[256,2048]{1,0:T(8,128)(2,1)}, bf16[256,2048]{1,0:T(8,128)(2,1)}, u32[]{:S(2)}, u32[]{:S(2)}) collective-permute-start(bf16[256,2048]{1,0:T(8,128)(2,1)} %get-tuple-element.226), channel_id=1, source_target_pairs={{0,1},{4,5},{8,9},{12,13},{16,17},{20,21},{24,25},{28,29}} | collective-permute-start | bytes 3145736 | tf_op jit(solution)/shard_map/ppermute | solution.py:288
  415.4 28.2 %collective-permute-start.27 = (bf16[256,2048]{1,0:T(8,128)(2,1)}, bf16[256,2048]{1,0:T(8,128)(2,1)}, u32[]{:S(2)}, u32[]{:S(2)}) collective-permute-start(bf16[256,2048]{1,0:T(8,128)(2,1)} %collective-permute-done.23), channel_id=1, source_target_pairs={{2,3},{6,7},{10,11},{14,15},{18,19},{22,23},{26,27},{30,31}} | collective-permute-start | bytes 3145736 | tf_op jit(solution)/shard_map/ppermute | solution.py:272
  417.1 26.6 %collective-permute-start.28 = (bf16[256,2048]{1,0:T(8,128)(2,1)}, bf16[256,2048]{1,0:T(8,128)(2,1)}, u32[]{:S(2)}, u32[]{:S(2)}) collective-permute-start(bf16[256,2048]{1,0:T(8,128)(2,1)} %collective-permute-done.24), channel_id=1, source_target_pairs={{1,0},{5,4},{9,8},{13,12},{17,16},{21,20},{25,24},{29,28}} | collective-permute-start | bytes 3145736 | tf_op jit(solution)/shard_map/ppermute | solution.py:273
  452.7 27.1 %collective-permute-start.32 = (bf16[256,2048]{1,0:T(8,128)(2,1)}, bf16[256,2048]{1,0:T(8,128)(2,1)}, u32[]{:S(2)}, u32[]{:S(2)}) collective-permute-start(bf16[256,2048]{1,0:T(8,128)(2,1)} %get-tuple-element.409), channel_id=1, source_target_pairs={{1,0},{2,1},{3,2},{5,4},{6,5},{7,6},{9,8},{10,9},{11,10},{13,12},{... | collective-permute-start | bytes 3145736 | tf_op jit(solution)/shard_map/ppermute | solution.py:289
  454.0 25.8 %collective-permute-start.31 = (bf16[256,2048]{1,0:T(8,128)(2,1)}, bf16[256,2048]{1,0:T(8,128)(2,1)}, u32[]{:S(2)}, u32[]{:S(2)}) collective-permute-start(bf16[256,2048]{1,0:T(8,128)(2,1)} %get-tuple-element.410), channel_id=1, source_target_pairs={{0,1},{1,2},{2,3},{4,5},{5,6},{6,7},{8,9},{9,10},{10,11},{12,13},{... | collective-permute-start | bytes 3145736 | tf_op jit(solution)/shard_map/ppermute | solution.py:288
  485.0 27.8 %collective-permute-start.34 = (bf16[256,2048]{1,0:T(8,128)(2,1)}, bf16[256,2048]{1,0:T(8,128)(2,1)}, u32[]{:S(2)}, u32[]{:S(2)}) collective-permute-start(bf16[256,2048]{1,0:T(8,128)(2,1)} %add_convert_fusion.4), channel_id=1, source_target_pairs={{1,0},{2,1},{3,2},{5,4},{6,5},{7,6},{9,8},{10,9},{11,10},{13,12},{... | collective-permute-start | bytes 3145736 | tf_op jit(solution)/shard_map/ppermute | solution.py:273
  486.3 26.6 %collective-permute-start.33 = (bf16[256,2048]{1,0:T(8,128)(2,1)}, bf16[256,2048]{1,0:T(8,128)(2,1)}, u32[]{:S(2)}, u32[]{:S(2)}) collective-permute-start(bf16[256,2048]{1,0:T(8,128)(2,1)} %add_convert_fusion.4), channel_id=1, source_target_pairs={{0,1},{1,2},{2,3},{4,5},{5,6},{6,7},{8,9},{9,10},{10,11},{12,13},{... | collective-permute-start | bytes 3145736 | tf_op jit(solution)/shard_map/ppermute | solution.py:272
  512.9 36.2 %collective-permute-start.38 = (bf16[256,2048]{1,0:T(8,128)(2,1)}, bf16[256,2048]{1,0:T(8,128)(2,1)S(1)}, u32[]{:S(2)}, u32[]{:S(2)}) collective-permute-start(bf16[256,2048]{1,0:T(8,128)(2,1)} %collective-permute-done.33), channel_id=1, source_target_pairs={{1,2},{2,3},{5,6},{6,7},{9,10},{10,11},{13,14},{14,15},{17,18},{18... | collective-permute-start | bytes 3145736 | tf_op jit(solution)/shard_map/ppermute | solution.py:272
  513.8 35.3 %collective-permute-start.39 = (bf16[256,2048]{1,0:T(8,128)(2,1)}, bf16[256,2048]{1,0:T(8,128)(2,1)}, u32[]{:S(2)}, u32[]{:S(2)}) collective-permute-start(bf16[256,2048]{1,0:T(8,128)(2,1)} %collective-permute-done.34), channel_id=1, source_target_pairs={{1,0},{2,1},{5,4},{6,5},{9,8},{10,9},{13,12},{14,13},{17,16},{18,1... | collective-permute-start | bytes 3145736 | tf_op jit(solution)/shard_map/ppermute | solution.py:273
  516.9 31.2 %collective-permute-start.36 = (bf16[256,2048]{1,0:T(8,128)(2,1)S(1)}, bf16[256,2048]{1,0:T(8,128)(2,1)S(1)}, u32[]{:S(2)}, u32[]{:S(2)}) collective-permute-start(bf16[256,2048]{1,0:T(8,128)(2,1)S(1)} %get-tuple-element.272), channel_id=1, source_target_pairs={{0,1},{4,5},{8,9},{12,13},{16,17},{20,21},{24,25},{28,29}} | collective-permute-start | bytes 3145736 | tf_op jit(solution)/shard_map/ppermute | solution.py:305
  554.0 26.4 %collective-permute-start.40 = (bf16[256,2048]{1,0:T(8,128)(2,1)}, bf16[256,2048]{1,0:T(8,128)(2,1)}, u32[]{:S(2)}, u32[]{:S(2)}) collective-permute-start(bf16[256,2048]{1,0:T(8,128)(2,1)} %get-tuple-element.286), channel_id=1, source_target_pairs={{0,1},{1,2},{4,5},{5,6},{8,9},{9,10},{12,13},{13,14},{16,17},{17,1... | collective-permute-start | bytes 3145736 | tf_op jit(solution)/shard_map/ppermute | solution.py:305
  561.1 34.1 %collective-permute-start.42 = (bf16[256,2048]{1,0:T(8,128)(2,1)S(1)}, bf16[256,2048]{1,0:T(8,128)(2,1)}, u32[]{:S(2)}, u32[]{:S(2)}) collective-permute-start(bf16[256,2048]{1,0:T(8,128)(2,1)S(1)} %collective-permute-done.38), channel_id=1, source_target_pairs={{2,3},{6,7},{10,11},{14,15},{18,19},{22,23},{26,27},{30,31}} | collective-permute-start | bytes 3145736 | tf_op jit(solution)/shard_map/ppermute | solution.py:272
  562.8 32.5 %collective-permute-start.43 = (bf16[256,2048]{1,0:T(8,128)(2,1)}, bf16[256,2048]{1,0:T(8,128)(2,1)}, u32[]{:S(2)}, u32[]{:S(2)}) collective-permute-start(bf16[256,2048]{1,0:T(8,128)(2,1)} %collective-permute-done.39), channel_id=1, source_target_pairs={{1,0},{5,4},{9,8},{13,12},{17,16},{21,20},{25,24},{29,28}} | collective-permute-start | bytes 3145736 | tf_op jit(solution)/shard_map/ppermute | solution.py:273
  595.2 114.5 %reduce-scatter.14.cloned.1.call-start = ((), (), s32[]{:S(2)}) async-start(), calls=%async_computation.9 | async-start | bytes 5898240 | tf_op jit(solution)/shard_map/reduce_scatter | solution.py:717
  (194 other events, 2115.0 us)
Sparse Core Ops, SparseCore 0:
  10.2 106.9 all-gather.1
  253.4 71.5 reduce-scatter.7
  328.4 71.4 reduce-scatter.9
  403.3 71.5 reduce-scatter.11
  595.3 35.1 reduce-scatter.15
  633.7 56.5 reduce-scatter.13
